TPU v7x, 32 devices: a whole 2x2x4 slice. The times are simulated.
32 devices in a mesh: runs: 2 (over y), lon: 4 (over x, core), lat: 4 (over z).
Axes of the slice: x: 2, y: 2, z: 4, core: 2. Of those that a mesh axis runs over, the one named last changes fastest.
Arguments:
- latent: bfloat16 [8, 24, 48, 512], P('runs', 'lat', 'lon'), parts along dimension 0, may hold values from -16 to 16
- cotangent: bfloat16 [8, 24, 48, 512], P('runs', 'lat', 'lon'), parts along dimension 0, may hold values from -6 to 6
- mask_ids: int32 [8, 24, 48], P('runs', 'lat', 'lon'), parts along dimension 0, may hold values from 0 to 1
- position_bias: float32 [8, 37], replicated, may hold values from -2 to 302
- norm_gain: float32 [512], replicated, may hold values from 0.1 to 1.9
- w_qkv: bfloat16 [512, 1536], replicated, may hold values from -0.25 to 0.25
- qkv_down: bfloat16 [16, 512], replicated, may hold values from -0.25 to 0.25
- qkv_up: bfloat16 [16, 1536], replicated, may hold values from -0.75 to 0.75
- w_proj: bfloat16 [512, 512], replicated, may hold values from -0.25 to 0.25
- proj_down: bfloat16 [16, 512], replicated, may hold values from -0.25 to 0.25
- proj_up: bfloat16 [16, 512], replicated, may hold values from -0.75 to 0.75
Outputs:
- output: bfloat16 [8, 24, 48, 512], P('runs', 'lat', 'lon'), parts along dimension 0
- latent_grad: bfloat16 [8, 24, 48, 512], P('runs', 'lat', 'lon'), parts along dimension 0
- qkv_down_grad: float32 [32, 512], P('runs'), parts along dimension 0
- qkv_up_grad: float32 [32, 1536], P('runs'), parts along dimension 0
- proj_down_grad: float32 [32, 512], P('runs'), parts along dimension 0
- proj_up_grad: float32 [32, 512], P('runs'), parts along dimension 0
There are 2 independent parts, one for each index of `runs`. A program takes and returns all parts, laid end to end along the dimension named above; an argument that names none is the same for every part. Nothing has to cross between parts.
All inputs are finite; a program needn't handle non-finite values.
Results may differ from a plain program's by a relative error of at most 0.011.
Values may be sent and summed in bfloat16 or wider, within the bound.
No kernel may reach another device: no remote copies, remote signals or barrier semaphores. Data moves between devices by JAX's collectives and lax.ppermute only.
A program may use at most 64 MiB of HBM per device.

v0:
```python
import math

import jax
import jax.numpy as jnp
from jax import lax
from jax.sharding import PartitionSpec as P

HEADS = 8
WIN_LEV = 2
WIN_LAT = 6
WIN_LON = 12


epsilon = 1e-05
masked_value = -1e30


def from_behind(array, axis, by):
    length = lax.axis_size(axis)
    return lax.ppermute(array, axis, [(i, (i + by) % length) for i in range(length)])


def dot_rows(left_side, right_side):
    return lax.dot_general(
        left_side, right_side, (((1,), (1,)), ((), ())), preferred_element_type=jnp.float32
    )


def dot_cols(left_side, right_side):
    return lax.dot_general(
        left_side, right_side, (((0,), (0,)), ((), ())), preferred_element_type=jnp.float32
    )


def window_bias(position_bias):
    window_size = WIN_LEV * WIN_LAT * WIN_LON
    places = jnp.arange(window_size, dtype=jnp.int32)
    level_pos = places // (WIN_LAT * WIN_LON)
    lat_pos = places // WIN_LON % WIN_LAT
    lon_pos = places % WIN_LON
    level_col = level_pos[:, None] - level_pos[None, :] + WIN_LEV - 1
    lat_col = lat_pos[:, None] - lat_pos[None, :] + 2 * WIN_LEV - 1 + WIN_LAT - 1
    lon_col = lon_pos[:, None] - lon_pos[None, :] + 2 * WIN_LEV + 2 * WIN_LAT - 2 + WIN_LON - 1
    columns = jnp.arange(position_bias.shape[1], dtype=jnp.int32)[:, None, None]
    one_hot = (columns == level_col[None]) | (columns == lat_col[None]) | (columns == lon_col[None])
    one_hot = one_hot.astype(jnp.float32).reshape(position_bias.shape[1], window_size * window_size)
    table = jnp.dot(position_bias, one_hot, precision=lax.Precision.HIGHEST)
    return table.reshape(position_bias.shape[0], window_size, window_size)


def to_windows(grid):
    levels, lat_rows, lon_cols, chans = grid.shape
    blocks = grid.reshape(
        levels // WIN_LEV,
        WIN_LEV,
        lat_rows // WIN_LAT,
        WIN_LAT,
        lon_cols // WIN_LON,
        WIN_LON,
        chans,
    )
    return blocks.transpose(0, 2, 4, 1, 3, 5, 6).reshape(-1, WIN_LEV * WIN_LAT * WIN_LON, chans)


def from_windows(windows, levels, lat_rows, lon_cols):
    chans = windows.shape[-1]
    blocks = windows.reshape(
        levels // WIN_LEV,
        lat_rows // WIN_LAT,
        lon_cols // WIN_LON,
        WIN_LEV,
        WIN_LAT,
        WIN_LON,
        chans,
    )
    return blocks.transpose(0, 3, 1, 4, 2, 5, 6).reshape(levels, lat_rows, lon_cols, chans)


def attach(kept, received, axis_pos, after):
    joined = []
    start = 0
    for piece in kept:
        chans = piece.shape[3]
        start = start + chans
        if after:
            joined.append(jnp.concatenate((piece, received), axis_pos))
        else:
            joined.append(jnp.concatenate((received, piece), axis_pos))
    return joined


def lon_in(pieces):
    half_cols = WIN_LON // 2
    strip = jnp.concatenate([piece[:, :, :half_cols] for piece in pieces], 3)
    received = from_behind(strip, "lon", -1)
    return attach([piece[:, :, half_cols:] for piece in pieces], received, 2, True)


def lat_in(pieces):
    half_rows = WIN_LAT // 2
    strip = jnp.concatenate([piece[:, :half_rows] for piece in pieces], 3)
    received = from_behind(strip, "lat", -1)
    return attach([piece[:, half_rows:] for piece in pieces], received, 1, True)


def lon_out(pieces):
    half_cols = WIN_LON // 2
    strip = jnp.concatenate([piece[:, :, -half_cols:] for piece in pieces], 3)
    received = from_behind(strip, "lon", 1)
    return attach([piece[:, :, :-half_cols] for piece in pieces], received, 2, False)


def lat_out(pieces):
    half_rows = WIN_LAT // 2
    strip = jnp.concatenate([piece[:, -half_rows:] for piece in pieces], 3)
    received = from_behind(strip, "lat", 1)
    return attach([piece[:, :-half_rows] for piece in pieces], received, 1, False)


def roll_in(pieces):
    pieces = lat_in(lon_in(pieces))
    return [jnp.roll(piece, -(WIN_LEV // 2), axis=0) for piece in pieces]


def roll_out(pieces):
    pieces = [jnp.roll(piece, WIN_LEV // 2, axis=0) for piece in pieces]
    return lat_out(lon_out(pieces))


def forward_pass(
    x_windows,
    id_windows,
    bias_table,
    norm_gain,
    w_qkv,
    qkv_down,
    qkv_up,
    w_proj,
    proj_down,
    proj_up,
):
    windows, window_size, width = x_windows.shape
    rows_total = windows * window_size
    head_size = width // HEADS
    score_scale = 1.0 / math.sqrt(head_size)
    flat_rows = x_windows.reshape(rows_total, width).astype(jnp.float32)
    average = jnp.mean(flat_rows, axis=-1, keepdims=True)
    centered = flat_rows - average
    variance = jnp.mean(centered * centered, axis=-1, keepdims=True)
    inv_std = lax.rsqrt(variance + epsilon)
    unit_rows = centered * inv_std
    normed = (unit_rows * norm_gain).astype(jnp.bfloat16)
    low_qkv = dot_rows(normed, qkv_down).astype(jnp.bfloat16)
    qkv = (
        jnp.dot(normed, w_qkv, preferred_element_type=jnp.float32)
        + jnp.dot(low_qkv, qkv_up, preferred_element_type=jnp.float32)
    ).astype(jnp.bfloat16)
    pieces = qkv.reshape(windows, window_size, 3, HEADS, head_size)
    query, keys, values = (pieces[:, :, 0], pieces[:, :, 1], pieces[:, :, 2])
    allowed = id_windows[:, None, :, None] == id_windows[:, None, None, :]
    scores = (
        jnp.einsum("bqhd,bkhd->bhqk", query, keys, preferred_element_type=jnp.float32) * score_scale
        + bias_table[None]
    )
    scores = jnp.where(allowed, scores, masked_value)
    row_max = jnp.max(scores, axis=-1, keepdims=True)
    exp_terms = jnp.where(allowed, jnp.exp(scores - row_max), 0.0)
    probs_full = exp_terms / jnp.sum(exp_terms, axis=-1, keepdims=True)
    probs = probs_full.astype(jnp.bfloat16)
    attn = jnp.einsum("bhqk,bkhd->bqhd", probs, values, preferred_element_type=jnp.float32)
    attn = attn.astype(jnp.bfloat16).reshape(rows_total, width)
    low_proj = dot_rows(attn, proj_down).astype(jnp.bfloat16)
    out_rows = (
        flat_rows
        + jnp.dot(attn, w_proj, preferred_element_type=jnp.float32)
        + jnp.dot(low_proj, proj_up, preferred_element_type=jnp.float32)
    ).astype(jnp.bfloat16)
    saved = (
        unit_rows,
        inv_std,
        normed,
        low_qkv,
        query,
        keys,
        values,
        probs_full,
        probs,
        attn,
        low_proj,
    )
    return (out_rows.reshape(x_windows.shape), saved)


def backward_proj(grad_windows, saved, w_proj, proj_down, proj_up):
    attn, low_proj = (saved[9], saved[10])
    grad_rows = grad_windows.reshape(attn.shape)
    proj_up_raw = dot_cols(low_proj, grad_rows)
    d_low_proj = dot_rows(grad_rows, proj_up).astype(jnp.bfloat16)
    proj_down_raw = dot_cols(d_low_proj, attn)
    d_attn = (
        dot_rows(grad_rows, w_proj)
        + jnp.dot(d_low_proj, proj_down, preferred_element_type=jnp.float32)
    ).astype(jnp.bfloat16)
    return (d_attn, proj_down_raw, proj_up_raw)


def backward_qkv(grad_windows, d_attn, saved, norm_gain, w_qkv, qkv_down, qkv_up):
    unit_rows, inv_std, normed, low_qkv, query, keys, values, probs_full, probs = saved[:9]
    windows, window_size, width = grad_windows.shape
    rows_total = windows * window_size
    head_size = width // HEADS
    score_scale = 1.0 / math.sqrt(head_size)
    d_heads = d_attn.reshape(windows, window_size, HEADS, head_size)
    d_probs = jnp.einsum("bqhd,bkhd->bhqk", d_heads, values, preferred_element_type=jnp.float32)
    d_values = jnp.einsum("bhqk,bqhd->bkhd", probs, d_heads, preferred_element_type=jnp.float32)
    d_scores = (
        probs_full * (d_probs - jnp.sum(d_probs * probs_full, axis=-1, keepdims=True)) * score_scale
    ).astype(jnp.bfloat16)
    d_query = jnp.einsum("bhqk,bkhd->bqhd", d_scores, keys, preferred_element_type=jnp.float32)
    d_keys = jnp.einsum("bhqk,bqhd->bkhd", d_scores, query, preferred_element_type=jnp.float32)
    d_qkv = (
        jnp.stack([d_query, d_keys, d_values], axis=2)
        .astype(jnp.bfloat16)
        .reshape(rows_total, 3 * width)
    )
    qkv_up_raw = dot_cols(low_qkv, d_qkv)
    d_low_qkv = dot_rows(d_qkv, qkv_up).astype(jnp.bfloat16)
    qkv_down_raw = dot_cols(d_low_qkv, normed)
    d_normed = dot_rows(d_qkv, w_qkv) + jnp.dot(
        d_low_qkv, qkv_down, preferred_element_type=jnp.float32
    )
    d_unit = d_normed * norm_gain
    norm_back = inv_std * (
        d_unit
        - jnp.mean(d_unit, axis=-1, keepdims=True)
        - unit_rows * jnp.mean(d_unit * unit_rows, axis=-1, keepdims=True)
    )
    grad_rows = grad_windows.reshape(rows_total, width).astype(jnp.float32)
    grad_in = (grad_rows + norm_back).astype(jnp.bfloat16)
    return (grad_in.reshape(grad_windows.shape), qkv_down_raw, qkv_up_raw)


def on_device(
    latent,
    cotangent,
    mask_ids,
    position_bias,
    norm_gain,
    w_qkv,
    qkv_down,
    qkv_up,
    w_proj,
    proj_down,
    proj_up,
):
    levels, lat_rows, lon_cols, width = latent.shape
    shifted = roll_in([latent])[0]
    bias_table = window_bias(position_bias)
    id_windows = to_windows(mask_ids[..., None])[..., 0]
    out_windows, saved = forward_pass(
        to_windows(shifted),
        id_windows,
        bias_table,
        norm_gain,
        w_qkv,
        qkv_down,
        qkv_up,
        w_proj,
        proj_down,
        proj_up,
    )
    shifted_out = from_windows(out_windows, levels, lat_rows, lon_cols)
    output = roll_out([shifted_out])[0]
    grad_shifted = roll_in([cotangent])[0]
    grad_windows = to_windows(grad_shifted)
    d_attn, proj_down_raw, proj_up_raw = backward_proj(
        grad_windows, saved, w_proj, proj_down, proj_up
    )
    proj_down_raw, proj_up_raw = lax.psum((proj_down_raw, proj_up_raw), ("lon", "lat"))
    back_windows, qkv_down_raw, qkv_up_raw = backward_qkv(
        grad_windows, d_attn, saved, norm_gain, w_qkv, qkv_down, qkv_up
    )
    qkv_down_raw, qkv_up_raw = lax.psum((qkv_down_raw, qkv_up_raw), ("lon", "lat"))
    grad_in = from_windows(back_windows, levels, lat_rows, lon_cols)
    latent_grad = roll_out([grad_in])[0]
    grad_scale = 1.0 / math.sqrt(
        levels * lat_rows * lon_cols * lax.axis_size("lat") * lax.axis_size("lon")
    )
    return (
        output,
        latent_grad,
        qkv_down_raw * grad_scale,
        qkv_up_raw * grad_scale,
        proj_down_raw * grad_scale,
        proj_up_raw * grad_scale,
    )


def solution(mesh):
    return jax.shard_map(
        on_device,
        mesh=mesh,
        in_specs=(
            P("runs", "lat", "lon", None),
            P("runs", "lat", "lon", None),
            P("runs", "lat", "lon"),
            P(),
            P(),
            P(),
            P(),
            P(),
            P(),
            P(),
            P(),
        ),
        out_specs=(
            P("runs", "lat", "lon", None),
            P("runs", "lat", "lon", None),
            P("runs", None),
            P("runs", None),
            P("runs", None),
            P("runs", None),
        ),
        check_vma=False,
    )
```

profile of v0, /device:TPU:0, one launch (start us, length us, event | category | flops | bytes accessed | tf_op | source)
XLA Modules:
  0.0 297.6 jit_solution(11945016169374373017)
XLA Ops:
  8.4 2.5 collective-permute-start
  15.6 2.5 convolution_bitcast_fusion
  19.0 3.6 %collective-permute-start.1 = (bf16[4,3,12,512]{3,0,2,1:T(4,128)(2,1)}, bf16[4,3,12,512]{3,0,2,1:T(4,128)(2,1)S(1)}, u32[]{:S(2)}, u32[]{:S(2)}) collective-permute-start(bf16[4,3,12,512]{3,0,2,1:T(4,128)(2,1)} %get-tuple-element.25), channel_id=1, source_target_pairs={{0,3},{1,0},{2,1},{3,2},{4,7},{5,4},{6,5},{7,6},{8,11},{9,8},{10,9... | collective-permute-start | bytes 442376 | tf_op jit(solution)/shard_map/ppermute | solution.py:20
  23.3 2.0 add.150
  25.3 1.6 copy.84
  30.1 3.3 %collective-permute-done.5 = bf16[4,3,12,512]{3,0,2,1:T(4,128)(2,1)} collective-permute-done((bf16[4,3,12,512]{3,0,2,1:T(4,128)(2,1)}, bf16[4,3,12,512]{3,0,2,1:T(4,128)(2,1)}, u32[]{:S(2)}, u32[]{:S(2)}) %collective-permute-start.5) | collective-permute-done | bytes 147488 | tf_op jit(solution)/shard_map/ppermute | solution.py:20
  39.1 2.2 reshape.236
  41.3 2.6 fusion.85
  43.9 2.2 copy.103
  46.1 2.2 copy.102
  49.5 4.3 %fusion.90 = (f32[2,8,144]{2,1,0:T(8,128)S(1)}, f32[2,8,144,144]{2,3,1,0:T(8,128)}) fusion(f32[8,144,144]{1,2,0:T(8,128)} %copy.84, pred[2,144,144]{1,2,0:T(8,128)(4,1)S(1)} %copy-done.14, bf16[2,144,1,8,64]{1,4,3,0,2:T(8,128)(2,1)} %copy.104, bf16[2,144,1,8,64]{1,4,3,0,2:T(8,128)(2,1)} %copy.103), kind=kOutput, calls=%fused_computation.130 | convolution fusion | flops 44458128 | bytes 2631168 | tf_op jit(solution)/shard_map/sub | solution.py:167
  53.9 2.8 fusion.26
  63.7 3.2 %fusion.27 = bf16[2,144,1,8,64]{1,4,3,0,2:T(8,128)(2,1)} fusion(bf16[2,144,8,64]{1,3,2,0:T(8,128)(2,1)} %copy.90, f32[2,8,144,144]{2,3,1,0:T(8,128)} %get-tuple-element.29, f32[2,8,144]{2,1,0:T(8,128)S(1)} %get-tuple-element.28), kind=kOutput, calls=%fused_computation.32 | convolution fusion | flops 43278336 | bytes 1926144 | tf_op jit(solution)/shard_map/bhqk,bqhd->bkhd/dot_general | solution.py:215
  66.9 2.0 fusion.49
  68.9 5.5 %fusion.31 = bf16[2,144,1,8,64]{1,4,3,0,2:T(8,128)(2,1)} fusion(f32[2,8,144,144]{2,3,1,0:T(8,128)} %fusion.49, bf16[2,144,1,8,64]{1,4,3,0,2:T(8,128)(2,1)S(1)} %copy-done.9, f32[2,8,144,144]{2,3,1,0:T(8,128)} %get-tuple-element.29, f32[2,8,144]{2,1,0:T(8,128)} %copy-done.28), kind=kOutput, calls=%fused_computation.34 | convolution fusion | flops 44939664 | bytes 3253248 | tf_op jit(solution)/shard_map/bhqk,bkhd->bqhd/dot_general | solution.py:219
  74.4 5.5 %fusion.28 = bf16[2,144,1,8,64]{1,4,3,0,2:T(8,128)(2,1)} fusion(f32[2,8,144,144]{2,3,1,0:T(8,128)} %fusion.49, bf16[2,144,1,8,64]{1,4,3,0,2:T(8,128)(2,1)S(1)} %copy-done.8, f32[2,8,144,144]{2,3,1,0:T(8,128)} %get-tuple-element.29, f32[2,8,144]{2,1,0:T(8,128)} %copy-done.28), kind=kOutput, calls=%fused_computation.33 | convolution fusion | flops 44939664 | bytes 3253248 | tf_op jit(solution)/shard_map/bhqk,bqhd->bkhd/dot_general | solution.py:220
  79.9 2.7 pad_maximum_fusion
  82.6 3.9 %copy.95 = bf16[2,144,3,8,64]{4,3,2,1,0:T(8,128)(2,1)} copy(bf16[2,144,3,8,64]{1,4,3,0,2:T(8,128)(2,1)} %pad_maximum_fusion) | data formatting | bytes 1769472 | tf_op jit(solution)/shard_map/stack | solution.py:222
  86.5 2.9 convert_element_type.73
  90.6 1.7 fusion.98
  96.2 88.8 %all-reduce.6.cloned.1.call-done = (f32[16,512]{1,0:T(8,128)}, f32[16,512]{1,0:T(8,128)}, f32[16,512]{1,0:T(8,128)}) async-done(((f32[16,512]{1,0:T(8,128)}, f32[16,512]{1,0:T(8,128)}, f32[16,512]{1,0:T(8,128)}), (f32[16,512]{1,0:T(8,128)}, f32[16,512]{1,0:T(8,128)}, f32[16,512]{1,0:T(8,128)})) %all-reduce.6.cloned.1.call-update) | async-done | bytes 98320 | tf_op jit(solution)/shard_map/psum | solution.py:283
  186.4 90.3 %all-reduce.4.cloned.1.call-done = f32[16,1536]{1,0:T(8,128)} async-done(((f32[16,1536]{1,0:T(8,128)}), f32[16,1536]{1,0:T(8,128)}) %all-reduce.4.cloned.1.call-update) | async-done | bytes 98320 | tf_op jit(solution)/shard_map/psum | solution.py:283
  276.8 1.5 broadcast_multiply_fusion
  283.1 5.1 %collective-permute-done.3 = bf16[4,3,12,512]{3,0,2,1:T(4,128)(2,1)S(1)} collective-permute-done((bf16[4,3,12,512]{3,0,2,1:T(4,128)(2,1)S(1)}, bf16[4,3,12,512]{3,0,2,1:T(4,128)(2,1)S(1)}, u32[]{:S(2)}, u32[]{:S(2)}) %collective-permute-start.3) | collective-permute-done | bytes 147488 | tf_op jit(solution)/shard_map/ppermute | solution.py:20
  (160 shorter events, 37.9 us)
Async XLA Ops:
  7.2 30.7 %copy-start = (bf16[512,1536]{1,0:T(8,128)(2,1)S(1)}, bf16[512,1536]{1,0:T(8,128)(2,1)}, u32[]{:S(2)}) copy-start(bf16[512,1536]{1,0:T(8,128)(2,1)} %param.16) | copy-start | bytes 4718596
  7.2 8.4 %copy-start.27 = (f32[8,37]{1,0:T(8,128)S(1)}, f32[8,37]{1,0:T(8,128)}, u32[]{:S(2)}) copy-start(f32[8,37]{1,0:T(8,128)} %param.14) | copy-start | bytes 3556
  7.2 177.9 %all-reduce.6.cloned.1.call-start = ((), (), s32[]{:S(2)}) async-start(), calls=%async_computation.1 | async-start | bytes 196608 | tf_op jit(solution)/shard_map/psum | solution.py:283
  8.4 9.7 %collective-permute-start = (bf16[4,6,6,512]{3,0,2,1:T(4,128)(2,1)S(1)}, bf16[4,6,6,512]{3,0,2,1:T(4,128)(2,1)S(1)}, u32[]{:S(2)}, u32[]{:S(2)}) collective-permute-start(bf16[4,6,6,512]{3,0,2,1:T(4,128)(2,1)S(1)} %get-tuple-element.27), channel_id=1, source_target_pairs={{0,12},{4,0},{8,4},{12,8},{1,13},{5,1},{9,5},{13,9},{2,14},{6,2},{... | collective-permute-start | bytes 442376 | tf_op jit(solution)/shard_map/ppermute | solution.py:20
  12.0 14.9 %collective-permute-start.4 = (bf16[4,6,6,512]{3,0,2,1:T(4,128)(2,1)S(1)}, bf16[4,6,6,512]{3,0,2,1:T(4,128)(2,1)S(1)}, u32[]{:S(2)}, u32[]{:S(2)}) collective-permute-start(bf16[4,6,6,512]{3,0,2,1:T(4,128)(2,1)S(1)} %get-tuple-element.21), channel_id=1, source_target_pairs={{0,12},{4,0},{8,4},{12,8},{1,13},{5,1},{9,5},{13,9},{2,14},{6,2},{... | collective-permute-start | bytes 442376 | tf_op jit(solution)/shard_map/ppermute | solution.py:20
  19.0 9.3 %collective-permute-start.1 = (bf16[4,3,12,512]{3,0,2,1:T(4,128)(2,1)}, bf16[4,3,12,512]{3,0,2,1:T(4,128)(2,1)S(1)}, u32[]{:S(2)}, u32[]{:S(2)}) collective-permute-start(bf16[4,3,12,512]{3,0,2,1:T(4,128)(2,1)} %get-tuple-element.25), channel_id=1, source_target_pairs={{0,3},{1,0},{2,1},{3,2},{4,7},{5,4},{6,5},{7,6},{8,11},{9,8},{10,9... | collective-permute-start | bytes 442376 | tf_op jit(solution)/shard_map/ppermute | solution.py:20
  27.8 5.6 %collective-permute-start.5 = (bf16[4,3,12,512]{3,0,2,1:T(4,128)(2,1)}, bf16[4,3,12,512]{3,0,2,1:T(4,128)(2,1)}, u32[]{:S(2)}, u32[]{:S(2)}) collective-permute-start(bf16[4,3,12,512]{3,0,2,1:T(4,128)(2,1)} %get-tuple-element.19), channel_id=1, source_target_pairs={{0,3},{1,0},{2,1},{3,2},{4,7},{5,4},{6,5},{7,6},{8,11},{9,8},{10,9... | collective-permute-start | bytes 442376 | tf_op jit(solution)/shard_map/ppermute | solution.py:20
  29.6 6.5 %copy-start.15 = (bf16[16,512]{1,0:T(8,128)(2,1)S(1)}, bf16[16,512]{1,0:T(8,128)(2,1)}, u32[]{:S(2)}) copy-start(bf16[16,512]{1,0:T(8,128)(2,1)} %param.21) | copy-start | bytes 49156
  29.7 7.8 %copy-start.20 = (f32[288]{0:T(512)}, f32[288]{0:T(512)S(1)}, u32[]{:S(2)}) copy-start(f32[288]{0:T(512)S(1)} %div.49) | copy-start | bytes 3460
  29.7 6.6 %copy-start.6 = (bf16[512,512]{1,0:T(8,128)(2,1)S(1)}, bf16[512,512]{1,0:T(8,128)(2,1)}, u32[]{:S(2)}) copy-start(bf16[512,512]{1,0:T(8,128)(2,1)} %param.19) | copy-start | bytes 1572868
  30.0 7.5 %copy-start.22 = (f32[288]{0:T(512)}, f32[288]{0:T(512)S(1)}, u32[]{:S(2)}) copy-start(f32[288]{0:T(512)S(1)} %rsqrt.12) | copy-start | bytes 3460
  30.1 7.5 %copy-start.25 = (f32[512]{0:T(512)S(1)}, f32[512]{0:T(512)}, u32[]{:S(2)}) copy-start(f32[512]{0:T(512)} %param.15) | copy-start | bytes 6148
  43.9 5.6 %copy-start.14 = (pred[2,144,144]{1,2,0:T(8,128)(4,1)S(1)}, pred[2,144,144]{1,2,0:T(8,128)(4,1)}, u32[]{:S(2)}) copy-start(pred[2,144,144]{1,2,0:T(8,128)(4,1)} %broadcast_compare_fusion) | copy-start | bytes 124420
  53.9 9.8 %copy-start.28 = (f32[2,8,144]{2,1,0:T(8,128)}, f32[2,8,144]{2,1,0:T(8,128)S(1)}, u32[]{:S(2)}) copy-start(f32[2,8,144]{2,1,0:T(8,128)S(1)} %get-tuple-element.28) | copy-start | bytes 27652
  86.5 5.9 %copy-start.19 = (bf16[16,512]{1,0:T(8,128)(2,1)S(1)}, bf16[16,512]{1,0:T(8,128)(2,1)}, u32[]{:S(2)}) copy-start(bf16[16,512]{1,0:T(8,128)(2,1)} %param.17) | copy-start | bytes 49156
  86.5 6.1 %copy-start.21 = (f32[288]{0:T(512)S(1)}, f32[288]{0:T(512)}, u32[]{:S(2)}) copy-start(f32[288]{0:T(512)} %copy-done.20) | copy-start | bytes 3460
  86.5 6.2 %copy-start.23 = (f32[288]{0:T(512)S(1)}, f32[288]{0:T(512)}, u32[]{:S(2)}) copy-start(f32[288]{0:T(512)} %copy-done.22) | copy-start | bytes 3460
  86.5 6.2 %copy-start.26 = (f32[512]{0:T(512)S(1)}, f32[512]{0:T(512)}, u32[]{:S(2)}) copy-start(f32[512]{0:T(512)} %param.15) | copy-start | bytes 6148
  94.9 184.8 %collective-permute-start.2 = (bf16[4,6,6,512]{3,0,2,1:T(4,128)(2,1)S(1)}, bf16[4,6,6,512]{3,0,2,1:T(4,128)(2,1)S(1)}, u32[]{:S(2)}, u32[]{:S(2)}) collective-permute-start(bf16[4,6,6,512]{3,0,2,1:T(4,128)(2,1)S(1)} %fusion.67), channel_id=1, source_target_pairs={{0,4},{4,8},{8,12},{12,0},{1,5},{5,9},{9,13},{13,1},{2,6},{6,10},{... | collective-permute-start | bytes 442376 | tf_op jit(solution)/shard_map/ppermute | solution.py:20
  95.3 181.5 %all-reduce.4.cloned.1.call-start = ((), (), s32[]{:S(2)}) async-start(), calls=%async_computation | async-start | bytes 196608 | tf_op jit(solution)/shard_map/psum | solution.py:283
  95.5 186.1 %collective-permute-start.6 = (bf16[4,6,6,512]{3,0,2,1:T(4,128)(2,1)S(1)}, bf16[4,6,6,512]{3,0,2,1:T(4,128)(2,1)S(1)}, u32[]{:S(2)}, u32[]{:S(2)}) collective-permute-start(bf16[4,6,6,512]{3,0,2,1:T(4,128)(2,1)S(1)} %fusion.65), channel_id=1, source_target_pairs={{0,4},{4,8},{8,12},{12,0},{1,5},{5,9},{9,13},{13,1},{2,6},{6,10},{... | collective-permute-start | bytes 442376 | tf_op jit(solution)/shard_map/ppermute | solution.py:20
  185.0 97.5 %copy-start.24 = (f32[16,512]{1,0:T(8,128)S(1)}, f32[16,512]{1,0:T(8,128)}, u32[]{:S(2)}) copy-start(f32[16,512]{1,0:T(8,128)} %get-tuple-element.10) | copy-start | bytes 98308
  280.0 8.2 %collective-permute-start.3 = (bf16[4,3,12,512]{3,0,2,1:T(4,128)(2,1)S(1)}, bf16[4,3,12,512]{3,0,2,1:T(4,128)(2,1)S(1)}, u32[]{:S(2)}, u32[]{:S(2)}) collective-permute-start(bf16[4,3,12,512]{3,0,2,1:T(4,128)(2,1)S(1)} %get-tuple-element.22), channel_id=1, source_target_pairs={{0,1},{1,2},{2,3},{3,0},{4,5},{5,6},{6,7},{7,4},{8,9},{9,10},{10,1... | collective-permute-start | bytes 442376 | tf_op jit(solution)/shard_map/ppermute | solution.py:20
  281.9 8.0 %collective-permute-start.7 = (bf16[4,3,12,512]{3,0,2,1:T(4,128)(2,1)S(1)}, bf16[4,3,12,512]{3,0,2,1:T(4,128)(2,1)S(1)}, u32[]{:S(2)}, u32[]{:S(2)}) collective-permute-start(bf16[4,3,12,512]{3,0,2,1:T(4,128)(2,1)S(1)} %get-tuple-element.16), channel_id=1, source_target_pairs={{0,1},{1,2},{2,3},{3,0},{4,5},{5,6},{6,7},{7,4},{8,9},{9,10},{10,1... | collective-permute-start | bytes 442376 | tf_op jit(solution)/shard_map/ppermute | solution.py:20
  (17 other events, 46.2 us)
Sparse Core Ops, SparseCore 0:
  95.4 89.6 all-reduce.5
  189.0 87.6 all-reduce.3
where the time goes:
time: 299 us; the launch traced here: 298 us
  waiting for transfers between devices  188 us (63%)
  matrix products  36.1 us (12%)
  local copies, waits for them, and re-layouts  31.5 us (11%)
  other arithmetic  16.7 us (6%)
  between operations  14.7 us (5%)
  starting transfers between devices  10.2 us (3%)
    psum x2, waiting for transfers between devices, on_device(): lax.psum((qkv_down_raw, qkv_up_raw), ('lon', 'lat'))  179 us
    ppermute x8, starting transfers between devices, from_behind(): lax.ppermute(array, axis, [(i, (i + by) % length) for i in range(length)])  10.2 us
    ppermute x8, waiting for transfers between devices, from_behind(): lax.ppermute(array, axis, [(i, (i + by) % length) for i in range(length)])  9.14 us
    unnamed x62, local copies, waits for them, and re-layouts  6.64 us
  transfers between devices with their start and end apart: 10, of which 5 were waited for; matrix products, arithmetic and copies ran while one was open for 7% of the time, Pallas kernels for 0%

commit v1 on v0

v1 whole, which is shorter than its diff:
```python
import math

import jax
import jax.numpy as jnp
import numpy as np
from jax import lax
from jax.experimental import pallas as pl
from jax.experimental.pallas import tpu as pltpu
from jax.sharding import PartitionSpec as P

HEADS = 8
WIN_LEV = 2
WIN_LAT = 6
WIN_LON = 12
HALF_LAT = WIN_LAT // 2
HALF_LON = WIN_LON // 2
HALF_LEV = WIN_LEV // 2
WINDOW = WIN_LEV * WIN_LAT * WIN_LON
QUAD = WINDOW // 4

epsilon = 1e-05
masked_value = -1e30
f32 = jnp.float32
bf16 = jnp.bfloat16


def nn(a, b):
    return lax.dot_general(a, b, (((1,), (0,)), ((), ())), preferred_element_type=f32)


def nt(a, b):
    return lax.dot_general(a, b, (((1,), (1,)), ((), ())), preferred_element_type=f32)


def tn(a, b):
    return lax.dot_general(a, b, (((0,), (0,)), ((), ())), preferred_element_type=f32)


def call(kernel, out_shape, scratch=(), **kw):
    return pl.pallas_call(
        kernel,
        out_shape=out_shape,
        scratch_shapes=list(scratch),
        compiler_params=pltpu.CompilerParams(vmem_limit_bytes=56 * 1024 * 1024),
        **kw,
    )


def struct(shape, dtype):
    return jax.ShapeDtypeStruct(shape, dtype)


def pack_kernel(x_ref, *refs):
    outs, scratch = refs[:4], refs[4]
    levels = x_ref.shape[0]
    rows = levels * HALF_LAT * HALF_LON
    for level in range(levels):
        for lat in range(WIN_LAT):
            slab = x_ref[(level + HALF_LEV) % levels, lat].astype(f32)
            for half in range(2):
                quad = (2 if lat < HALF_LAT else 0) + (1 if half == 0 else 0)
                at = quad * rows + (level * HALF_LAT + lat % HALF_LAT) * HALF_LON
                scratch[at : at + HALF_LON, :] = slab[half * HALF_LON : (half + 1) * HALF_LON, :]
    for quad in range(4):
        outs[quad][...] = scratch[quad * rows : (quad + 1) * rows, :].astype(bf16)


def pack(x):
    levels, _, _, width = x.shape
    rows = levels * HALF_LAT * HALF_LON
    return call(
        pack_kernel,
        [struct((rows, width), bf16)] * 4,
        [pltpu.VMEM((4 * rows, width), f32)],
        name="pack",
    )(x)


def unpack_kernel(q0, q1, q2, q3, out_ref, scratch):
    quads = (q0, q1, q2, q3)
    levels = out_ref.shape[0]
    rows = levels * HALF_LAT * HALF_LON
    for quad in range(4):
        scratch[quad * rows : (quad + 1) * rows, :] = quads[quad][...].astype(f32)
    for level in range(levels):
        for lat in range(WIN_LAT):
            parts = []
            for half in range(2):
                quad = (2 if lat < HALF_LAT else 0) + (1 if half == 0 else 0)
                at = quad * rows + (level * HALF_LAT + lat % HALF_LAT) * HALF_LON
                parts.append(scratch[at : at + HALF_LON, :])
            out_ref[(level + HALF_LEV) % levels, lat] = jnp.concatenate(parts, 0).astype(bf16)


def unpack(quads, shape):
    levels, _, _, width = shape
    rows = levels * HALF_LAT * HALF_LON
    return call(
        unpack_kernel,
        struct(shape, bf16),
        [pltpu.VMEM((4 * rows, width), f32)],
        name="unpack",
    )(*quads)


def coordinates():
    n = np.arange(WINDOW)
    quad, r = n // QUAD, n % QUAD
    lev = r // (HALF_LAT * HALF_LON)
    lat = (quad // 2) * HALF_LAT + r // HALF_LON % HALF_LAT
    lon = (quad % 2) * HALF_LON + r % HALF_LON
    return np.stack([lev, lat, lon]).astype(np.int32)


def table_kernel(pb_ref, col_ref, row_ref, id_col_ref, id_row_ref, out_ref):
    windows = id_col_ref.shape[0]
    bases = (WIN_LEV - 1, 2 * WIN_LEV - 1 + WIN_LAT - 1, 2 * WIN_LEV + 2 * WIN_LAT - 2 + WIN_LON - 1)
    extents = (WIN_LEV, WIN_LAT, WIN_LON)
    block = 8

    def step(b, carry):
        at = pl.multiple_of(b * block, block)
        sums = [None] * HEADS
        for axis in range(3):
            diff = row_ref[axis : axis + 1, :] - col_ref[axis, pl.ds(at, block), :]
            parts = [jnp.zeros((block, WINDOW), f32)] * HEADS
            for offset in range(1 - extents[axis], extents[axis]):
                hit = diff == offset
                parts = [
                    jnp.where(hit, pb_ref[h, bases[axis] + offset], parts[h]) for h in range(HEADS)
                ]
            sums = parts if axis == 0 else [s + p for s, p in zip(sums, parts)]
        for w in range(windows):
            allowed = id_col_ref[w, pl.ds(at, block), :] == id_row_ref[w]
            for h in range(HEADS):
                out_ref[w * HEADS + h, pl.ds(at, block), :] = jnp.where(
                    allowed, sums[h], masked_value
                )
        return carry

    lax.fori_loop(0, WINDOW // block, step, 0)


def score_table(position_bias, mask_ids):
    levels = mask_ids.shape[0]
    windows = levels // WIN_LEV
    ids = mask_ids.reshape(windows, WIN_LEV, 2, HALF_LAT, 2, HALF_LON)
    ids = ids.transpose(0, 2, 4, 1, 3, 5).reshape(windows, WINDOW)
    coords = coordinates()
    vmem = pl.BlockSpec(memory_space=pltpu.VMEM)
    return call(
        table_kernel,
        struct((windows * HEADS, WINDOW, WINDOW), f32),
        in_specs=[pl.BlockSpec(memory_space=pltpu.SMEM), vmem, vmem, vmem, vmem],
        name="table",
    )(
        position_bias,
        jnp.asarray(coords[:, :, None]),
        jnp.asarray(coords),
        ids[:, :, None],
        ids[:, None, :],
    )


def gather_rows(quads, scratch):
    windows = scratch.shape[0] // WINDOW
    for quad in range(4):
        piece = quads[quad][...].astype(f32)
        for w in range(windows):
            at = w * WINDOW + quad * QUAD
            scratch[at : at + QUAD, :] = piece[w * QUAD : (w + 1) * QUAD, :]


def scatter_rows(scratch, outs):
    windows = scratch.shape[0] // WINDOW
    for quad in range(4):
        pieces = [
            scratch[w * WINDOW + quad * QUAD : w * WINDOW + (quad + 1) * QUAD, :]
            for w in range(windows)
        ]
        outs[quad][...] = jnp.concatenate(pieces, 0).astype(bf16)


def forward_kernel(
    x0, x1, x2, x3, table, gain, w_qkv, qkv_down, qkv_up, w_proj, proj_down, proj_up,
    o0, o1, o2, o3, unit_ref, inv_ref, normed_ref, low_ref, qkv_ref, probs_ref, attn_ref, low_proj_ref,
    scratch,
):
    gather_rows((x0, x1, x2, x3), scratch)
    width = scratch.shape[1]
    windows = scratch.shape[0] // WINDOW
    head = width // HEADS
    pair = 2 * head
    rows = scratch[...]
    average = jnp.mean(rows, axis=-1, keepdims=True)
    centered = rows - average
    variance = jnp.mean(centered * centered, axis=-1, keepdims=True)
    inv_std = lax.rsqrt(variance + epsilon)
    unit = centered * inv_std
    normed = (unit * gain[...]).astype(bf16)
    unit_ref[...] = unit
    inv_ref[...] = inv_std
    normed_ref[...] = normed
    low = nt(normed, qkv_down[...]).astype(bf16)
    low_ref[...] = low
    qkv_ref[...] = (nn(normed, w_qkv[...]) + nn(low, qkv_up[...])).astype(bf16)
    scale = 1.0 / math.sqrt(head)
    lane = lax.broadcasted_iota(jnp.int32, (WINDOW, pair), 1)
    for w in range(windows):
        at = slice(w * WINDOW, (w + 1) * WINDOW)
        for p in range(HEADS // 2):
            query = qkv_ref[at, p * pair : (p + 1) * pair]
            keys = qkv_ref[at, width + p * pair : width + (p + 1) * pair]
            values = qkv_ref[at, 2 * width + p * pair : 2 * width + (p + 1) * pair]
            mixed = []
            for h in range(2):
                mine = (lane < head) if h == 0 else (lane >= head)
                index = w * HEADS + 2 * p + h
                scores = nt(keys, jnp.where(mine, query, 0)) * scale + table[index]
                top = jnp.max(scores, axis=0, keepdims=True)
                terms = jnp.exp(scores - top)
                probs = terms * (1.0 / jnp.sum(terms, axis=0, keepdims=True))
                probs_ref[index] = probs
                mixed.append(tn(probs.astype(bf16), values))
            attn_ref[at, p * pair : (p + 1) * pair] = jnp.where(
                lane < head, mixed[0], mixed[1]
            ).astype(bf16)
    attn = attn_ref[...]
    low_proj = nt(attn, proj_down[...]).astype(bf16)
    low_proj_ref[...] = low_proj
    scratch[...] = scratch[...] + nn(attn, w_proj[...]) + nn(low_proj, proj_up[...])
    scatter_rows(scratch, (o0, o1, o2, o3))


def backward_kernel(
    g0, g1, g2, g3, normed_ref, low_ref, qkv_ref, probs_ref, attn_ref, low_proj_ref,
    qkv_up, w_proj, proj_down, proj_up,
    grad_ref, d_qkv_ref, d_low_ref, raw_ref,
):
    gather_rows((g0, g1, g2, g3), grad_ref)
    width = grad_ref.shape[1]
    windows = grad_ref.shape[0] // WINDOW
    head = width // HEADS
    pair = 2 * head
    scale = 1.0 / math.sqrt(head)
    grad = grad_ref[...].astype(bf16)
    d_low_proj = nt(grad, proj_up[...]).astype(bf16)
    d_attn = (nt(grad, w_proj[...]) + nn(d_low_proj, proj_down[...])).astype(bf16)
    lane = lax.broadcasted_iota(jnp.int32, (WINDOW, pair), 1)
    for w in range(windows):
        at = slice(w * WINDOW, (w + 1) * WINDOW)
        for p in range(HEADS // 2):
            cols = [slice(s * width + p * pair, s * width + (p + 1) * pair) for s in range(3)]
            query = qkv_ref[at, cols[0]]
            keys = qkv_ref[at, cols[1]]
            values = qkv_ref[at, cols[2]]
            d_out = d_attn[at, p * pair : (p + 1) * pair]
            d_q, d_k, d_v = [], [], []
            for h in range(2):
                mine = (lane < head) if h == 0 else (lane >= head)
                probs = probs_ref[w * HEADS + 2 * p + h]
                d_probs = nt(values, jnp.where(mine, d_out, 0))
                inner = jnp.sum(d_probs * probs, axis=0, keepdims=True)
                d_scores = (probs * (d_probs - inner) * scale).astype(bf16)
                d_v.append(nn(probs.astype(bf16), d_out))
                d_k.append(nn(d_scores, query))
                d_q.append(tn(d_scores, keys))
            for s, parts in enumerate((d_q, d_k, d_v)):
                d_qkv_ref[at, cols[s]] = jnp.where(lane < head, parts[0], parts[1]).astype(bf16)
    d_qkv = d_qkv_ref[...]
    d_low = nt(d_qkv, qkv_up[...]).astype(bf16)
    d_low_ref[...] = d_low
    raw_ref[:, 0:width] = tn(d_low, normed_ref[...]).astype(bf16)
    raw_ref[:, width : 4 * width] = tn(low_ref[...], d_qkv).astype(bf16)
    raw_ref[:, 4 * width : 5 * width] = tn(d_low_proj, attn_ref[...]).astype(bf16)
    raw_ref[:, 5 * width : 6 * width] = tn(low_proj_ref[...], grad).astype(bf16)


def norm_kernel(
    grad_ref, d_qkv_ref, d_low_ref, unit_ref, inv_ref, gain, w_qkv, qkv_down, o0, o1, o2, o3, scratch
):
    d_normed = nt(d_qkv_ref[...], w_qkv[...]) + nn(d_low_ref[...], qkv_down[...])
    d_unit = d_normed * gain[...]
    unit = unit_ref[...]
    back = inv_ref[...] * (
        d_unit
        - jnp.mean(d_unit, axis=-1, keepdims=True)
        - unit * jnp.mean(d_unit * unit, axis=-1, keepdims=True)
    )
    scratch[...] = grad_ref[...] + back
    scatter_rows(scratch, (o0, o1, o2, o3))


def step_pairs(mesh_shape, lon_by, lat_by):
    lons, lats = mesh_shape
    return [
        (i * lats + j, (i + lon_by) % lons * lats + (j + lat_by) % lats)
        for i in range(lons)
        for j in range(lats)
    ]


def exchange(quads, sizes, by):
    axes = ("lon", "lat")
    far = lax.ppermute(quads[3], axes, step_pairs(sizes, by, by))
    side = lax.ppermute(quads[2], axes, step_pairs(sizes, 0, by))
    near = lax.ppermute(quads[1], axes, step_pairs(sizes, by, 0))
    return [quads[0], near, side, far]


def sum_over(raw, sizes):
    total = None
    for axis, length in (("lon", sizes[0]), ("lat", sizes[1])):
        bit = 1
        while bit < length:
            if total is not None:
                raw = total.astype(bf16)
            other = lax.ppermute(raw, axis, [(i, i ^ bit) for i in range(length)])
            total = raw.astype(f32) + other.astype(f32)
            bit *= 2
    return raw.astype(f32) if total is None else total


def on_device(sizes):
    def body(
        latent, cotangent, mask_ids, position_bias, norm_gain,
        w_qkv, qkv_down, qkv_up, w_proj, proj_down, proj_up,
    ):
        levels, lat_rows, lon_cols, width = latent.shape
        assert (lat_rows, lon_cols) == (WIN_LAT, WIN_LON)
        windows = levels // WIN_LEV
        total = windows * WINDOW
        rank = qkv_down.shape[0]
        quarter = struct((windows * QUAD, width), bf16)
        gain = norm_gain[None, :]
        x_quads = exchange(pack(latent), sizes, -1)
        g_quads = exchange(pack(cotangent), sizes, -1)
        table = score_table(position_bias, mask_ids)
        (
            o0, o1, o2, o3, unit, inv_std, normed, low, qkv, probs, attn, low_proj,
        ) = call(
            forward_kernel,
            [quarter] * 4
            + [
                struct((total, width), f32),
                struct((total, 1), f32),
                struct((total, width), bf16),
                struct((total, rank), bf16),
                struct((total, 3 * width), bf16),
                struct((windows * HEADS, WINDOW, WINDOW), f32),
                struct((total, width), bf16),
                struct((total, rank), bf16),
            ],
            [pltpu.VMEM((total, width), f32)],
            name="forward",
        )(*x_quads, table, gain, w_qkv, qkv_down, qkv_up, w_proj, proj_down, proj_up)
        out_quads = exchange((o0, o1, o2, o3), sizes, 1)
        grad, d_qkv, d_low, raw = call(
            backward_kernel,
            [
                struct((total, width), f32),
                struct((total, 3 * width), bf16),
                struct((total, rank), bf16),
                struct((rank, 6 * width), bf16),
            ],
            name="backward",
        )(*g_quads, normed, low, qkv, probs, attn, low_proj, qkv_up, w_proj, proj_down, proj_up)
        sums = sum_over(raw, sizes)
        back = call(
            norm_kernel,
            [quarter] * 4,
            [pltpu.VMEM((total, width), f32)],
            name="norm_back",
        )(grad, d_qkv, d_low, unit, inv_std, gain, w_qkv, qkv_down)
        back_quads = exchange(back, sizes, 1)
        output = unpack(out_quads, latent.shape)
        latent_grad = unpack(back_quads, latent.shape)
        grad_scale = 1.0 / math.sqrt(levels * lat_rows * lon_cols * sizes[0] * sizes[1])
        sums = sums * grad_scale
        return (
            output,
            latent_grad,
            sums[:, 0:width],
            sums[:, width : 4 * width],
            sums[:, 4 * width : 5 * width],
            sums[:, 5 * width : 6 * width],
        )

    return body


def solution(mesh):
    block = P("runs", "lat", "lon", None)
    sizes = (mesh.shape["lon"], mesh.shape["lat"])
    return jax.shard_map(
        on_device(sizes),
        mesh=mesh,
        in_specs=(block, block, P("runs", "lat", "lon")) + (P(),) * 8,
        out_specs=(block, block) + (P("runs", None),) * 4,
        check_vma=False,
    )
```

time: 299 us -> 75.6 us (0.25)
  waiting for transfers between devices: 188 us -> 10.3 us
  matrix products: 36.1 us -> 0 us
  Pallas kernels: 0 us -> 33.2 us
  local copies, waits for them, and re-layouts: 31.5 us -> 13.6 us
  other arithmetic: 16.7 us -> 1 us
  between operations: 14.7 us -> 0.78 us
  starting transfers between devices: 10.2 us -> 16.2 us
    psum x2 -> x0, waiting for transfers between devices: 179 us -> none  [on_device(): lax.psum((qkv_down_raw, qkv_up_raw), ('lon', 'lat'))]
    pallas_call x0 -> x8, Pallas kernels: none -> 33.2 us  [the longest x1 8.23 us: body(): call(backward_kernel, [struct((total, width), f32), struct((total, 3 * wi...]
    dot_general x22 -> x0, matrix products: 31.8 us -> none  [the longest x1 5.53 us: backward_qkv(): jnp.einsum('bhqk,bkhd->bqhd', d_scores, keys, preferred_element_type=jnp....]
    concatenate x11 -> x0, other arithmetic: 7.15 us -> none  [the longest x4 3.28 us: attach(): joined.append(jnp.concatenate((piece, received), axis_pos))]
    ppermute x8 -> x16, starting transfers between devices: 10.2 us -> 16.2 us  [the longest x4 5.17 us: sum_over(): other = lax.ppermute(raw, axis, [(i, i ^ bit) for i in range(length)])]
    slice x17 -> x2, local copies, waits for them, and re-layouts: 6.21 us -> 1.29 us  [the longest x1 0.65 us: body(): sums[:, width:4 * width]]
    mul x4 -> x1, other arithmetic: 4.92 us -> 0.03 us  [body(): sums = sums * grad_scale]
    convert_element_type x4 -> x0, local copies, waits for them, and re-layouts: 4.56 us -> none  [the longest x1 2.88 us: backward_qkv(): d_qkv = jnp.stack([d_query, d_keys, d_values], axis=2).astype(jnp.bfloat1...]
  transfers between devices with their start and end apart: 10 -> 16, of which waited for: 5 -> 7; matrix products, arithmetic and copies ran while one was open for 7% -> 11% of each run, Pallas kernels for 0% -> 31%
where the time goes in v1:
time: 75.6 us; the launch traced here: 75 us
  Pallas kernels  33.2 us (44%)
  starting transfers between devices  16.2 us (21%)
  local copies, waits for them, and re-layouts  13.6 us (18%)
  waiting for transfers between devices  10.3 us (14%)
  other arithmetic  1 us (1%)
  between operations  0.78 us (1%)
    unnamed x34, local copies, waits for them, and re-layouts  10 us
    pallas_call x1, Pallas kernels, body(): call(backward_kernel, [struct((total, width), f32), struct((total, 3 * wi...  8.23 us
    pallas_call x1, Pallas kernels, score_table(): call(table_kernel, struct((windows * HEADS, WINDOW, WINDOW), f32), in_spe...  7.12 us
    pallas_call x1, Pallas kernels, body(): call(forward_kernel, [quarter] * 4 + [struct((total, width), f32), struct...  6.95 us
    ppermute x4, starting transfers between devices, sum_over(): other = lax.ppermute(raw, axis, [(i, i ^ bit) for i in range(length)])  5.17 us
    ppermute x4, starting transfers between devices, exchange(): near = lax.ppermute(quads[1], axes, step_pairs(sizes, by, 0))  4.94 us
    ppermute x4, waiting for transfers between devices, sum_over(): other = lax.ppermute(raw, axis, [(i, i ^ bit) for i in range(length)])  4.75 us
    ppermute x4, starting transfers between devices, exchange(): side = lax.ppermute(quads[2], axes, step_pairs(sizes, 0, by))  4.51 us
  transfers between devices with their start and end apart: 16, of which 7 were waited for; matrix products, arithmetic and copies ran while one was open for 11% of the time, Pallas kernels for 31%

profile of v1, /device:TPU:0, one launch (start us, length us, event | category | flops | bytes accessed | tf_op | source)
XLA Modules:
  0.0 75.0 jit_solution(5197242481674338358)
XLA Ops:
  0.6 1.8 %copy.24.x_ref = bf16[4,6,12,512]{3,2,1,0:T(8,128)(2,1)} copy(bf16[4,6,12,512]{3,0,2,1:T(4,128)(2,1)} %param.13) | data formatting | bytes 589824 | tf_op args[0]
  2.4 1.8 %pack.2 = (bf16[72,512]{1,0:T(8,128)(2,1)}, bf16[72,512]{1,0:T(8,128)(2,1)}, bf16[72,512]{1,0:T(8,128)(2,1)}, bf16[72,512]{1,0:T(8,128)(2,1)}) custom-call(bf16[4,6,12,512]{3,2,1,0:T(8,128)(2,1)} %copy.24.x_ref), custom_call_target="tpu_custom_call" | custom-call | tf_op jit(solution)/shard_map/pack/pallas_call | solution.py:71
  4.2 2.4 %collective-permute-start = (bf16[72,512]{1,0:T(8,128)(2,1)}, bf16[72,512]{1,0:T(8,128)(2,1)S(1)}, u32[]{:S(2)}, u32[]{:S(2)}) collective-permute-start(bf16[72,512]{1,0:T(8,128)(2,1)} %get-tuple-element.35), channel_id=1, source_target_pairs={{0,12},{1,13},{2,14},{3,15},{4,0},{5,1},{6,2},{7,3},{8,4},{9,5},{1... | collective-permute-start | bytes 221192 | tf_op jit(solution)/shard_map/ppermute | solution.py:307
  6.6 3.6 %collective-permute-start.1 = (bf16[72,512]{1,0:T(8,128)(2,1)}, bf16[72,512]{1,0:T(8,128)(2,1)S(1)}, u32[]{:S(2)}, u32[]{:S(2)}) collective-permute-start(bf16[72,512]{1,0:T(8,128)(2,1)} %get-tuple-element.36), channel_id=1, source_target_pairs={{0,3},{1,0},{2,1},{3,2},{4,7},{5,4},{6,5},{7,6},{8,11},{9,8},{10,9... | collective-permute-start | bytes 221192 | tf_op jit(solution)/shard_map/ppermute | solution.py:306
  10.5 1.8 %copy.28.x_ref = bf16[4,6,12,512]{3,2,1,0:T(8,128)(2,1)} copy(bf16[4,6,12,512]{3,0,2,1:T(4,128)(2,1)} %param.14) | data formatting | bytes 589824 | tf_op args[1]
  12.2 1.8 %pack.3 = (bf16[72,512]{1,0:T(8,128)(2,1)}, bf16[72,512]{1,0:T(8,128)(2,1)}, bf16[72,512]{1,0:T(8,128)(2,1)}, bf16[72,512]{1,0:T(8,128)(2,1)}) custom-call(bf16[4,6,12,512]{3,2,1,0:T(8,128)(2,1)} %copy.28.x_ref), custom_call_target="tpu_custom_call" | custom-call | tf_op jit(solution)/shard_map/pack/pallas_call | solution.py:71
  17.3 7.1 %table.1 = f32[16,144,144]{2,1,0:T(8,128)} custom-call(f32[8,37]{1,0:T(8,128)} %pb_ref.1, s32[3,144,1]{2,1,0:T(8,128)} %constant.6.clone.col_ref, s32[3,144]{1,0:T(4,128)} %constant.7.clone.row_ref, s32[2,144,1]{2,1,0:T(8,128)} %broadcast_in_dim_reshape.8.id_col_ref, s32[2,1,144]{2,1,0:T(1,128)} %broadcast_in_dim_reshape.9.id_row_ref), custom_call_target="tpu_custom_call" | custom-call | tf_op jit(solution)/shard_map/table/pallas_call | solution.py:151
  25.0 6.9 %forward.1 = (bf16[72,512]{1,0:T(8,128)(2,1)}, bf16[72,512]{1,0:T(8,128)(2,1)}, bf16[72,512]{1,0:T(8,128)(2,1)}, bf16[72,512]{1,0:T(8,128)(2,1)}, f32[288,512]{1...) custom-call(bf16[72,512]{1,0:T(8,128)(2,1)} %get-tuple-element.34.x0, ...), custom_call_target="tpu_custom_call" | custom-call | tf_op jit(solution)/shard_map/forward/pallas_call | solution.py:341
  32.7 8.2 %backward.1 = (f32[288,512]{1,0:T(8,128)}, bf16[288,1536]{1,0:T(8,128)(2,1)}, bf16[288,16]{1,0:T(8,128)(2,1)}, bf16[16,3072]{1,0:T(8,128)(2,1)}) custom-call(bf16[72,512]{1,0:T(8,128)(2,1)} %get-tuple-element.42.g0, bf16[72,512]{1,0:T(8,128)(2,1)} %copy-done.6, bf16[72,512]{1,0:T(8,128)(2,1)} %copy-done.7, bf16[72,512]{1,0:T(8,128)(2,1)} %copy-done.11, ...), custom_call_target="tpu_custom_call" | custom-call | tf_op jit(solution)/shard_map/backward/pallas_call | solution.py:358
  41.5 1.2 %collective-permute-done.12 = bf16[16,3072]{1,0:T(8,128)(2,1)S(1)} collective-permute-done((bf16[16,3072]{1,0:T(8,128)(2,1)}, bf16[16,3072]{1,0:T(8,128)(2,1)S(1)}, u32[]{:S(2)}, u32[]{:S(2)}) %collective-permute-start.12) | collective-permute-done | bytes 98336 | tf_op jit(solution)/shard_map/ppermute | solution.py:318
  43.6 1.5 %collective-permute-start.13 = (bf16[16,3072]{1,0:T(8,128)(2,1)S(1)}, bf16[16,3072]{1,0:T(8,128)(2,1)S(1)}, u32[]{:S(2)}, u32[]{:S(2)}) collective-permute-start(bf16[16,3072]{1,0:T(8,128)(2,1)S(1)} %add_convert_fusion.2), channel_id=1, source_target_pairs={{0,8},{4,12},{8,0},{12,4},{1,9},{5,13},{9,1},{13,5},{2,10},{6,14},... | collective-permute-start | bytes 294920 | tf_op jit(solution)/shard_map/ppermute | solution.py:318
  45.2 3.6 %collective-permute-done.13 = bf16[16,3072]{1,0:T(8,128)(2,1)S(1)} collective-permute-done((bf16[16,3072]{1,0:T(8,128)(2,1)S(1)}, bf16[16,3072]{1,0:T(8,128)(2,1)S(1)}, u32[]{:S(2)}, u32[]{:S(2)}) %collective-permute-start.13) | collective-permute-done | bytes 98336 | tf_op jit(solution)/shard_map/ppermute | solution.py:318
  48.8 1.6 %collective-permute-start.14 = (bf16[16,3072]{1,0:T(8,128)(2,1)S(1)}, bf16[16,3072]{1,0:T(8,128)(2,1)S(1)}, u32[]{:S(2)}, u32[]{:S(2)}) collective-permute-start(bf16[16,3072]{1,0:T(8,128)(2,1)S(1)} %add_convert_fusion.1), channel_id=1, source_target_pairs={{0,1},{1,0},{2,3},{3,2},{4,5},{5,4},{6,7},{7,6},{8,9},{9,8},{10,11... | collective-permute-start | bytes 294920 | tf_op jit(solution)/shard_map/ppermute | solution.py:318
  50.4 3.6 %norm_back.1 = (bf16[72,512]{1,0:T(8,128)(2,1)}, bf16[72,512]{1,0:T(8,128)(2,1)}, bf16[72,512]{1,0:T(8,128)(2,1)}, bf16[72,512]{1,0:T(8,128)(2,1)}) custom-call(f32[288,512]{1,0:T(8,128)} %get-tuple-element.52.grad_ref, bf16[288,1536]{1,0:T(8,128)(2,1)} %get-tuple-element.53.d_qkv_ref, bf16[288,16]{1,0:T(8,128)(2,1)} %get-tuple-element.54.d_low_ref, ...), custom_call_target="tpu_custom_call" | custom-call | tf_op jit(solution)/shard_map/norm_back/pallas_call | solution.py:369
  54.5 1.2 %collective-permute-start.11 = (bf16[72,512]{1,0:T(8,128)(2,1)}, bf16[72,512]{1,0:T(8,128)(2,1)S(1)}, u32[]{:S(2)}, u32[]{:S(2)}) collective-permute-start(bf16[72,512]{1,0:T(8,128)(2,1)} %get-tuple-element.60), channel_id=1, source_target_pairs={{0,5},{1,6},{2,7},{3,4},{4,9},{5,10},{6,11},{7,8},{8,13},{9,14},{1... | collective-permute-start | bytes 221192 | tf_op jit(solution)/shard_map/ppermute | solution.py:305
  55.8 1.4 %collective-permute-start.15 = (bf16[16,3072]{1,0:T(8,128)(2,1)S(1)}, bf16[16,3072]{1,0:T(8,128)(2,1)S(1)}, u32[]{:S(2)}, u32[]{:S(2)}) collective-permute-start(bf16[16,3072]{1,0:T(8,128)(2,1)S(1)} %add_convert_fusion), channel_id=1, source_target_pairs={{0,2},{1,3},{2,0},{3,1},{4,6},{5,7},{6,4},{7,5},{8,10},{9,11},{10,... | collective-permute-start | bytes 294920 | tf_op jit(solution)/shard_map/ppermute | solution.py:318
  57.2 2.1 %collective-permute-start.9 = (bf16[72,512]{1,0:T(8,128)(2,1)}, bf16[72,512]{1,0:T(8,128)(2,1)S(1)}, u32[]{:S(2)}, u32[]{:S(2)}) collective-permute-start(bf16[72,512]{1,0:T(8,128)(2,1)} %get-tuple-element.58), channel_id=1, source_target_pairs={{0,4},{1,5},{2,6},{3,7},{4,8},{5,9},{6,10},{7,11},{8,12},{9,13},{1... | collective-permute-start | bytes 221192 | tf_op jit(solution)/shard_map/ppermute | solution.py:307
  59.3 1.2 %collective-permute-done.10.q2 = bf16[72,512]{1,0:T(8,128)(2,1)S(1)} collective-permute-done((bf16[72,512]{1,0:T(8,128)(2,1)}, bf16[72,512]{1,0:T(8,128)(2,1)S(1)}, u32[]{:S(2)}, u32[]{:S(2)}) %collective-permute-start.10) | collective-permute-done | bytes 73760 | tf_op jit(solution)/shard_map/ppermute | solution.py:306
  60.4 1.5 %collective-permute-done.11.q3 = bf16[72,512]{1,0:T(8,128)(2,1)S(1)} collective-permute-done((bf16[72,512]{1,0:T(8,128)(2,1)}, bf16[72,512]{1,0:T(8,128)(2,1)S(1)}, u32[]{:S(2)}, u32[]{:S(2)}) %collective-permute-start.11) | collective-permute-done | bytes 73760 | tf_op jit(solution)/shard_map/ppermute | solution.py:305
  62.8 1.9 %unpack.3 = bf16[4,6,12,512]{3,2,1,0:T(8,128)(2,1)} custom-call(bf16[72,512]{1,0:T(8,128)(2,1)} %get-tuple-element.57.q0, bf16[72,512]{1,0:T(8,128)(2,1)} %copy-done.4, bf16[72,512]{1,0:T(8,128)(2,1)} %copy-done, bf16[72,512]{1,0:T(8,128)(2,1)} %copy-done.2), custom_call_target="tpu_custom_call" | custom-call | tf_op jit(solution)/shard_map/unpack/pallas_call | solution.py:98
  64.6 1.9 %copy.30 = bf16[4,6,12,512]{3,0,2,1:T(4,128)(2,1)} copy(bf16[4,6,12,512]{3,2,1,0:T(8,128)(2,1)} %unpack.3) | data formatting | bytes 589824
  66.7 2.6 %collective-permute-done.5.q3 = bf16[72,512]{1,0:T(8,128)(2,1)S(1)} collective-permute-done((bf16[72,512]{1,0:T(8,128)(2,1)S(1)}, bf16[72,512]{1,0:T(8,128)(2,1)S(1)}, u32[]{:S(2)}, u32[]{:S(2)}) %collective-permute-start.5) | collective-permute-done | bytes 73760 | tf_op jit(solution)/shard_map/ppermute | solution.py:305
  69.9 1.9 %unpack.2 = bf16[4,6,12,512]{3,2,1,0:T(8,128)(2,1)} custom-call(bf16[72,512]{1,0:T(8,128)(2,1)} %get-tuple-element.38.q0, bf16[72,512]{1,0:T(8,128)(2,1)} %copy-done.1, bf16[72,512]{1,0:T(8,128)(2,1)} %copy-done.3, bf16[72,512]{1,0:T(8,128)(2,1)} %copy-done.5), custom_call_target="tpu_custom_call" | custom-call | tf_op jit(solution)/shard_map/unpack/pallas_call | solution.py:98
  71.8 1.9 %copy.29 = bf16[4,6,12,512]{3,0,2,1:T(4,128)(2,1)} copy(bf16[4,6,12,512]{3,2,1,0:T(8,128)(2,1)} %unpack.2) | data formatting | bytes 589824
  (60 shorter events, 9.7 us)
Async XLA Ops:
  4.2 10.8 %collective-permute-start = (bf16[72,512]{1,0:T(8,128)(2,1)}, bf16[72,512]{1,0:T(8,128)(2,1)S(1)}, u32[]{:S(2)}, u32[]{:S(2)}) collective-permute-start(bf16[72,512]{1,0:T(8,128)(2,1)} %get-tuple-element.35), channel_id=1, source_target_pairs={{0,12},{1,13},{2,14},{3,15},{4,0},{5,1},{6,2},{7,3},{8,4},{9,5},{1... | collective-permute-start | bytes 221192 | tf_op jit(solution)/shard_map/ppermute | solution.py:307
  6.6 17.8 %collective-permute-start.1 = (bf16[72,512]{1,0:T(8,128)(2,1)}, bf16[72,512]{1,0:T(8,128)(2,1)S(1)}, u32[]{:S(2)}, u32[]{:S(2)}) collective-permute-start(bf16[72,512]{1,0:T(8,128)(2,1)} %get-tuple-element.36), channel_id=1, source_target_pairs={{0,3},{1,0},{2,1},{3,2},{4,7},{5,4},{6,5},{7,6},{8,11},{9,8},{10,9... | collective-permute-start | bytes 221192 | tf_op jit(solution)/shard_map/ppermute | solution.py:306
  10.2 14.2 %collective-permute-start.2 = (bf16[72,512]{1,0:T(8,128)(2,1)}, bf16[72,512]{1,0:T(8,128)(2,1)S(1)}, u32[]{:S(2)}, u32[]{:S(2)}) collective-permute-start(bf16[72,512]{1,0:T(8,128)(2,1)} %get-tuple-element.37), channel_id=1, source_target_pairs={{0,15},{1,12},{2,13},{3,14},{4,3},{5,0},{6,1},{7,2},{8,7},{9,4},{1... | collective-permute-start | bytes 221192 | tf_op jit(solution)/shard_map/ppermute | solution.py:305
  14.0 18.0 %collective-permute-start.6 = (bf16[72,512]{1,0:T(8,128)(2,1)}, bf16[72,512]{1,0:T(8,128)(2,1)S(1)}, u32[]{:S(2)}, u32[]{:S(2)}) collective-permute-start(bf16[72,512]{1,0:T(8,128)(2,1)} %get-tuple-element.43), channel_id=1, source_target_pairs={{0,12},{1,13},{2,14},{3,15},{4,0},{5,1},{6,2},{7,3},{8,4},{9,5},{1... | collective-permute-start | bytes 221192 | tf_op jit(solution)/shard_map/ppermute | solution.py:307
  14.5 17.5 %collective-permute-start.7 = (bf16[72,512]{1,0:T(8,128)(2,1)}, bf16[72,512]{1,0:T(8,128)(2,1)S(1)}, u32[]{:S(2)}, u32[]{:S(2)}) collective-permute-start(bf16[72,512]{1,0:T(8,128)(2,1)} %get-tuple-element.44), channel_id=1, source_target_pairs={{0,3},{1,0},{2,1},{3,2},{4,7},{5,4},{6,5},{7,6},{8,11},{9,8},{10,9... | collective-permute-start | bytes 221192 | tf_op jit(solution)/shard_map/ppermute | solution.py:306
  15.0 9.5 %copy-start.8 = (bf16[72,512]{1,0:T(8,128)(2,1)}, bf16[72,512]{1,0:T(8,128)(2,1)S(1)}, u32[]{:S(2)}) copy-start(bf16[72,512]{1,0:T(8,128)(2,1)S(1)} %collective-permute-done.x1) | copy-start | bytes 221188
  15.0 17.1 %collective-permute-start.8 = (bf16[72,512]{1,0:T(8,128)(2,1)}, bf16[72,512]{1,0:T(8,128)(2,1)S(1)}, u32[]{:S(2)}, u32[]{:S(2)}) collective-permute-start(bf16[72,512]{1,0:T(8,128)(2,1)} %get-tuple-element.45), channel_id=1, source_target_pairs={{0,15},{1,12},{2,13},{3,14},{4,3},{5,0},{6,1},{7,2},{8,7},{9,4},{1... | collective-permute-start | bytes 221192 | tf_op jit(solution)/shard_map/ppermute | solution.py:305
  32.0 0.7 copy-start.11
  40.9 18.3 %copy-start.14 = (bf16[72,512]{1,0:T(8,128)(2,1)S(1)}, bf16[72,512]{1,0:T(8,128)(2,1)}, u32[]{:S(2)}) copy-start(bf16[72,512]{1,0:T(8,128)(2,1)} %get-tuple-element.39) | copy-start | bytes 221188
  40.9 19.5 %copy-start.13 = (bf16[72,512]{1,0:T(8,128)(2,1)S(1)}, bf16[72,512]{1,0:T(8,128)(2,1)}, u32[]{:S(2)}) copy-start(bf16[72,512]{1,0:T(8,128)(2,1)} %get-tuple-element.40) | copy-start | bytes 221188
  40.9 21.0 %copy-start.12 = (bf16[72,512]{1,0:T(8,128)(2,1)S(1)}, bf16[72,512]{1,0:T(8,128)(2,1)}, u32[]{:S(2)}) copy-start(bf16[72,512]{1,0:T(8,128)(2,1)} %get-tuple-element.41) | copy-start | bytes 221188
  40.9 1.7 %collective-permute-start.12 = (bf16[16,3072]{1,0:T(8,128)(2,1)}, bf16[16,3072]{1,0:T(8,128)(2,1)S(1)}, u32[]{:S(2)}, u32[]{:S(2)}) collective-permute-start(bf16[16,3072]{1,0:T(8,128)(2,1)} %get-tuple-element.61), channel_id=1, source_target_pairs={{0,4},{4,0},{8,12},{12,8},{1,5},{5,1},{9,13},{13,9},{2,6},{6,2},{1... | collective-permute-start | bytes 294920 | tf_op jit(solution)/shard_map/ppermute | solution.py:318
  43.6 5.1 %collective-permute-start.13 = (bf16[16,3072]{1,0:T(8,128)(2,1)S(1)}, bf16[16,3072]{1,0:T(8,128)(2,1)S(1)}, u32[]{:S(2)}, u32[]{:S(2)}) collective-permute-start(bf16[16,3072]{1,0:T(8,128)(2,1)S(1)} %add_convert_fusion.2), channel_id=1, source_target_pairs={{0,8},{4,12},{8,0},{12,4},{1,9},{5,13},{9,1},{13,5},{2,10},{6,14},... | collective-permute-start | bytes 294920 | tf_op jit(solution)/shard_map/ppermute | solution.py:318
  48.8 7.0 %collective-permute-start.14 = (bf16[16,3072]{1,0:T(8,128)(2,1)S(1)}, bf16[16,3072]{1,0:T(8,128)(2,1)S(1)}, u32[]{:S(2)}, u32[]{:S(2)}) collective-permute-start(bf16[16,3072]{1,0:T(8,128)(2,1)S(1)} %add_convert_fusion.1), channel_id=1, source_target_pairs={{0,1},{1,0},{2,3},{3,2},{4,5},{5,4},{6,7},{7,6},{8,9},{9,8},{10,11... | collective-permute-start | bytes 294920 | tf_op jit(solution)/shard_map/ppermute | solution.py:318
  54.0 6.4 %collective-permute-start.10 = (bf16[72,512]{1,0:T(8,128)(2,1)}, bf16[72,512]{1,0:T(8,128)(2,1)S(1)}, u32[]{:S(2)}, u32[]{:S(2)}) collective-permute-start(bf16[72,512]{1,0:T(8,128)(2,1)} %get-tuple-element.59), channel_id=1, source_target_pairs={{0,1},{1,2},{2,3},{3,0},{4,5},{5,6},{6,7},{7,4},{8,9},{9,10},{10,1... | collective-permute-start | bytes 221192 | tf_op jit(solution)/shard_map/ppermute | solution.py:306
  54.5 7.4 %collective-permute-start.11 = (bf16[72,512]{1,0:T(8,128)(2,1)}, bf16[72,512]{1,0:T(8,128)(2,1)S(1)}, u32[]{:S(2)}, u32[]{:S(2)}) collective-permute-start(bf16[72,512]{1,0:T(8,128)(2,1)} %get-tuple-element.60), channel_id=1, source_target_pairs={{0,5},{1,6},{2,7},{3,4},{4,9},{5,10},{6,11},{7,8},{8,13},{9,14},{1... | collective-permute-start | bytes 221192 | tf_op jit(solution)/shard_map/ppermute | solution.py:305
  55.8 17.9 %collective-permute-start.15 = (bf16[16,3072]{1,0:T(8,128)(2,1)S(1)}, bf16[16,3072]{1,0:T(8,128)(2,1)S(1)}, u32[]{:S(2)}, u32[]{:S(2)}) collective-permute-start(bf16[16,3072]{1,0:T(8,128)(2,1)S(1)} %add_convert_fusion), channel_id=1, source_target_pairs={{0,2},{1,3},{2,0},{3,1},{4,6},{5,7},{6,4},{7,5},{8,10},{9,11},{10,... | collective-permute-start | bytes 294920 | tf_op jit(solution)/shard_map/ppermute | solution.py:318
  57.2 5.0 %collective-permute-start.9 = (bf16[72,512]{1,0:T(8,128)(2,1)}, bf16[72,512]{1,0:T(8,128)(2,1)S(1)}, u32[]{:S(2)}, u32[]{:S(2)}) collective-permute-start(bf16[72,512]{1,0:T(8,128)(2,1)} %get-tuple-element.58), channel_id=1, source_target_pairs={{0,4},{1,5},{2,6},{3,7},{4,8},{5,9},{6,10},{7,11},{8,12},{9,13},{1... | collective-permute-start | bytes 221192 | tf_op jit(solution)/shard_map/ppermute | solution.py:307
  59.3 7.3 %collective-permute-start.3 = (bf16[72,512]{1,0:T(8,128)(2,1)S(1)}, bf16[72,512]{1,0:T(8,128)(2,1)S(1)}, u32[]{:S(2)}, u32[]{:S(2)}) collective-permute-start(bf16[72,512]{1,0:T(8,128)(2,1)S(1)} %copy-done.14), channel_id=1, source_target_pairs={{0,4},{1,5},{2,6},{3,7},{4,8},{5,9},{6,10},{7,11},{8,12},{9,13},{1... | collective-permute-start | bytes 221192 | tf_op jit(solution)/shard_map/ppermute | solution.py:307
  60.4 1.7 %copy-start = (bf16[72,512]{1,0:T(8,128)(2,1)}, bf16[72,512]{1,0:T(8,128)(2,1)S(1)}, u32[]{:S(2)}) copy-start(bf16[72,512]{1,0:T(8,128)(2,1)S(1)} %collective-permute-done.10.q2) | copy-start | bytes 221188
  60.4 6.3 %collective-permute-start.4 = (bf16[72,512]{1,0:T(8,128)(2,1)S(1)}, bf16[72,512]{1,0:T(8,128)(2,1)S(1)}, u32[]{:S(2)}, u32[]{:S(2)}) collective-permute-start(bf16[72,512]{1,0:T(8,128)(2,1)S(1)} %copy-done.13), channel_id=1, source_target_pairs={{0,1},{1,2},{2,3},{3,0},{4,5},{5,6},{6,7},{7,4},{8,9},{9,10},{10,1... | collective-permute-start | bytes 221192 | tf_op jit(solution)/shard_map/ppermute | solution.py:306
  61.9 7.4 %collective-permute-start.5 = (bf16[72,512]{1,0:T(8,128)(2,1)S(1)}, bf16[72,512]{1,0:T(8,128)(2,1)S(1)}, u32[]{:S(2)}, u32[]{:S(2)}) collective-permute-start(bf16[72,512]{1,0:T(8,128)(2,1)S(1)} %copy-done.12), channel_id=1, source_target_pairs={{0,5},{1,6},{2,7},{3,4},{4,9},{5,10},{6,11},{7,8},{8,13},{9,14},{1... | collective-permute-start | bytes 221192 | tf_op jit(solution)/shard_map/ppermute | solution.py:305
  66.6 2.7 %copy-start.1 = (bf16[72,512]{1,0:T(8,128)(2,1)}, bf16[72,512]{1,0:T(8,128)(2,1)S(1)}, u32[]{:S(2)}) copy-start(bf16[72,512]{1,0:T(8,128)(2,1)S(1)} %collective-permute-done.3.q1) | copy-start | bytes 221188
  66.7 2.6 %copy-start.3 = (bf16[72,512]{1,0:T(8,128)(2,1)}, bf16[72,512]{1,0:T(8,128)(2,1)S(1)}, u32[]{:S(2)}) copy-start(bf16[72,512]{1,0:T(8,128)(2,1)S(1)} %collective-permute-done.4.q2) | copy-start | bytes 221188
  (7 other events, 4.4 us)

commit v2 on v1

v2 whole, which is shorter than its diff:
```python
import functools
import math

import jax
import jax.numpy as jnp
import numpy as np
from jax import lax
from jax.experimental import pallas as pl
from jax.experimental.pallas import tpu as pltpu
from jax.sharding import PartitionSpec as P

HEADS = 8
WIN_LEV = 2
WIN_LAT = 6
WIN_LON = 12
HALF_LAT = WIN_LAT // 2
HALF_LON = WIN_LON // 2
HALF_LEV = WIN_LEV // 2
WINDOW = WIN_LEV * WIN_LAT * WIN_LON

epsilon = 1e-05
masked_value = -1e30
f32 = jnp.float32
bf16 = jnp.bfloat16


def nn(a, b):
    return lax.dot_general(a, b, (((1,), (0,)), ((), ())), preferred_element_type=f32)


def nt(a, b):
    return lax.dot_general(a, b, (((1,), (1,)), ((), ())), preferred_element_type=f32)


def tn(a, b):
    return lax.dot_general(a, b, (((0,), (0,)), ((), ())), preferred_element_type=f32)


def call(kernel, out_shape, scratch=(), vmem=16, **kw):
    return pl.pallas_call(
        kernel,
        out_shape=out_shape,
        scratch_shapes=list(scratch),
        compiler_params=pltpu.CompilerParams(vmem_limit_bytes=vmem * 1024 * 1024),
        **kw,
    )


def in_hbm(array):
    return pltpu.with_memory_space_constraint(array, pltpu.HBM)


def struct(shape, dtype):
    return jax.ShapeDtypeStruct(shape, dtype)


ANY = pl.BlockSpec(memory_space=pl.ANY)
HBM = pl.BlockSpec(memory_space=pltpu.HBM)
VMEM = pl.BlockSpec(memory_space=pltpu.VMEM)


def corner(ref, quad):
    lat = 0 if quad >= 2 else HALF_LAT
    lon = 0 if quad % 2 else HALF_LON
    return ref.at[lat : lat + HALF_LAT, lon : lon + HALF_LON]


def run_copies(pairs, sems):
    copies = [pltpu.make_async_copy(src, dst, sems.at[i]) for i, (src, dst) in enumerate(pairs)]
    for copy in copies:
        copy.start()
    return copies


def pack_kernel(x_ref, g_ref, *refs):
    outs, sems = refs[:8], refs[8]
    pairs = [(corner(x_ref, q), outs[q]) for q in range(4)]
    pairs += [(corner(g_ref, q), outs[4 + q]) for q in range(4)]
    for copy in run_copies(pairs, sems):
        copy.wait()


def pack(x, g):
    _, _, levels, width = x.shape
    quads = call(
        pack_kernel,
        [struct((HALF_LAT, HALF_LON, levels, width), bf16)] * 8,
        [pltpu.SemaphoreType.DMA((8,))],
        vmem=2,
        in_specs=[HBM] * 2,
        out_specs=[ANY] * 8,
        name="pack",
    )(in_hbm(x), in_hbm(g))
    return quads[:4], quads[4:]


def unpack_kernel(q0, q1, q2, q3, out_ref, sems):
    quads = (q0, q1, q2, q3)
    for copy in run_copies([(quads[q], corner(out_ref, q)) for q in range(4)], sems):
        copy.wait()


def unpack(quads, shape):
    return call(
        unpack_kernel,
        struct(shape, bf16),
        [pltpu.SemaphoreType.DMA((4,))],
        vmem=2,
        in_specs=[ANY] * 4,
        out_specs=ANY,
        name="unpack",
    )(*quads)


AXES = (WIN_LEV, WIN_LAT, WIN_LON)
PLACES = sum(AXES)
SPLITS = 3
MARK = SPLITS * PLACES
LANES = 128


def score_constants():
    n = np.arange(WINDOW)
    lev, r = n // (WINDOW // WIN_LEV), n % (WINDOW // WIN_LEV)
    quad, s = r // (HALF_LAT * HALF_LON), r % (HALF_LAT * HALF_LON)
    lat = (quad // 2) * HALF_LAT + s // HALF_LON
    lon = (quad % 2) * HALF_LON + s % HALF_LON
    starts = (0, WIN_LEV, WIN_LEV + WIN_LAT)
    place = np.zeros((WINDOW, PLACES), np.float32)
    for start, where in zip(starts, (lev, lat, lon)):
        place[n, start + where] = 1
    axis_of = np.repeat(np.arange(3), AXES)
    spot = np.concatenate([np.arange(extent) for extent in AXES])
    bases = (WIN_LEV - 1, 2 * WIN_LEV - 1 + WIN_LAT - 1, 2 * WIN_LEV + 2 * WIN_LAT - 2 + WIN_LON - 1)
    column = np.full((PLACES, HEADS, LANES), -1, np.int32)
    for key in range(PLACES):
        for query in range(PLACES):
            if axis_of[key] == axis_of[query]:
                at = bases[axis_of[key]] + spot[query] - spot[key]
                for part in range(SPLITS):
                    column[key, :, part * PLACES + query] = at
    spread = np.zeros((SPLITS, HEADS, HEADS, LANES), np.float32)
    for part in range(SPLITS):
        for h in range(HEADS):
            spread[part, h, h, part * PLACES : (part + 1) * PLACES] = 1
    query_side = np.zeros((WINDOW, LANES), np.float32)
    query_side[:, :MARK] = np.tile(place, (1, SPLITS))
    first = lev == 0
    lat_of = place[first][:, WIN_LEV : WIN_LEV + WIN_LAT]
    lon_of = place[first][:, WIN_LEV + WIN_LAT :]
    return (
        jnp.asarray(column.reshape(PLACES, HEADS * LANES)),
        jnp.asarray(spread.reshape(SPLITS, HEADS, HEADS * LANES), bf16),
        jnp.asarray(place, bf16),
        jnp.asarray(query_side, f32),
        jnp.asarray(lat_of, f32),
        jnp.asarray(lon_of, f32),
    )


def table_kernel(*refs, count):
    inputs, refs = refs[: 8 + count], refs[8 + count :]
    key_out, query_out = refs[:2]
    kept, local, sems = refs[2 : 2 + count], refs[2 + count : 10 + count], refs[10 + count]
    copies = run_copies(list(zip(inputs, tuple(local) + tuple(kept))), sems)
    for copy in copies[:8]:
        copy.wait()
    make_columns(*local, key_out, query_out)
    for copy in copies[8:]:
        copy.wait()


def make_columns(
    pb_ref, ids_ref, column_ref, spread_ref, place_ref, query_ref, lat_ref, lon_ref, key_out, query_out
):
    windows = key_out.shape[0]
    rest = pb_ref[...]
    wide = None
    for part in range(SPLITS):
        piece = rest.astype(bf16)
        rest = rest - piece.astype(f32)
        term = tn(piece, spread_ref[part])
        wide = term if wide is None else wide + term
    column = column_ref[...]
    table = jnp.zeros(column.shape, f32)
    for c in range(pb_ref.shape[1]):
        table = jnp.where(column == c, wide[c : c + 1, :], table)
    keys = nn(place_ref[...], table.astype(bf16))
    ids = None
    for lat in range(WIN_LAT):
        term = lat_ref[:, lat : lat + 1] * nt(lon_ref[...], ids_ref[lat].astype(f32))
        ids = term if ids is None else ids + term
    half = WINDOW // WIN_LEV
    key_lane = lax.broadcasted_iota(jnp.int32, (half, HEADS * LANES), 1) % LANES
    query_lane = lax.broadcasted_iota(jnp.int32, (half, LANES), 1)
    for w in range(windows):
        key_rows, query_rows = [], []
        for lev in range(WIN_LEV):
            mine = ids[:, w * WIN_LEV + lev : w * WIN_LEV + lev + 1]
            rows = slice(lev * half, (lev + 1) * half)
            key_rows.append(
                jnp.where(
                    key_lane == MARK,
                    masked_value * mine,
                    jnp.where(key_lane == MARK + 1, masked_value * (1.0 - mine), keys[rows]),
                )
            )
            query_rows.append(
                jnp.where(
                    query_lane == MARK,
                    1.0 - mine,
                    jnp.where(query_lane == MARK + 1, mine, query_ref[rows, :]),
                )
            )
        key_out[w] = jnp.concatenate(key_rows, 0).astype(bf16)
        query_out[w] = jnp.concatenate(query_rows, 0).astype(bf16)


def score_columns(position_bias, mask_ids, weights):
    windows = mask_ids.shape[0] // WIN_LEV
    inputs = (position_bias, mask_ids.transpose(1, 0, 2)) + score_constants()
    return call(
        functools.partial(table_kernel, count=len(weights)),
        [struct((windows, WINDOW, HEADS * LANES), bf16), struct((windows, WINDOW, LANES), bf16)]
        + [struct(w.shape, w.dtype) for w in weights],
        [pltpu.VMEM(x.shape, x.dtype) for x in inputs]
        + [pltpu.SemaphoreType.DMA((len(inputs) + len(weights),))],
        in_specs=[HBM] * (len(inputs) + len(weights)),
        name="table",
    )(*map(in_hbm, inputs), *map(in_hbm, weights))


def slabs(quads):
    _, _, levels, _ = quads[0].shape
    for quad in range(4):
        for lat in range(HALF_LAT):
            for lon in range(HALF_LON):
                yield quads[quad], lat, lon, ((quad * HALF_LAT + lat) * HALF_LON + lon) * levels


def gather_rows(quads, scratch, out_ref):
    levels = quads[0].shape[2]
    tiles, total, _ = scratch.shape
    rows = total // levels
    for ref, lat, lon, at in slabs(quads):
        slab = ref[lat, lon].astype(f32)
        for t in range(tiles):
            scratch[t, at : at + levels, :] = slab[:, t * LANES : (t + 1) * LANES]
    for level in range(levels):
        for t in range(tiles):
            out_ref[level * rows : (level + 1) * rows, t * LANES : (t + 1) * LANES] = scratch[
                t, pl.ds((level + HALF_LEV) % levels, rows, stride=levels), :
            ]


def scatter_rows(value, scratch, outs):
    levels = outs[0].shape[2]
    tiles, total, _ = scratch.shape
    rows = total // levels
    for level in range(levels):
        for t in range(tiles):
            scratch[t, pl.ds((level + HALF_LEV) % levels, rows, stride=levels), :] = value[
                level * rows : (level + 1) * rows, t * LANES : (t + 1) * LANES
            ]
    for ref, lat, lon, at in slabs(outs):
        for t in range(tiles):
            ref[lat, lon, :, t * LANES : (t + 1) * LANES] = scratch[t, at : at + levels, :].astype(bf16)


def forward_kernel(
    x0, x1, x2, x3, key_cols, query_cols, gain, w_qkv, qkv_down, qkv_up, w_proj, proj_down, proj_up,
    o0, o1, o2, o3, unit_ref, inv_ref, normed_ref, low_ref, qkv_ref, probs_ref, attn_ref, low_proj_ref,
    scratch, rows_ref,
):
    gather_rows((x0, x1, x2, x3), scratch, rows_ref)
    total, width = rows_ref.shape
    windows = total // WINDOW
    head = width // HEADS
    pair = 2 * head
    rows = rows_ref[...]
    average = jnp.mean(rows, axis=-1, keepdims=True)
    centered = rows - average
    variance = jnp.mean(centered * centered, axis=-1, keepdims=True)
    inv_std = lax.rsqrt(variance + epsilon)
    unit = centered * inv_std
    normed = (unit * gain[...]).astype(bf16)
    unit_ref[...] = unit
    inv_ref[...] = inv_std
    normed_ref[...] = normed
    low = nt(normed, qkv_down[...]).astype(bf16)
    low_ref[...] = low
    qkv_ref[...] = (nn(normed, w_qkv[...]) + nn(low, qkv_up[...])).astype(bf16)
    scale = 1.0 / math.sqrt(head)
    assert math.frexp(scale)[0] == 0.5
    lane = lax.broadcasted_iota(jnp.int32, (WINDOW, pair), 1)
    for w in range(windows):
        at = slice(w * WINDOW, (w + 1) * WINDOW)
        more = query_cols[w]
        for p in range(HEADS // 2):
            query = qkv_ref[at, p * pair : (p + 1) * pair] * jnp.asarray(scale, bf16)
            keys = qkv_ref[at, width + p * pair : width + (p + 1) * pair]
            values = qkv_ref[at, 2 * width + p * pair : 2 * width + (p + 1) * pair]
            mixed = []
            for h in range(2):
                mine = (lane < head) if h == 0 else (lane >= head)
                number = 2 * p + h
                wide_query = jnp.concatenate([jnp.where(mine, query, 0), more], 1)
                wide_keys = jnp.concatenate(
                    [keys, key_cols[w, :, number * LANES : (number + 1) * LANES]], 1
                )
                scores = nt(wide_keys, wide_query)
                top = jnp.max(scores, axis=0, keepdims=True)
                terms = jnp.exp(scores - top)
                probs = terms * (1.0 / jnp.sum(terms, axis=0, keepdims=True))
                probs_ref[w * HEADS + number] = probs
                mixed.append(tn(probs.astype(bf16), values))
            attn_ref[at, p * pair : (p + 1) * pair] = jnp.where(
                lane < head, mixed[0], mixed[1]
            ).astype(bf16)
    attn = attn_ref[...]
    low_proj = nt(attn, proj_down[...]).astype(bf16)
    low_proj_ref[...] = low_proj
    out = rows_ref[...] + nn(attn, w_proj[...]) + nn(low_proj, proj_up[...])
    scatter_rows(out, scratch, (o0, o1, o2, o3))


def backward_kernel(
    g0, g1, g2, g3, normed_ref, low_ref, qkv_ref, probs_ref, attn_ref, low_proj_ref,
    qkv_up, w_proj, proj_down, proj_up,
    grad_ref, d_qkv_ref, d_low_ref, keep_ref, send_ref, scratch,
):
    gather_rows((g0, g1, g2, g3), scratch, grad_ref)
    width = grad_ref.shape[1]
    windows = grad_ref.shape[0] // WINDOW
    head = width // HEADS
    pair = 2 * head
    scale = 1.0 / math.sqrt(head)
    grad = grad_ref[...].astype(bf16)
    d_low_proj = nt(grad, proj_up[...]).astype(bf16)
    d_attn = (nt(grad, w_proj[...]) + nn(d_low_proj, proj_down[...])).astype(bf16)
    lane = lax.broadcasted_iota(jnp.int32, (WINDOW, pair), 1)
    for w in range(windows):
        at = slice(w * WINDOW, (w + 1) * WINDOW)
        for p in range(HEADS // 2):
            cols = [slice(s * width + p * pair, s * width + (p + 1) * pair) for s in range(3)]
            query = qkv_ref[at, cols[0]]
            keys = qkv_ref[at, cols[1]]
            values = qkv_ref[at, cols[2]]
            d_out = d_attn[at, p * pair : (p + 1) * pair]
            d_q, d_k, d_v = [], [], []
            for h in range(2):
                mine = (lane < head) if h == 0 else (lane >= head)
                probs = probs_ref[w * HEADS + 2 * p + h]
                d_probs = nt(values, jnp.where(mine, d_out, 0))
                inner = jnp.sum(d_probs * probs, axis=0, keepdims=True)
                d_scores = (probs * (d_probs - inner) * scale).astype(bf16)
                d_v.append(nn(probs.astype(bf16), d_out))
                d_k.append(nn(d_scores, query))
                d_q.append(tn(d_scores, keys))
            for s, parts in enumerate((d_q, d_k, d_v)):
                d_qkv_ref[at, cols[s]] = jnp.where(lane < head, parts[0], parts[1]).astype(bf16)
    d_qkv = d_qkv_ref[...]
    d_low = nt(d_qkv, qkv_up[...]).astype(bf16)
    d_low_ref[...] = d_low
    raw = jnp.concatenate(
        [
            tn(d_low, normed_ref[...]),
            tn(low_ref[...], d_qkv),
            tn(d_low_proj, attn_ref[...]),
            tn(low_proj_ref[...], grad),
        ],
        1,
    )
    half = keep_ref.shape[1]
    odd = lax.axis_index("lon") % 2

    @pl.when(odd == 0)
    def _():
        keep_ref[...] = raw[:, :half]
        send_ref[...] = raw[:, half:]

    @pl.when(odd == 1)
    def _():
        keep_ref[...] = raw[:, half:]
        send_ref[...] = raw[:, :half]


def norm_kernel(
    grad_ref, d_qkv_ref, d_low_ref, unit_ref, inv_ref, gain, w_qkv, qkv_down, o0, o1, o2, o3, scratch
):
    d_normed = nt(d_qkv_ref[...], w_qkv[...]) + nn(d_low_ref[...], qkv_down[...])
    d_unit = d_normed * gain[...]
    unit = unit_ref[...]
    back = inv_ref[...] * (
        d_unit
        - jnp.mean(d_unit, axis=-1, keepdims=True)
        - unit * jnp.mean(d_unit * unit, axis=-1, keepdims=True)
    )
    scatter_rows(grad_ref[...] + back, scratch, (o0, o1, o2, o3))


def finish_kernel(a_ref, b_ref, *outs, scale):
    total = (a_ref[...].astype(f32) + b_ref[...].astype(f32)) * scale
    start = 0
    for out in outs:
        stop = start + out.shape[1]
        out[...] = total[:, start:stop]
        start = stop


def step_pairs(mesh_shape, lon_by, lat_by):
    lons, lats = mesh_shape
    return [
        (i * lats + j, (i + lon_by) % lons * lats + (j + lat_by) % lats)
        for i in range(lons)
        for j in range(lats)
    ]


def exchange(quads, sizes, by):
    axes = ("lon", "lat")
    near = lax.ppermute(quads[1], axes, step_pairs(sizes, by, 0))
    side = lax.ppermute(quads[2], axes, step_pairs(sizes, 0, by))
    far = lax.ppermute(quads[3], axes, step_pairs(sizes, by, by))
    return [quads[0], near, side, far]


def swap(value, axis, length, bit):
    return lax.ppermute(value, axis, [(i, i ^ bit) for i in range(length)])


def sum_over(keep, send, sizes):
    lons, lats = sizes
    total = keep + swap(send, "lon", lons, 1)
    steps = [("lon", lons, bit) for bit in powers(2, lons)]
    steps += [("lat", lats, bit) for bit in powers(1, lats)]
    for axis, length, bit in steps:
        raw = total.astype(bf16)
        other = swap(raw, axis, length, bit)
        total = raw.astype(f32) + other.astype(f32)
    return total, swap(total, "lon", lons, 1)


def powers(bit, length):
    while bit < length:
        yield bit
        bit *= 2


def finish_kernel(mine_ref, other_ref, *outs, scale):
    half = mine_ref.shape[1]
    odd = lax.axis_index("lon") % 2

    def write(first, second):
        start = 0
        for out in outs:
            stop = start + out.shape[1]
            if start < half:
                cut = min(stop, half)
                out[:, : cut - start] = first[:, start:cut] * scale
            if stop > half:
                cut = max(start, half)
                out[:, cut - start :] = second[:, cut - half : stop - half] * scale
            start = stop

    @pl.when(odd == 0)
    def _():
        write(mine_ref, other_ref)

    @pl.when(odd == 1)
    def _():
        write(other_ref, mine_ref)


def on_device(sizes):
    def layer(
        latent, cotangent, mask_ids, position_bias, norm_gain,
        w_qkv, qkv_down, qkv_up, w_proj, proj_down, proj_up,
    ):
        levels, lat_rows, lon_cols, width = latent.shape
        assert (lat_rows, lon_cols) == (WIN_LAT, WIN_LON)
        windows = levels // WIN_LEV
        total = windows * WINDOW
        rank = qkv_down.shape[0]
        quarter = struct((HALF_LAT, HALF_LON, levels, width), bf16)
        columns = pltpu.VMEM((width // LANES, total, LANES), f32)
        x_quads, g_quads = pack(latent.transpose(1, 2, 0, 3), cotangent.transpose(1, 2, 0, 3))
        x_quads = exchange(x_quads, sizes, -1)
        g_quads = exchange(g_quads, sizes, -1)
        key_cols, query_cols, *weights = score_columns(
            position_bias,
            mask_ids,
            (norm_gain[None, :], w_qkv, qkv_down, qkv_up, w_proj, proj_down, proj_up),
        )
        gain, w_qkv, qkv_down, qkv_up, w_proj, proj_down, proj_up = weights
        (
            o0, o1, o2, o3, unit, inv_std, normed, low, qkv, probs, attn, low_proj,
        ) = call(
            forward_kernel,
            [quarter] * 4
            + [
                struct((total, width), f32),
                struct((total, 1), f32),
                struct((total, width), bf16),
                struct((total, rank), bf16),
                struct((total, 3 * width), bf16),
                struct((windows * HEADS, WINDOW, WINDOW), f32),
                struct((total, width), bf16),
                struct((total, rank), bf16),
            ],
            [columns, pltpu.VMEM((total, width), f32)],
            name="forward",
        )(*x_quads, key_cols, query_cols, *weights)
        out_quads = exchange((o0, o1, o2, o3), sizes, 1)
        grad, d_qkv, d_low, keep, send = call(
            backward_kernel,
            [
                struct((total, width), f32),
                struct((total, 3 * width), bf16),
                struct((total, rank), bf16),
                struct((rank, 3 * width), f32),
                struct((rank, 3 * width), f32),
            ],
            [columns],
            name="backward",
        )(*g_quads, normed, low, qkv, probs, attn, low_proj, qkv_up, w_proj, proj_down, proj_up)
        sums = sum_over(keep, send, sizes)
        back = call(norm_kernel, [quarter] * 4, [columns], name="norm_back")(
            grad, d_qkv, d_low, unit, inv_std, gain, w_qkv, qkv_down
        )
        back_quads = exchange(back, sizes, 1)
        shape = (lat_rows, lon_cols, levels, width)
        output = unpack(out_quads, shape).transpose(2, 0, 1, 3)
        latent_grad = unpack(back_quads, shape).transpose(2, 0, 1, 3)
        grad_scale = 1.0 / math.sqrt(levels * lat_rows * lon_cols * sizes[0] * sizes[1])
        down, up, down_proj, up_proj = call(
            functools.partial(finish_kernel, scale=grad_scale),
            [struct((rank, n * width), f32) for n in (1, 3, 1, 1)],
            vmem=2,
            name="finish",
        )(*sums)
        return (output, latent_grad, down, up, down_proj, up_proj)

    return layer


def solution(mesh):
    block = P("runs", "lat", "lon", None)
    sizes = (mesh.shape["lon"], mesh.shape["lat"])
    return jax.shard_map(
        on_device(sizes),
        mesh=mesh,
        in_specs=(block, block, P("runs", "lat", "lon")) + (P(),) * 8,
        out_specs=(block, block) + (P("runs", None),) * 4,
        check_vma=False,
    )
```

time: 75.6 us -> 49.7 us (0.66)
  Pallas kernels: 33.2 us -> 15.6 us
  local copies, waits for them, and re-layouts: 13.6 us -> 0 us
  waiting for transfers between devices: 10.3 us -> 14.8 us
  starting transfers between devices: 16.2 us -> 18.3 us
  other arithmetic: 1 us -> 0.06 us
    pallas_call x8, Pallas kernels: 33.2 us -> 15.6 us  [the longest x1 5.29 us: layer(): call(backward_kernel, [struct((total, width), f32), struct((total, 3 * wi...]
    unnamed x34 -> x0, local copies, waits for them, and re-layouts: 10 us -> none
    ppermute x4 -> x5, waiting for transfers between devices: 4.75 us -> 10.9 us  [swap(): return lax.ppermute(value, axis, [(i, i ^ bit) for i in range(length)])]
    ppermute x4, starting transfers between devices: 1.54 us -> 4.82 us  [exchange(): far = lax.ppermute(quads[3], axes, step_pairs(sizes, by, by))]
    ppermute x4 -> x5, starting transfers between devices: 5.17 us -> 2 us  [swap(): return lax.ppermute(value, axis, [(i, i ^ bit) for i in range(length)])]
    ppermute x4, starting transfers between devices: 4.51 us -> 7.54 us  [exchange(): side = lax.ppermute(quads[2], axes, step_pairs(sizes, 0, by))]
    ppermute x4, waiting for transfers between devices: 4.07 us -> 2.59 us  [exchange(): far = lax.ppermute(quads[3], axes, step_pairs(sizes, by, by))]
    another operation x2 -> x0, local copies, waits for them, and re-layouts: 1.46 us -> none  [the longest x1 0.77 us: score_table(): ids[:, :, None]]
  transfers between devices with their start and end apart: 16 -> 17, of which waited for: 7 -> 7; matrix products, arithmetic and copies ran while one was open for 11% -> 0% of each run, Pallas kernels for 31% -> 17%
where the time goes in v2:
time: 49.7 us; the launch traced here: 49.5 us
  starting transfers between devices  18.3 us (37%)
  Pallas kernels  15.6 us (31%)
  waiting for transfers between devices  14.8 us (30%)
  between operations  0.77 us (2%)
    ppermute x5, waiting for transfers between devices, swap(): return lax.ppermute(value, axis, [(i, i ^ bit) for i in range(length)])  10.9 us
    ppermute x4, starting transfers between devices, exchange(): side = lax.ppermute(quads[2], axes, step_pairs(sizes, 0, by))  7.54 us
    pallas_call x1, Pallas kernels, layer(): call(backward_kernel, [struct((total, width), f32), struct((total, 3 * wi...  5.29 us
    ppermute x4, starting transfers between devices, exchange(): far = lax.ppermute(quads[3], axes, step_pairs(sizes, by, by))  4.82 us
    ppermute x4, starting transfers between devices, exchange(): near = lax.ppermute(quads[1], axes, step_pairs(sizes, by, 0))  3.91 us
    pallas_call x1, Pallas kernels, layer(): call(forward_kernel, [quarter] * 4 + [struct((total, width), f32), struct...  3.75 us
    ppermute x4, waiting for transfers between devices, exchange(): far = lax.ppermute(quads[3], axes, step_pairs(sizes, by, by))  2.59 us
    pallas_call x1, Pallas kernels, score_columns(): call(functools.partial(table_kernel, count=len(weights)), [struct((window...  2.25 us
  transfers between devices with their start and end apart: 17, of which 7 were waited for; matrix products, arithmetic and copies ran while one was open for 0% of the time, Pallas kernels for 17%

profile of v2, /device:TPU:0, one launch (start us, length us, event | category | flops | bytes accessed | tf_op | source)
XLA Modules:
  0.0 49.5 jit_solution(10820806117185930460)
XLA Ops:
  0.6 1.2 %pack.1 = (bf16[3,6,4,512]{3,2,1,0:T(4,128)(2,1)S(1)}, bf16[3,6,4,512]{3,2,1,0:T(4,128)(2,1)S(1)}, bf16[3,6,4,512]{3,2,1,0:T(4,128)(2,1)S(1)}, bf16[3,6,4,512]{3...) custom-call(bf16[6,12,4,512]{3,2,1,0:T(4,128)(2,1)} %bitcast.6, ...), custom_call_target="tpu_custom_call" | custom-call | tf_op jit(solution)/shard_map/pack/pallas_call | solution.py:85
  1.8 2.5 %collective-permute-start = (bf16[3,6,4,512]{3,2,1,0:T(4,128)(2,1)S(1)}, bf16[3,6,4,512]{3,2,1,0:T(4,128)(2,1)S(1)}, u32[]{:S(2)}, u32[]{:S(2)}) collective-permute-start(bf16[3,6,4,512]{3,2,1,0:T(4,128)(2,1)S(1)} %get-tuple-element.49), channel_id=1, source_target_pairs={{0,12},{1,13},{2,14},{3,15},{4,0},{5,1},{6,2},{7,3},{8,4},{9,5},{1... | collective-permute-start | bytes 221192 | tf_op jit(solution)/shard_map/ppermute | solution.py:422
  4.3 3.6 %collective-permute-start.1 = (bf16[3,6,4,512]{3,2,1,0:T(4,128)(2,1)S(1)}, bf16[3,6,4,512]{3,2,1,0:T(4,128)(2,1)S(1)}, u32[]{:S(2)}, u32[]{:S(2)}) collective-permute-start(bf16[3,6,4,512]{3,2,1,0:T(4,128)(2,1)S(1)} %get-tuple-element.50), channel_id=1, source_target_pairs={{0,3},{1,0},{2,1},{3,2},{4,7},{5,4},{6,5},{7,6},{8,11},{9,8},{10,9... | collective-permute-start | bytes 221192 | tf_op jit(solution)/shard_map/ppermute | solution.py:423
  9.2 2.0 %collective-permute-start.8 = (bf16[3,6,4,512]{3,2,1,0:T(4,128)(2,1)S(1)}, bf16[3,6,4,512]{3,2,1,0:T(4,128)(2,1)S(1)}, u32[]{:S(2)}, u32[]{:S(2)}) collective-permute-start(bf16[3,6,4,512]{3,2,1,0:T(4,128)(2,1)S(1)} %get-tuple-element.68), channel_id=1, source_target_pairs={{0,15},{1,12},{2,13},{3,14},{4,3},{5,0},{6,1},{7,2},{8,7},{9,4},{1... | collective-permute-start | bytes 221192 | tf_op jit(solution)/shard_map/ppermute | solution.py:424
  11.1 2.3 %table.1 = (bf16[2,144,1024]{2,1,0:T(8,128)(2,1)S(1)}, bf16[2,144,128]{2,1,0:T(8,128)(2,1)S(1)}, f32[1,512]{1,0:T(1,128)S(1)}, bf16[512,1536]{1,0:T(8,128)(2,1)S...) custom-call(f32[8,37]{1,0:T(8,128)} %refs_0_.1, ...), custom_call_target="tpu_custom_call" | custom-call | tf_op jit(solution)/shard_map/table/pallas_call | solution.py:222
  13.4 3.7 %forward.1 = (bf16[3,6,4,512]{3,2,1,0:T(4,128)(2,1)S(1)}, bf16[3,6,4,512]{3,2,1,0:T(4,128)(2,1)S(1)}, bf16[3,6,4,512]{3,2,1,0:T(4,128)(2,1)S(1)}, bf16[3,6,4,512...) custom-call(bf16[3,6,4,512]{3,2,1,0:T(4,128)(2,1)S(1)} %get-tuple-el, ...), custom_call_target="tpu_custom_call" | custom-call | tf_op jit(solution)/shard_map/forward/pallas_call | solution.py:498
  17.2 5.3 %backward.1 = (f32[288,512]{1,0:T(8,128)S(1)}, bf16[288,1536]{1,0:T(8,128)(2,1)S(1)}, bf16[288,16]{1,0:T(8,128)(2,1)S(1)}, f32[16,1536]{1,0:T(8,128)S(1)}, f32[16,1536]{1,0:T(8,128)S(1)}) custom-call(bf16[3,6,4,512]{3,2,1,0:T(4,128)(2,1)S(1)} %get-tuple-element.65.g0, bf16[3,6,4,512]{3,2,1,0:T(4,128)(2,1)S(1)} %collective-permute-done.6.g1, ...), custom_call_target="tpu_custom_call" | custom-call | tf_op jit(solution)/shard_map/backward/pallas_call | solution.py:515
  22.5 1.3 %collective-permute-done.12 = f32[16,1536]{1,0:T(8,128)S(1)} collective-permute-done((f32[16,1536]{1,0:T(8,128)S(1)}, f32[16,1536]{1,0:T(8,128)S(1)}, u32[]{:S(2)}, u32[]{:S(2)}) %collective-permute-start.12) | collective-permute-done | bytes 98336 | tf_op jit(solution)/shard_map/ppermute | solution.py:429
  23.8 0.6 %collective-permute-start.13 = (bf16[16,1536]{1,0:T(8,128)(2,1)S(1)}, bf16[16,1536]{1,0:T(8,128)(2,1)S(1)}, u32[]{:S(2)}, u32[]{:S(2)}) collective-permute-start(bf16[16,1536]{1,0:T(8,128)(2,1)S(1)} %add_convert_fusion.2), channel_id=1, source_target_pairs={{0,8},{4,12},{8,0},{12,4},{1,9},{5,13},{9,1},{13,5},{2,10},{6,14},... | collective-permute-start | bytes 147464 | tf_op jit(solution)/shard_map/ppermute | solution.py:429
  24.4 3.5 %collective-permute-done.13 = bf16[16,1536]{1,0:T(8,128)(2,1)S(1)} collective-permute-done((bf16[16,1536]{1,0:T(8,128)(2,1)S(1)}, bf16[16,1536]{1,0:T(8,128)(2,1)S(1)}, u32[]{:S(2)}, u32[]{:S(2)}) %collective-permute-start.13) | collective-permute-done | bytes 49184 | tf_op jit(solution)/shard_map/ppermute | solution.py:429
  28.1 4.1 %collective-permute-done.14 = bf16[16,1536]{1,0:T(8,128)(2,1)S(1)} collective-permute-done((bf16[16,1536]{1,0:T(8,128)(2,1)S(1)}, bf16[16,1536]{1,0:T(8,128)(2,1)S(1)}, u32[]{:S(2)}, u32[]{:S(2)}) %collective-permute-start.14) | collective-permute-done | bytes 49184 | tf_op jit(solution)/shard_map/ppermute | solution.py:429
  32.2 1.2 %collective-permute-start.15 = (bf16[16,1536]{1,0:T(8,128)(2,1)S(1)}, bf16[16,1536]{1,0:T(8,128)(2,1)S(1)}, u32[]{:S(2)}, u32[]{:S(2)}) collective-permute-start(bf16[16,1536]{1,0:T(8,128)(2,1)S(1)} %add_convert_fusion), channel_id=1, source_target_pairs={{0,2},{1,3},{2,0},{3,1},{4,6},{5,7},{6,4},{7,5},{8,10},{9,11},{10,... | collective-permute-start | bytes 147464 | tf_op jit(solution)/shard_map/ppermute | solution.py:429
  33.4 2.0 %collective-permute-start.4 = (bf16[3,6,4,512]{3,2,1,0:T(4,128)(2,1)S(1)}, bf16[3,6,4,512]{3,2,1,0:T(4,128)(2,1)S(1)}, u32[]{:S(2)}, u32[]{:S(2)}) collective-permute-start(bf16[3,6,4,512]{3,2,1,0:T(4,128)(2,1)S(1)} %get-tuple-element.63), channel_id=1, source_target_pairs={{0,1},{1,2},{2,3},{3,0},{4,5},{5,6},{6,7},{7,4},{8,9},{9,10},{10,1... | collective-permute-start | bytes 221192 | tf_op jit(solution)/shard_map/ppermute | solution.py:423
  35.4 2.0 %collective-permute-done.15 = bf16[16,1536]{1,0:T(8,128)(2,1)S(1)} collective-permute-done((bf16[16,1536]{1,0:T(8,128)(2,1)S(1)}, bf16[16,1536]{1,0:T(8,128)(2,1)S(1)}, u32[]{:S(2)}, u32[]{:S(2)}) %collective-permute-start.15) | collective-permute-done | bytes 49184 | tf_op jit(solution)/shard_map/ppermute | solution.py:429
  37.7 0.9 %norm_back.1 = (bf16[3,6,4,512]{3,2,1,0:T(4,128)(2,1)S(1)}, bf16[3,6,4,512]{3,2,1,0:T(4,128)(2,1)S(1)}, bf16[3,6,4,512]{3,2,1,0:T(4,128)(2,1)S(1)}, bf16[3,6,4,512]{3,2,1,0:T(4,128)(2,1)S(1)}) custom-call(f32[288,512]{1,0:T(8,128)S(1)} %get-tuple-element.75.grad_ref, bf16[288,1536]{1,0:T(8,128)(2,1)S(1)} %get-tuple-element.76.d_qkv_ref, ...), custom_call_target="tpu_custom_call" | custom-call | tf_op jit(solution)/shard_map/norm_back/pallas_call | solution.py:528
  38.6 0.9 %collective-permute-start.9 = (bf16[3,6,4,512]{3,2,1,0:T(4,128)(2,1)S(1)}, bf16[3,6,4,512]{3,2,1,0:T(4,128)(2,1)S(1)}, u32[]{:S(2)}, u32[]{:S(2)}) collective-permute-start(bf16[3,6,4,512]{3,2,1,0:T(4,128)(2,1)S(1)} %get-tuple-element.81), channel_id=1, source_target_pairs={{0,4},{1,5},{2,6},{3,7},{4,8},{5,9},{6,10},{7,11},{8,12},{9,13},{1... | collective-permute-start | bytes 221192 | tf_op jit(solution)/shard_map/ppermute | solution.py:422
  39.5 1.5 %collective-permute-start.10 = (bf16[3,6,4,512]{3,2,1,0:T(4,128)(2,1)S(1)}, bf16[3,6,4,512]{3,2,1,0:T(4,128)(2,1)S(1)}, u32[]{:S(2)}, u32[]{:S(2)}) collective-permute-start(bf16[3,6,4,512]{3,2,1,0:T(4,128)(2,1)S(1)} %get-tuple-element.82), channel_id=1, source_target_pairs={{0,1},{1,2},{2,3},{3,0},{4,5},{5,6},{6,7},{7,4},{8,9},{9,10},{10,1... | collective-permute-start | bytes 221192 | tf_op jit(solution)/shard_map/ppermute | solution.py:423
  41.0 2.4 %collective-permute-start.11 = (bf16[3,6,4,512]{3,2,1,0:T(4,128)(2,1)S(1)}, bf16[3,6,4,512]{3,2,1,0:T(4,128)(2,1)S(1)}, u32[]{:S(2)}, u32[]{:S(2)}) collective-permute-start(bf16[3,6,4,512]{3,2,1,0:T(4,128)(2,1)S(1)} %get-tuple-element.83), channel_id=1, source_target_pairs={{0,5},{1,6},{2,7},{3,4},{4,9},{5,10},{6,11},{7,8},{8,13},{9,14},{1... | collective-permute-start | bytes 221192 | tf_op jit(solution)/shard_map/ppermute | solution.py:424
  43.4 1.0 %collective-permute-done.5.q3 = bf16[3,6,4,512]{3,2,1,0:T(4,128)(2,1)S(1)} collective-permute-done((bf16[3,6,4,512]{3,2,1,0:T(4,128)(2,1)S(1)}, bf16[3,6,4,512]{3,2,1,0:T(4,128)(2,1)S(1)}, u32[]{:S(2)}, u32[]{:S(2)}) %collective-permute-start.5) | collective-permute-done | bytes 73760 | tf_op jit(solution)/shard_map/ppermute | solution.py:424
  44.4 0.7 %unpack.2 = bf16[6,12,4,512]{3,2,1,0:T(4,128)(2,1)} custom-call(bf16[3,6,4,512]{3,2,1,0:T(4,128)(2,1)S(1)} %get-tuple-element.61.q0, bf16[3,6,4,512]{3,2,1,0:T(4,128)(2,1)S(1)} %collective-permute-done.3.q1, bf16[3,6,4,512]{3,2,1,0:T(4,128)(2,1)S(1)} %collective-permute-done.4.q2, bf16[3,6,4,512]{3,2,1,0:T(4,128)(2,1)S(1)} %collective-permute-done.5.q3), custom_call_target="tpu_custom_call" | custom-call | tf_op jit(solution)/shard_map/unpack/pallas_call | solution.py:104
  45.1 1.2 %collective-permute-done.10.q2 = bf16[3,6,4,512]{3,2,1,0:T(4,128)(2,1)S(1)} collective-permute-done((bf16[3,6,4,512]{3,2,1,0:T(4,128)(2,1)S(1)}, bf16[3,6,4,512]{3,2,1,0:T(4,128)(2,1)S(1)}, u32[]{:S(2)}, u32[]{:S(2)}) %collective-permute-start.10) | collective-permute-done | bytes 73760 | tf_op jit(solution)/shard_map/ppermute | solution.py:423
  46.4 1.6 %collective-permute-done.11.q3 = bf16[3,6,4,512]{3,2,1,0:T(4,128)(2,1)S(1)} collective-permute-done((bf16[3,6,4,512]{3,2,1,0:T(4,128)(2,1)S(1)}, bf16[3,6,4,512]{3,2,1,0:T(4,128)(2,1)S(1)}, u32[]{:S(2)}, u32[]{:S(2)}) %collective-permute-start.11) | collective-permute-done | bytes 73760 | tf_op jit(solution)/shard_map/ppermute | solution.py:424
  48.0 0.7 %unpack.3 = bf16[6,12,4,512]{3,2,1,0:T(4,128)(2,1)} custom-call(bf16[3,6,4,512]{3,2,1,0:T(4,128)(2,1)S(1)} %get-tuple-element.80.q0, bf16[3,6,4,512]{3,2,1,0:T(4,128)(2,1)S(1)} %collective-permute-done.9.q1, bf16[3,6,4,512]{3,2,1,0:T(4,128)(2,1)S(1)} %collective-permute-done.10.q2, bf16[3,6,4,512]{3,2,1,0:T(4,128)(2,1)S(1)} %collective-permute-done.11.q3), custom_call_target="tpu_custom_call" | custom-call | tf_op jit(solution)/shard_map/unpack/pallas_call | solution.py:104
  48.8 0.7 %finish.1 = (f32[16,512]{1,0:T(8,128)}, f32[16,1536]{1,0:T(8,128)}, f32[16,512]{1,0:T(8,128)}, f32[16,512]{1,0:T(8,128)}) custom-call(f32[16,1536]{1,0:T(8,128)S(1)} %convert_add_fusion.mine_ref, f32[16,1536]{1,0:T(8,128)S(1)} %collective-permute-done.16.other_ref), custom_call_target="tpu_custom_call" | custom-call | tf_op jit(solution)/shard_map/finish/pallas_call | solution.py:536
  (22 shorter events, 1.6 us)
Async XLA Ops:
  1.8 7.3 %collective-permute-start = (bf16[3,6,4,512]{3,2,1,0:T(4,128)(2,1)S(1)}, bf16[3,6,4,512]{3,2,1,0:T(4,128)(2,1)S(1)}, u32[]{:S(2)}, u32[]{:S(2)}) collective-permute-start(bf16[3,6,4,512]{3,2,1,0:T(4,128)(2,1)S(1)} %get-tuple-element.49), channel_id=1, source_target_pairs={{0,12},{1,13},{2,14},{3,15},{4,0},{5,1},{6,2},{7,3},{8,4},{9,5},{1... | collective-permute-start | bytes 221192 | tf_op jit(solution)/shard_map/ppermute | solution.py:422
  4.3 9.1 %collective-permute-start.1 = (bf16[3,6,4,512]{3,2,1,0:T(4,128)(2,1)S(1)}, bf16[3,6,4,512]{3,2,1,0:T(4,128)(2,1)S(1)}, u32[]{:S(2)}, u32[]{:S(2)}) collective-permute-start(bf16[3,6,4,512]{3,2,1,0:T(4,128)(2,1)S(1)} %get-tuple-element.50), channel_id=1, source_target_pairs={{0,3},{1,0},{2,1},{3,2},{4,7},{5,4},{6,5},{7,6},{8,11},{9,8},{10,9... | collective-permute-start | bytes 221192 | tf_op jit(solution)/shard_map/ppermute | solution.py:423
  7.9 5.5 %collective-permute-start.2 = (bf16[3,6,4,512]{3,2,1,0:T(4,128)(2,1)S(1)}, bf16[3,6,4,512]{3,2,1,0:T(4,128)(2,1)S(1)}, u32[]{:S(2)}, u32[]{:S(2)}) collective-permute-start(bf16[3,6,4,512]{3,2,1,0:T(4,128)(2,1)S(1)} %get-tuple-element.51), channel_id=1, source_target_pairs={{0,15},{1,12},{2,13},{3,14},{4,3},{5,0},{6,1},{7,2},{8,7},{9,4},{1... | collective-permute-start | bytes 221192 | tf_op jit(solution)/shard_map/ppermute | solution.py:424
  8.2 9.0 %collective-permute-start.6 = (bf16[3,6,4,512]{3,2,1,0:T(4,128)(2,1)S(1)}, bf16[3,6,4,512]{3,2,1,0:T(4,128)(2,1)S(1)}, u32[]{:S(2)}, u32[]{:S(2)}) collective-permute-start(bf16[3,6,4,512]{3,2,1,0:T(4,128)(2,1)S(1)} %get-tuple-element.66), channel_id=1, source_target_pairs={{0,12},{1,13},{2,14},{3,15},{4,0},{5,1},{6,2},{7,3},{8,4},{9,5},{1... | collective-permute-start | bytes 221192 | tf_op jit(solution)/shard_map/ppermute | solution.py:422
  8.7 8.5 %collective-permute-start.7 = (bf16[3,6,4,512]{3,2,1,0:T(4,128)(2,1)S(1)}, bf16[3,6,4,512]{3,2,1,0:T(4,128)(2,1)S(1)}, u32[]{:S(2)}, u32[]{:S(2)}) collective-permute-start(bf16[3,6,4,512]{3,2,1,0:T(4,128)(2,1)S(1)} %get-tuple-element.67), channel_id=1, source_target_pairs={{0,3},{1,0},{2,1},{3,2},{4,7},{5,4},{6,5},{7,6},{8,11},{9,8},{10,9... | collective-permute-start | bytes 221192 | tf_op jit(solution)/shard_map/ppermute | solution.py:423
  9.2 8.0 %collective-permute-start.8 = (bf16[3,6,4,512]{3,2,1,0:T(4,128)(2,1)S(1)}, bf16[3,6,4,512]{3,2,1,0:T(4,128)(2,1)S(1)}, u32[]{:S(2)}, u32[]{:S(2)}) collective-permute-start(bf16[3,6,4,512]{3,2,1,0:T(4,128)(2,1)S(1)} %get-tuple-element.68), channel_id=1, source_target_pairs={{0,15},{1,12},{2,13},{3,14},{4,3},{5,0},{6,1},{7,2},{8,7},{9,4},{1... | collective-permute-start | bytes 221192 | tf_op jit(solution)/shard_map/ppermute | solution.py:424
  22.5 1.3 %collective-permute-start.12 = (f32[16,1536]{1,0:T(8,128)S(1)}, f32[16,1536]{1,0:T(8,128)S(1)}, u32[]{:S(2)}, u32[]{:S(2)}) collective-permute-start(f32[16,1536]{1,0:T(8,128)S(1)} %get-tuple-element.85), channel_id=1, source_target_pairs={{0,4},{4,0},{8,12},{12,8},{1,5},{5,1},{9,13},{13,9},{2,6},{6,2},{1... | collective-permute-start | bytes 294920 | tf_op jit(solution)/shard_map/ppermute | solution.py:429
  23.8 4.2 %collective-permute-start.13 = (bf16[16,1536]{1,0:T(8,128)(2,1)S(1)}, bf16[16,1536]{1,0:T(8,128)(2,1)S(1)}, u32[]{:S(2)}, u32[]{:S(2)}) collective-permute-start(bf16[16,1536]{1,0:T(8,128)(2,1)S(1)} %add_convert_fusion.2), channel_id=1, source_target_pairs={{0,8},{4,12},{8,0},{12,4},{1,9},{5,13},{9,1},{13,5},{2,10},{6,14},... | collective-permute-start | bytes 147464 | tf_op jit(solution)/shard_map/ppermute | solution.py:429
  28.0 4.2 %collective-permute-start.14 = (bf16[16,1536]{1,0:T(8,128)(2,1)S(1)}, bf16[16,1536]{1,0:T(8,128)(2,1)S(1)}, u32[]{:S(2)}, u32[]{:S(2)}) collective-permute-start(bf16[16,1536]{1,0:T(8,128)(2,1)S(1)} %add_convert_fusion.1), channel_id=1, source_target_pairs={{0,1},{1,0},{2,3},{3,2},{4,5},{5,4},{6,7},{7,6},{8,9},{9,8},{10,11... | collective-permute-start | bytes 147464 | tf_op jit(solution)/shard_map/ppermute | solution.py:429
  32.2 5.3 %collective-permute-start.15 = (bf16[16,1536]{1,0:T(8,128)(2,1)S(1)}, bf16[16,1536]{1,0:T(8,128)(2,1)S(1)}, u32[]{:S(2)}, u32[]{:S(2)}) collective-permute-start(bf16[16,1536]{1,0:T(8,128)(2,1)S(1)} %add_convert_fusion), channel_id=1, source_target_pairs={{0,2},{1,3},{2,0},{3,1},{4,6},{5,7},{6,4},{7,5},{8,10},{9,11},{10,... | collective-permute-start | bytes 147464 | tf_op jit(solution)/shard_map/ppermute | solution.py:429
  33.4 6.2 %collective-permute-start.3 = (bf16[3,6,4,512]{3,2,1,0:T(4,128)(2,1)S(1)}, bf16[3,6,4,512]{3,2,1,0:T(4,128)(2,1)S(1)}, u32[]{:S(2)}, u32[]{:S(2)}) collective-permute-start(bf16[3,6,4,512]{3,2,1,0:T(4,128)(2,1)S(1)} %get-tuple-element.62), channel_id=1, source_target_pairs={{0,4},{1,5},{2,6},{3,7},{4,8},{5,9},{6,10},{7,11},{8,12},{9,13},{1... | collective-permute-start | bytes 221192 | tf_op jit(solution)/shard_map/ppermute | solution.py:422
  33.4 7.6 %collective-permute-start.4 = (bf16[3,6,4,512]{3,2,1,0:T(4,128)(2,1)S(1)}, bf16[3,6,4,512]{3,2,1,0:T(4,128)(2,1)S(1)}, u32[]{:S(2)}, u32[]{:S(2)}) collective-permute-start(bf16[3,6,4,512]{3,2,1,0:T(4,128)(2,1)S(1)} %get-tuple-element.63), channel_id=1, source_target_pairs={{0,1},{1,2},{2,3},{3,0},{4,5},{5,6},{6,7},{7,4},{8,9},{9,10},{10,1... | collective-permute-start | bytes 221192 | tf_op jit(solution)/shard_map/ppermute | solution.py:423
  37.5 11.3 %collective-permute-start.16 = (f32[16,1536]{1,0:T(8,128)S(1)}, f32[16,1536]{1,0:T(8,128)S(1)}, u32[]{:S(2)}, u32[]{:S(2)}) collective-permute-start(f32[16,1536]{1,0:T(8,128)S(1)} %convert_add_fusion.mine_ref), channel_id=1, source_target_pairs={{0,4},{4,0},{8,12},{12,8},{1,5},{5,1},{9,13},{13,9},{2,6},{6,2},{1... | collective-permute-start | bytes 294920 | tf_op jit(solution)/shard_map/ppermute | solution.py:429
  37.5 6.9 %collective-permute-start.5 = (bf16[3,6,4,512]{3,2,1,0:T(4,128)(2,1)S(1)}, bf16[3,6,4,512]{3,2,1,0:T(4,128)(2,1)S(1)}, u32[]{:S(2)}, u32[]{:S(2)}) collective-permute-start(bf16[3,6,4,512]{3,2,1,0:T(4,128)(2,1)S(1)} %get-tuple-element.64), channel_id=1, source_target_pairs={{0,5},{1,6},{2,7},{3,4},{4,9},{5,10},{6,11},{7,8},{8,13},{9,14},{1... | collective-permute-start | bytes 221192 | tf_op jit(solution)/shard_map/ppermute | solution.py:424
  38.6 6.5 %collective-permute-start.9 = (bf16[3,6,4,512]{3,2,1,0:T(4,128)(2,1)S(1)}, bf16[3,6,4,512]{3,2,1,0:T(4,128)(2,1)S(1)}, u32[]{:S(2)}, u32[]{:S(2)}) collective-permute-start(bf16[3,6,4,512]{3,2,1,0:T(4,128)(2,1)S(1)} %get-tuple-element.81), channel_id=1, source_target_pairs={{0,4},{1,5},{2,6},{3,7},{4,8},{5,9},{6,10},{7,11},{8,12},{9,13},{1... | collective-permute-start | bytes 221192 | tf_op jit(solution)/shard_map/ppermute | solution.py:422
  39.5 6.9 %collective-permute-start.10 = (bf16[3,6,4,512]{3,2,1,0:T(4,128)(2,1)S(1)}, bf16[3,6,4,512]{3,2,1,0:T(4,128)(2,1)S(1)}, u32[]{:S(2)}, u32[]{:S(2)}) collective-permute-start(bf16[3,6,4,512]{3,2,1,0:T(4,128)(2,1)S(1)} %get-tuple-element.82), channel_id=1, source_target_pairs={{0,1},{1,2},{2,3},{3,0},{4,5},{5,6},{6,7},{7,4},{8,9},{9,10},{10,1... | collective-permute-start | bytes 221192 | tf_op jit(solution)/shard_map/ppermute | solution.py:423
  41.0 7.0 %collective-permute-start.11 = (bf16[3,6,4,512]{3,2,1,0:T(4,128)(2,1)S(1)}, bf16[3,6,4,512]{3,2,1,0:T(4,128)(2,1)S(1)}, u32[]{:S(2)}, u32[]{:S(2)}) collective-permute-start(bf16[3,6,4,512]{3,2,1,0:T(4,128)(2,1)S(1)} %get-tuple-element.83), channel_id=1, source_target_pairs={{0,5},{1,6},{2,7},{3,4},{4,9},{5,10},{6,11},{7,8},{8,13},{9,14},{1... | collective-permute-start | bytes 221192 | tf_op jit(solution)/shard_map/ppermute | solution.py:424

commit v3 on v2

--- a/solution.py
+++ b/solution.py
@@ -17,6 +17,7 @@
 HALF_LON = WIN_LON // 2
 HALF_LEV = WIN_LEV // 2
 WINDOW = WIN_LEV * WIN_LAT * WIN_LON
+
 
 epsilon = 1e-05
 masked_value = -1e30
@@ -94,22 +95,37 @@
     return quads[:4], quads[4:]
 
 
-def unpack_kernel(q0, q1, q2, q3, out_ref, sems):
-    quads = (q0, q1, q2, q3)
-    for copy in run_copies([(quads[q], corner(out_ref, q)) for q in range(4)], sems):
+JOINED = (1, 2, 3)
+APART = tuple(quad for quad in range(1, 4) if quad not in JOINED)
+
+
+def unpack_kernel(*refs):
+    outs, sems = refs[-3:-1], refs[-1]
+    pairs = []
+    for i, quad in enumerate((0,) + APART):
+        for n in range(2):
+            pairs.append((refs[2 * i + n], corner(outs[n], quad)))
+    for i, quad in enumerate(JOINED):
+        for n in range(2):
+            pairs.append((refs[2 + 2 * len(APART) + i].at[n], corner(outs[n], quad)))
+    for copy in run_copies(pairs, sems):
         copy.wait()
 
 
-def unpack(quads, shape):
+def unpack(out, back, shape):
+    arrays = []
+    for quad in (0,) + APART:
+        arrays += [out[quad], back[quad]]
+    arrays += [back[quad] for quad in JOINED]
     return call(
         unpack_kernel,
-        struct(shape, bf16),
-        [pltpu.SemaphoreType.DMA((4,))],
+        [struct(shape, bf16)] * 2,
+        [pltpu.SemaphoreType.DMA((8,))],
         vmem=2,
-        in_specs=[ANY] * 4,
-        out_specs=ANY,
+        in_specs=[ANY] * len(arrays),
+        out_specs=[ANY] * 2,
         name="unpack",
-    )(*quads)
+    )(*arrays)
 
 
 AXES = (WIN_LEV, WIN_LAT, WIN_LON)
@@ -385,9 +401,16 @@
         send_ref[...] = raw[:, :half]
 
 
-def norm_kernel(
-    grad_ref, d_qkv_ref, d_low_ref, unit_ref, inv_ref, gain, w_qkv, qkv_down, o0, o1, o2, o3, scratch
-):
+def norm_kernel(*refs):
+    grad_ref, d_qkv_ref, d_low_ref, unit_ref, inv_ref, gain, w_qkv, qkv_down = refs[:8]
+    outgoing, refs = refs[8 : 8 + len(JOINED)], refs[8 + len(JOINED) :]
+    outs, scratch = list(refs[:4]), refs[4]
+    copies = []
+    if JOINED:
+        pairs = [(src, outs[quad].at[0]) for src, quad in zip(outgoing, JOINED)]
+        copies = run_copies(pairs, refs[5])
+        for quad in JOINED:
+            outs[quad] = outs[quad].at[1]
     d_normed = nt(d_qkv_ref[...], w_qkv[...]) + nn(d_low_ref[...], qkv_down[...])
     d_unit = d_normed * gain[...]
     unit = unit_ref[...]
@@ -396,16 +419,9 @@
         - jnp.mean(d_unit, axis=-1, keepdims=True)
         - unit * jnp.mean(d_unit * unit, axis=-1, keepdims=True)
     )
-    scatter_rows(grad_ref[...] + back, scratch, (o0, o1, o2, o3))
-
-
-def finish_kernel(a_ref, b_ref, *outs, scale):
-    total = (a_ref[...].astype(f32) + b_ref[...].astype(f32)) * scale
-    start = 0
-    for out in outs:
-        stop = start + out.shape[1]
-        out[...] = total[:, start:stop]
-        start = stop
+    scatter_rows(grad_ref[...] + back, scratch, outs)
+    for copy in copies:
+        copy.wait()
 
 
 def step_pairs(mesh_shape, lon_by, lat_by):
@@ -418,11 +434,12 @@
 
 
 def exchange(quads, sizes, by):
-    axes = ("lon", "lat")
-    near = lax.ppermute(quads[1], axes, step_pairs(sizes, by, 0))
-    side = lax.ppermute(quads[2], axes, step_pairs(sizes, 0, by))
-    far = lax.ppermute(quads[3], axes, step_pairs(sizes, by, by))
-    return [quads[0], near, side, far]
+    moved = dict(quads)
+    for quad in moved:
+        if quad:
+            pairs = step_pairs(sizes, by * (quad % 2), by * (quad // 2))
+            moved[quad] = lax.ppermute(moved[quad], ("lon", "lat"), pairs)
+    return moved
 
 
 def swap(value, axis, length, bit):
@@ -432,8 +449,8 @@
 def sum_over(keep, send, sizes):
     lons, lats = sizes
     total = keep + swap(send, "lon", lons, 1)
-    steps = [("lon", lons, bit) for bit in powers(2, lons)]
-    steps += [("lat", lats, bit) for bit in powers(1, lats)]
+    steps = [("lat", lats, bit) for bit in powers(1, lats)]
+    steps += [("lon", lons, bit) for bit in powers(2, lons)]
     for axis, length, bit in steps:
         raw = total.astype(bf16)
         other = swap(raw, axis, length, bit)
@@ -485,8 +502,8 @@
         quarter = struct((HALF_LAT, HALF_LON, levels, width), bf16)
         columns = pltpu.VMEM((width // LANES, total, LANES), f32)
         x_quads, g_quads = pack(latent.transpose(1, 2, 0, 3), cotangent.transpose(1, 2, 0, 3))
-        x_quads = exchange(x_quads, sizes, -1)
-        g_quads = exchange(g_quads, sizes, -1)
+        x_quads = exchange(enumerate(x_quads), sizes, -1).values()
+        g_quads = exchange(enumerate(g_quads), sizes, -1).values()
         key_cols, query_cols, *weights = score_columns(
             position_bias,
             mask_ids,
@@ -511,7 +528,7 @@
             [columns, pltpu.VMEM((total, width), f32)],
             name="forward",
         )(*x_quads, key_cols, query_cols, *weights)
-        out_quads = exchange((o0, o1, o2, o3), sizes, 1)
+        out = exchange({0: o0, **{q: (o1, o2, o3)[q - 1] for q in APART}}, sizes, 1)
         grad, d_qkv, d_low, keep, send = call(
             backward_kernel,
             [
@@ -525,13 +542,19 @@
             name="backward",
         )(*g_quads, normed, low, qkv, probs, attn, low_proj, qkv_up, w_proj, proj_down, proj_up)
         sums = sum_over(keep, send, sizes)
-        back = call(norm_kernel, [quarter] * 4, [columns], name="norm_back")(
-            grad, d_qkv, d_low, unit, inv_std, gain, w_qkv, qkv_down
-        )
-        back_quads = exchange(back, sizes, 1)
-        shape = (lat_rows, lon_cols, levels, width)
-        output = unpack(out_quads, shape).transpose(2, 0, 1, 3)
-        latent_grad = unpack(back_quads, shape).transpose(2, 0, 1, 3)
+        shapes = [quarter] * 4
+        for quad in JOINED:
+            shapes[quad] = struct((2,) + quarter.shape, bf16)
+        back = call(
+            norm_kernel,
+            shapes,
+            [columns] + [pltpu.SemaphoreType.DMA((len(JOINED),))] * bool(JOINED),
+            in_specs=[pl.BlockSpec()] * 8 + [ANY] * len(JOINED),
+            name="norm_back",
+        )(grad, d_qkv, d_low, unit, inv_std, gain, w_qkv, qkv_down, *[(o1, o2, o3)[q - 1] for q in JOINED])
+        back = exchange(enumerate(back), sizes, 1)
+        output, latent_grad = unpack(out, back, (lat_rows, lon_cols, levels, width))
+        output, latent_grad = (x.transpose(2, 0, 1, 3) for x in (output, latent_grad))
         grad_scale = 1.0 / math.sqrt(levels * lat_rows * lon_cols * sizes[0] * sizes[1])
         down, up, down_proj, up_proj = call(
             functools.partial(finish_kernel, scale=grad_scale),

time: 49.7 us -> 48.6 us (0.978)
  starting transfers between devices: 18.3 us -> 14.3 us
  waiting for transfers between devices: 14.8 us -> 18 us
    ppermute x12 -> x9, waiting for transfers between devices: 3.86 us -> 8.79 us  [exchange(): moved[quad] = lax.ppermute(moved[quad], ('lon', 'lat'), pairs)]
    ppermute x12 -> x9, starting transfers between devices: 16.3 us -> 12.1 us  [exchange(): moved[quad] = lax.ppermute(moved[quad], ('lon', 'lat'), pairs)]
    ppermute x5, waiting for transfers between devices: 10.9 us -> 9.25 us  [swap(): return lax.ppermute(value, axis, [(i, i ^ bit) for i in range(length)])]
    pallas_call x3 -> x2, Pallas kernels: 2.38 us -> 2.08 us  [the longest x1 1.2 us: layer(): call(norm_kernel, shapes, [columns] + [pltpu.SemaphoreType.DMA((len(JOINE...]
  transfers between devices with their start and end apart: 17 -> 14, of which waited for: 7 -> 6; matrix products, arithmetic and copies ran while one was open for 0% -> 0% of each run, Pallas kernels for 17% -> 17%
where the time goes in v3:
time: 48.6 us; the launch traced here: 48.4 us
  waiting for transfers between devices  18 us (37%)
  Pallas kernels  15.3 us (31%)
  starting transfers between devices  14.3 us (29%)
  between operations  0.75 us (2%)
    ppermute x9, starting transfers between devices, exchange(): moved[quad] = lax.ppermute(moved[quad], ('lon', 'lat'), pairs)  12.1 us
    ppermute x5, waiting for transfers between devices, swap(): return lax.ppermute(value, axis, [(i, i ^ bit) for i in range(length)])  9.25 us
    ppermute x9, waiting for transfers between devices, exchange(): moved[quad] = lax.ppermute(moved[quad], ('lon', 'lat'), pairs)  8.79 us
    pallas_call x1, Pallas kernels, layer(): call(backward_kernel, [struct((total, width), f32), struct((total, 3 * wi...  5.3 us
    pallas_call x1, Pallas kernels, layer(): call(forward_kernel, [quarter] * 4 + [struct((total, width), f32), struct...  3.75 us
    pallas_call x1, Pallas kernels, score_columns(): call(functools.partial(table_kernel, count=len(weights)), [struct((window...  2.25 us
    ppermute x5, starting transfers between devices, swap(): return lax.ppermute(value, axis, [(i, i ^ bit) for i in range(length)])  2.14 us
    pallas_call x1, Pallas kernels, pack(): call(pack_kernel, [struct((HALF_LAT, HALF_LON, levels, width), bf16)] * 8...  1.21 us
  transfers between devices with their start and end apart: 14, of which 6 were waited for; matrix products, arithmetic and copies ran while one was open for 0% of the time, Pallas kernels for 17%

profile of v3, /device:TPU:0, one launch (start us, length us, event | category | flops | bytes accessed | tf_op | source)
XLA Modules:
  0.0 48.4 jit_solution(516253779267671863)
XLA Ops:
  0.6 1.2 %pack.1 = (bf16[3,6,4,512]{3,2,1,0:T(4,128)(2,1)S(1)}, bf16[3,6,4,512]{3,2,1,0:T(4,128)(2,1)S(1)}, bf16[3,6,4,512]{3,2,1,0:T(4,128)(2,1)S(1)}, bf16[3,6,4,512]{3...) custom-call(bf16[6,12,4,512]{3,2,1,0:T(4,128)(2,1)} %bitcast.6, ...), custom_call_target="tpu_custom_call" | custom-call | tf_op jit(solution)/shard_map/pack/pallas_call | solution.py:86
  1.8 2.5 %collective-permute-start = (bf16[3,6,4,512]{3,2,1,0:T(4,128)(2,1)S(1)}, bf16[3,6,4,512]{3,2,1,0:T(4,128)(2,1)S(1)}, u32[]{:S(2)}, u32[]{:S(2)}) collective-permute-start(bf16[3,6,4,512]{3,2,1,0:T(4,128)(2,1)S(1)} %get-tuple-element.51), channel_id=1, source_target_pairs={{0,12},{1,13},{2,14},{3,15},{4,0},{5,1},{6,2},{7,3},{8,4},{9,5},{1... | collective-permute-start | bytes 221192 | tf_op jit(solution)/shard_map/ppermute | solution.py:441
  4.3 3.6 %collective-permute-start.1 = (bf16[3,6,4,512]{3,2,1,0:T(4,128)(2,1)S(1)}, bf16[3,6,4,512]{3,2,1,0:T(4,128)(2,1)S(1)}, u32[]{:S(2)}, u32[]{:S(2)}) collective-permute-start(bf16[3,6,4,512]{3,2,1,0:T(4,128)(2,1)S(1)} %get-tuple-element.52), channel_id=1, source_target_pairs={{0,3},{1,0},{2,1},{3,2},{4,7},{5,4},{6,5},{7,6},{8,11},{9,8},{10,9... | collective-permute-start | bytes 221192 | tf_op jit(solution)/shard_map/ppermute | solution.py:441
  7.9 0.3 collective-permute-start.2
  8.2 0.5 %collective-permute-start.3 = (bf16[3,6,4,512]{3,2,1,0:T(4,128)(2,1)S(1)}, bf16[3,6,4,512]{3,2,1,0:T(4,128)(2,1)S(1)}, u32[]{:S(2)}, u32[]{:S(2)}) collective-permute-start(bf16[3,6,4,512]{3,2,1,0:T(4,128)(2,1)S(1)} %get-tuple-element.65), channel_id=1, source_target_pairs={{0,12},{1,13},{2,14},{3,15},{4,0},{5,1},{6,2},{7,3},{8,4},{9,5},{1... | collective-permute-start | bytes 221192 | tf_op jit(solution)/shard_map/ppermute | solution.py:441
  8.7 0.4 collective-permute-start.4
  9.2 2.0 %collective-permute-start.5 = (bf16[3,6,4,512]{3,2,1,0:T(4,128)(2,1)S(1)}, bf16[3,6,4,512]{3,2,1,0:T(4,128)(2,1)S(1)}, u32[]{:S(2)}, u32[]{:S(2)}) collective-permute-start(bf16[3,6,4,512]{3,2,1,0:T(4,128)(2,1)S(1)} %get-tuple-element.67), channel_id=1, source_target_pairs={{0,15},{1,12},{2,13},{3,14},{4,3},{5,0},{6,1},{7,2},{8,7},{9,4},{1... | collective-permute-start | bytes 221192 | tf_op jit(solution)/shard_map/ppermute | solution.py:441
  11.1 2.3 %table.1 = (bf16[2,144,1024]{2,1,0:T(8,128)(2,1)S(1)}, bf16[2,144,128]{2,1,0:T(8,128)(2,1)S(1)}, f32[1,512]{1,0:T(1,128)S(1)}, bf16[512,1536]{1,0:T(8,128)(2,1)S...) custom-call(f32[8,37]{1,0:T(8,128)} %refs_0_.1, ...), custom_call_target="tpu_custom_call" | custom-call | tf_op jit(solution)/shard_map/table/pallas_call | solution.py:238
  13.4 3.7 %forward.1 = (bf16[3,6,4,512]{3,2,1,0:T(4,128)(2,1)S(1)}, bf16[3,6,4,512]{3,2,1,0:T(4,128)(2,1)S(1)}, bf16[3,6,4,512]{3,2,1,0:T(4,128)(2,1)S(1)}, bf16[3,6,4,512...) custom-call(bf16[3,6,4,512]{3,2,1,0:T(4,128)(2,1)S(1)} %get-tuple-el, ...), custom_call_target="tpu_custom_call" | custom-call | tf_op jit(solution)/shard_map/forward/pallas_call | solution.py:515
  17.2 5.3 %backward.1 = (f32[288,512]{1,0:T(8,128)S(1)}, bf16[288,1536]{1,0:T(8,128)(2,1)S(1)}, bf16[288,16]{1,0:T(8,128)(2,1)S(1)}, f32[16,1536]{1,0:T(8,128)S(1)}, f32[16,1536]{1,0:T(8,128)S(1)}) custom-call(bf16[3,6,4,512]{3,2,1,0:T(4,128)(2,1)S(1)} %get-tuple-element.64.g0, bf16[3,6,4,512]{3,2,1,0:T(4,128)(2,1)S(1)} %collective-permute-done.3.g1, ...), custom_call_target="tpu_custom_call" | custom-call | tf_op jit(solution)/shard_map/backward/pallas_call | solution.py:532
  22.5 1.3 %collective-permute-done.9 = f32[16,1536]{1,0:T(8,128)S(1)} collective-permute-done((f32[16,1536]{1,0:T(8,128)S(1)}, f32[16,1536]{1,0:T(8,128)S(1)}, u32[]{:S(2)}, u32[]{:S(2)}) %collective-permute-start.9) | collective-permute-done | bytes 98336 | tf_op jit(solution)/shard_map/ppermute | solution.py:446
  23.9 4.1 %collective-permute-done.10 = bf16[16,1536]{1,0:T(8,128)(2,1)S(1)} collective-permute-done((bf16[16,1536]{1,0:T(8,128)(2,1)S(1)}, bf16[16,1536]{1,0:T(8,128)(2,1)S(1)}, u32[]{:S(2)}, u32[]{:S(2)}) %collective-permute-start.10) | collective-permute-done | bytes 49184 | tf_op jit(solution)/shard_map/ppermute | solution.py:446
  28.0 1.4 %collective-permute-start.11 = (bf16[16,1536]{1,0:T(8,128)(2,1)S(1)}, bf16[16,1536]{1,0:T(8,128)(2,1)S(1)}, u32[]{:S(2)}, u32[]{:S(2)}) collective-permute-start(bf16[16,1536]{1,0:T(8,128)(2,1)S(1)} %add_convert_fusion.1), channel_id=1, source_target_pairs={{0,2},{1,3},{2,0},{3,1},{4,6},{5,7},{6,4},{7,5},{8,10},{9,11},{10,... | collective-permute-start | bytes 147464 | tf_op jit(solution)/shard_map/ppermute | solution.py:446
  29.4 3.9 %collective-permute-done.11 = bf16[16,1536]{1,0:T(8,128)(2,1)S(1)} collective-permute-done((bf16[16,1536]{1,0:T(8,128)(2,1)S(1)}, bf16[16,1536]{1,0:T(8,128)(2,1)S(1)}, u32[]{:S(2)}, u32[]{:S(2)}) %collective-permute-start.11) | collective-permute-done | bytes 49184 | tf_op jit(solution)/shard_map/ppermute | solution.py:446
  33.3 0.4 collective-permute-start.12
  33.7 1.2 %norm_back.1 = (bf16[3,6,4,512]{3,2,1,0:T(4,128)(2,1)S(1)}, bf16[2,3,6,4,512]{4,3,2,1,0:T(4,128)(2,1)S(1)}, bf16[2,3,6,4,512]{4,3,2,1,0:T(4,128)(2,1)S(1)}, bf16[2,3,6,4,512]{4,3,2,1,0:T(4,128)(2,1)S(1)}) custom-call(f32[288,512]{1,0:T(8,128)S(1)} %get-tuple-element.74.refs_0_, bf16[288,1536]{1,0:T(8,128)(2,1)S(1)} %get-tuple-element.75.refs_1_, ...), custom_call_target="tpu_custom_call" | custom-call | tf_op jit(solution)/shard_map/norm_back/pallas_call | solution.py:548
  35.0 1.2 %collective-permute-start.7 = (bf16[2,3,6,4,512]{4,3,2,1,0:T(4,128)(2,1)S(1)}, bf16[2,3,6,4,512]{4,3,2,1,0:T(4,128)(2,1)S(1)}, u32[]{:S(2)}, u32[]{:S(2)}) collective-permute-start(bf16[2,3,6,4,512]{4,3,2,1,0:T(4,128)(2,1)S(1)} %get-tuple-element.84), channel_id=1, source_target_pairs={{0,1},{1,2},{2,3},{3,0},{4,5},{5,6},{6,7},{7,4},{8,9},{9,10},{10,1... | collective-permute-start | bytes 442376 | tf_op jit(solution)/shard_map/ppermute | solution.py:441
  36.1 1.7 %collective-permute-start.8 = (bf16[2,3,6,4,512]{4,3,2,1,0:T(4,128)(2,1)S(1)}, bf16[2,3,6,4,512]{4,3,2,1,0:T(4,128)(2,1)S(1)}, u32[]{:S(2)}, u32[]{:S(2)}) collective-permute-start(bf16[2,3,6,4,512]{4,3,2,1,0:T(4,128)(2,1)S(1)} %get-tuple-element.85), channel_id=1, source_target_pairs={{0,5},{1,6},{2,7},{3,4},{4,9},{5,10},{6,11},{7,8},{8,13},{9,14},{1... | collective-permute-start | bytes 442376 | tf_op jit(solution)/shard_map/ppermute | solution.py:441
  37.8 0.2 collective-permute-start.13
  38.0 1.5 %collective-permute-done.6.refs_2_ = bf16[2,3,6,4,512]{4,3,2,1,0:T(4,128)(2,1)S(1)} collective-permute-done((bf16[2,3,6,4,512]{4,3,2,1,0:T(4,128)(2,1)S(1)}, bf16[2,3,6,4,512]{4,3,2,1,0:T(4,128)(2,1)S(1)}, u32[]{:S(2)}, u32[]{:S(2)}) %collective-permute-start.6) | collective-permute-done | bytes 147488 | tf_op jit(solution)/shard_map/ppermute | solution.py:441
  39.5 3.3 %collective-permute-done.7.refs_3_ = bf16[2,3,6,4,512]{4,3,2,1,0:T(4,128)(2,1)S(1)} collective-permute-done((bf16[2,3,6,4,512]{4,3,2,1,0:T(4,128)(2,1)S(1)}, bf16[2,3,6,4,512]{4,3,2,1,0:T(4,128)(2,1)S(1)}, u32[]{:S(2)}, u32[]{:S(2)}) %collective-permute-start.7) | collective-permute-done | bytes 147488 | tf_op jit(solution)/shard_map/ppermute | solution.py:441
  42.8 4.0 %collective-permute-done.8.refs_4_ = bf16[2,3,6,4,512]{4,3,2,1,0:T(4,128)(2,1)S(1)} collective-permute-done((bf16[2,3,6,4,512]{4,3,2,1,0:T(4,128)(2,1)S(1)}, bf16[2,3,6,4,512]{4,3,2,1,0:T(4,128)(2,1)S(1)}, u32[]{:S(2)}, u32[]{:S(2)}) %collective-permute-start.8) | collective-permute-done | bytes 147488 | tf_op jit(solution)/shard_map/ppermute | solution.py:441
  46.8 0.9 %unpack.1 = (bf16[6,12,4,512]{3,2,1,0:T(4,128)(2,1)}, bf16[6,12,4,512]{3,2,1,0:T(4,128)(2,1)}) custom-call(bf16[3,6,4,512]{3,2,1,0:T(4,128)(2,1)S(1)} %get-tuple-element.63.refs_0_, bf16[3,6,4,512]{3,2,1,0:T(4,128)(2,1)S(1)} %get-tuple-element.82.refs_1_, bf16[2,3,6,4,512]{4,3,2,1,0:T(4,128)(2,1)S(1)} %collective-permute-done.6.refs_2_, ...), custom_call_target="tpu_custom_call" | custom-call | tf_op jit(solution)/shard_map/unpack/pallas_call | solution.py:120
  47.7 0.7 %finish.1 = (f32[16,512]{1,0:T(8,128)}, f32[16,1536]{1,0:T(8,128)}, f32[16,512]{1,0:T(8,128)}, f32[16,512]{1,0:T(8,128)}) custom-call(f32[16,1536]{1,0:T(8,128)S(1)} %convert_add_fusion.mine_ref, f32[16,1536]{1,0:T(8,128)S(1)} %collective-permute-done.13.other_ref), custom_call_target="tpu_custom_call" | custom-call | tf_op jit(solution)/shard_map/finish/pallas_call | solution.py:559
  (15 shorter events, 0.2 us)
Async XLA Ops:
  1.8 7.3 %collective-permute-start = (bf16[3,6,4,512]{3,2,1,0:T(4,128)(2,1)S(1)}, bf16[3,6,4,512]{3,2,1,0:T(4,128)(2,1)S(1)}, u32[]{:S(2)}, u32[]{:S(2)}) collective-permute-start(bf16[3,6,4,512]{3,2,1,0:T(4,128)(2,1)S(1)} %get-tuple-element.51), channel_id=1, source_target_pairs={{0,12},{1,13},{2,14},{3,15},{4,0},{5,1},{6,2},{7,3},{8,4},{9,5},{1... | collective-permute-start | bytes 221192 | tf_op jit(solution)/shard_map/ppermute | solution.py:441
  4.3 9.1 %collective-permute-start.1 = (bf16[3,6,4,512]{3,2,1,0:T(4,128)(2,1)S(1)}, bf16[3,6,4,512]{3,2,1,0:T(4,128)(2,1)S(1)}, u32[]{:S(2)}, u32[]{:S(2)}) collective-permute-start(bf16[3,6,4,512]{3,2,1,0:T(4,128)(2,1)S(1)} %get-tuple-element.52), channel_id=1, source_target_pairs={{0,3},{1,0},{2,1},{3,2},{4,7},{5,4},{6,5},{7,6},{8,11},{9,8},{10,9... | collective-permute-start | bytes 221192 | tf_op jit(solution)/shard_map/ppermute | solution.py:441
  7.9 5.5 %collective-permute-start.2 = (bf16[3,6,4,512]{3,2,1,0:T(4,128)(2,1)S(1)}, bf16[3,6,4,512]{3,2,1,0:T(4,128)(2,1)S(1)}, u32[]{:S(2)}, u32[]{:S(2)}) collective-permute-start(bf16[3,6,4,512]{3,2,1,0:T(4,128)(2,1)S(1)} %get-tuple-element.53), channel_id=1, source_target_pairs={{0,15},{1,12},{2,13},{3,14},{4,3},{5,0},{6,1},{7,2},{8,7},{9,4},{1... | collective-permute-start | bytes 221192 | tf_op jit(solution)/shard_map/ppermute | solution.py:441
  8.2 9.0 %collective-permute-start.3 = (bf16[3,6,4,512]{3,2,1,0:T(4,128)(2,1)S(1)}, bf16[3,6,4,512]{3,2,1,0:T(4,128)(2,1)S(1)}, u32[]{:S(2)}, u32[]{:S(2)}) collective-permute-start(bf16[3,6,4,512]{3,2,1,0:T(4,128)(2,1)S(1)} %get-tuple-element.65), channel_id=1, source_target_pairs={{0,12},{1,13},{2,14},{3,15},{4,0},{5,1},{6,2},{7,3},{8,4},{9,5},{1... | collective-permute-start | bytes 221192 | tf_op jit(solution)/shard_map/ppermute | solution.py:441
  8.7 8.5 %collective-permute-start.4 = (bf16[3,6,4,512]{3,2,1,0:T(4,128)(2,1)S(1)}, bf16[3,6,4,512]{3,2,1,0:T(4,128)(2,1)S(1)}, u32[]{:S(2)}, u32[]{:S(2)}) collective-permute-start(bf16[3,6,4,512]{3,2,1,0:T(4,128)(2,1)S(1)} %get-tuple-element.66), channel_id=1, source_target_pairs={{0,3},{1,0},{2,1},{3,2},{4,7},{5,4},{6,5},{7,6},{8,11},{9,8},{10,9... | collective-permute-start | bytes 221192 | tf_op jit(solution)/shard_map/ppermute | solution.py:441
  9.2 8.0 %collective-permute-start.5 = (bf16[3,6,4,512]{3,2,1,0:T(4,128)(2,1)S(1)}, bf16[3,6,4,512]{3,2,1,0:T(4,128)(2,1)S(1)}, u32[]{:S(2)}, u32[]{:S(2)}) collective-permute-start(bf16[3,6,4,512]{3,2,1,0:T(4,128)(2,1)S(1)} %get-tuple-element.67), channel_id=1, source_target_pairs={{0,15},{1,12},{2,13},{3,14},{4,3},{5,0},{6,1},{7,2},{8,7},{9,4},{1... | collective-permute-start | bytes 221192 | tf_op jit(solution)/shard_map/ppermute | solution.py:441
  22.5 1.3 %collective-permute-start.9 = (f32[16,1536]{1,0:T(8,128)S(1)}, f32[16,1536]{1,0:T(8,128)S(1)}, u32[]{:S(2)}, u32[]{:S(2)}) collective-permute-start(f32[16,1536]{1,0:T(8,128)S(1)} %get-tuple-element.89), channel_id=1, source_target_pairs={{0,4},{4,0},{8,12},{12,8},{1,5},{5,1},{9,13},{13,9},{2,6},{6,2},{1... | collective-permute-start | bytes 294920 | tf_op jit(solution)/shard_map/ppermute | solution.py:446
  23.8 4.2 %collective-permute-start.10 = (bf16[16,1536]{1,0:T(8,128)(2,1)S(1)}, bf16[16,1536]{1,0:T(8,128)(2,1)S(1)}, u32[]{:S(2)}, u32[]{:S(2)}) collective-permute-start(bf16[16,1536]{1,0:T(8,128)(2,1)S(1)} %add_convert_fusion.2), channel_id=1, source_target_pairs={{0,1},{1,0},{2,3},{3,2},{4,5},{5,4},{6,7},{7,6},{8,9},{9,8},{10,11... | collective-permute-start | bytes 147464 | tf_op jit(solution)/shard_map/ppermute | solution.py:446
  28.0 5.3 %collective-permute-start.11 = (bf16[16,1536]{1,0:T(8,128)(2,1)S(1)}, bf16[16,1536]{1,0:T(8,128)(2,1)S(1)}, u32[]{:S(2)}, u32[]{:S(2)}) collective-permute-start(bf16[16,1536]{1,0:T(8,128)(2,1)S(1)} %add_convert_fusion.1), channel_id=1, source_target_pairs={{0,2},{1,3},{2,0},{3,1},{4,6},{5,7},{6,4},{7,5},{8,10},{9,11},{10,... | collective-permute-start | bytes 147464 | tf_op jit(solution)/shard_map/ppermute | solution.py:446
  33.3 4.5 %collective-permute-start.12 = (bf16[16,1536]{1,0:T(8,128)(2,1)S(1)}, bf16[16,1536]{1,0:T(8,128)(2,1)S(1)}, u32[]{:S(2)}, u32[]{:S(2)}) collective-permute-start(bf16[16,1536]{1,0:T(8,128)(2,1)S(1)} %add_convert_fusion), channel_id=1, source_target_pairs={{0,8},{4,12},{8,0},{12,4},{1,9},{5,13},{9,1},{13,5},{2,10},{6,14},... | collective-permute-start | bytes 147464 | tf_op jit(solution)/shard_map/ppermute | solution.py:446
  34.9 4.6 %collective-permute-start.6 = (bf16[2,3,6,4,512]{4,3,2,1,0:T(4,128)(2,1)S(1)}, bf16[2,3,6,4,512]{4,3,2,1,0:T(4,128)(2,1)S(1)}, u32[]{:S(2)}, u32[]{:S(2)}) collective-permute-start(bf16[2,3,6,4,512]{4,3,2,1,0:T(4,128)(2,1)S(1)} %get-tuple-element.83), channel_id=1, source_target_pairs={{0,4},{1,5},{2,6},{3,7},{4,8},{5,9},{6,10},{7,11},{8,12},{9,13},{1... | collective-permute-start | bytes 442376 | tf_op jit(solution)/shard_map/ppermute | solution.py:441
  35.0 7.8 %collective-permute-start.7 = (bf16[2,3,6,4,512]{4,3,2,1,0:T(4,128)(2,1)S(1)}, bf16[2,3,6,4,512]{4,3,2,1,0:T(4,128)(2,1)S(1)}, u32[]{:S(2)}, u32[]{:S(2)}) collective-permute-start(bf16[2,3,6,4,512]{4,3,2,1,0:T(4,128)(2,1)S(1)} %get-tuple-element.84), channel_id=1, source_target_pairs={{0,1},{1,2},{2,3},{3,0},{4,5},{5,6},{6,7},{7,4},{8,9},{9,10},{10,1... | collective-permute-start | bytes 442376 | tf_op jit(solution)/shard_map/ppermute | solution.py:441
  36.1 10.7 %collective-permute-start.8 = (bf16[2,3,6,4,512]{4,3,2,1,0:T(4,128)(2,1)S(1)}, bf16[2,3,6,4,512]{4,3,2,1,0:T(4,128)(2,1)S(1)}, u32[]{:S(2)}, u32[]{:S(2)}) collective-permute-start(bf16[2,3,6,4,512]{4,3,2,1,0:T(4,128)(2,1)S(1)} %get-tuple-element.85), channel_id=1, source_target_pairs={{0,5},{1,6},{2,7},{3,4},{4,9},{5,10},{6,11},{7,8},{8,13},{9,14},{1... | collective-permute-start | bytes 442376 | tf_op jit(solution)/shard_map/ppermute | solution.py:441
  37.8 9.9 %collective-permute-start.13 = (f32[16,1536]{1,0:T(8,128)S(1)}, f32[16,1536]{1,0:T(8,128)S(1)}, u32[]{:S(2)}, u32[]{:S(2)}) collective-permute-start(f32[16,1536]{1,0:T(8,128)S(1)} %convert_add_fusion.mine_ref), channel_id=1, source_target_pairs={{0,4},{4,0},{8,12},{12,8},{1,5},{5,1},{9,13},{13,9},{2,6},{6,2},{1... | collective-permute-start | bytes 294920 | tf_op jit(solution)/shard_map/ppermute | solution.py:446

commit v4 on v3

--- a/solution.py
+++ b/solution.py
@@ -286,7 +286,7 @@
 def forward_kernel(
     x0, x1, x2, x3, key_cols, query_cols, gain, w_qkv, qkv_down, qkv_up, w_proj, proj_down, proj_up,
     o0, o1, o2, o3, unit_ref, inv_ref, normed_ref, low_ref, qkv_ref, probs_ref, attn_ref, low_proj_ref,
-    scratch, rows_ref,
+    scratch, rows_ref, scores_ref, rounded_ref,
 ):
     gather_rows((x0, x1, x2, x3), scratch, rows_ref)
     total, width = rows_ref.shape
@@ -309,30 +309,41 @@
     scale = 1.0 / math.sqrt(head)
     assert math.frexp(scale)[0] == 0.5
     lane = lax.broadcasted_iota(jnp.int32, (WINDOW, pair), 1)
-    for w in range(windows):
+    pairs = [(w, p) for w in range(windows) for p in range(HEADS // 2)]
+
+    def start(w, p):
         at = slice(w * WINDOW, (w + 1) * WINDOW)
-        more = query_cols[w]
-        for p in range(HEADS // 2):
-            query = qkv_ref[at, p * pair : (p + 1) * pair] * jnp.asarray(scale, bf16)
-            keys = qkv_ref[at, width + p * pair : width + (p + 1) * pair]
-            values = qkv_ref[at, 2 * width + p * pair : 2 * width + (p + 1) * pair]
-            mixed = []
-            for h in range(2):
-                mine = (lane < head) if h == 0 else (lane >= head)
-                number = 2 * p + h
-                wide_query = jnp.concatenate([jnp.where(mine, query, 0), more], 1)
-                wide_keys = jnp.concatenate(
-                    [keys, key_cols[w, :, number * LANES : (number + 1) * LANES]], 1
-                )
-                scores = nt(wide_keys, wide_query)
-                top = jnp.max(scores, axis=0, keepdims=True)
-                terms = jnp.exp(scores - top)
-                probs = terms * (1.0 / jnp.sum(terms, axis=0, keepdims=True))
-                probs_ref[w * HEADS + number] = probs
-                mixed.append(tn(probs.astype(bf16), values))
-            attn_ref[at, p * pair : (p + 1) * pair] = jnp.where(
-                lane < head, mixed[0], mixed[1]
-            ).astype(bf16)
+        query = qkv_ref[at, p * pair : (p + 1) * pair] * jnp.asarray(scale, bf16)
+        keys = qkv_ref[at, width + p * pair : width + (p + 1) * pair]
+        for h in range(2):
+            mine = (lane < head) if h == 0 else (lane >= head)
+            number = 2 * p + h
+            wide_query = jnp.concatenate([jnp.where(mine, query, 0), query_cols[w]], 1)
+            wide_keys = jnp.concatenate(
+                [keys, key_cols[w, :, number * LANES : (number + 1) * LANES]], 1
+            )
+            scores_ref[w * HEADS + number] = nt(wide_keys, wide_query)
+
+    def middle(w, p):
+        for h in range(2):
+            index = w * HEADS + 2 * p + h
+            scores = scores_ref[index]
+            terms = jnp.exp(scores - jnp.max(scores, axis=0, keepdims=True))
+            probs = terms * (1.0 / jnp.sum(terms, axis=0, keepdims=True))
+            probs_ref[index] = probs
+            rounded_ref[index] = probs.astype(bf16)
+
+    def end(w, p):
+        at = slice(w * WINDOW, (w + 1) * WINDOW)
+        values = qkv_ref[at, 2 * width + p * pair : 2 * width + (p + 1) * pair]
+        mixed = [tn(rounded_ref[w * HEADS + 2 * p + h], values) for h in range(2)]
+        attn_ref[at, p * pair : (p + 1) * pair] = jnp.where(
+            lane < head, mixed[0], mixed[1]
+        ).astype(bf16)
+
+    for stage in (start, middle, end):
+        for w, p in pairs:
+            stage(w, p)
     attn = attn_ref[...]
     low_proj = nt(attn, proj_down[...]).astype(bf16)
     low_proj_ref[...] = low_proj
@@ -343,7 +354,7 @@
 def backward_kernel(
     g0, g1, g2, g3, normed_ref, low_ref, qkv_ref, probs_ref, attn_ref, low_proj_ref,
     qkv_up, w_proj, proj_down, proj_up,
-    grad_ref, d_qkv_ref, d_low_ref, keep_ref, send_ref, scratch,
+    grad_ref, d_qkv_ref, d_low_ref, keep_ref, send_ref, scratch, probs_grad, scores_grad,
 ):
     gather_rows((g0, g1, g2, g3), scratch, grad_ref)
     width = grad_ref.shape[1]
@@ -355,26 +366,48 @@
     d_low_proj = nt(grad, proj_up[...]).astype(bf16)
     d_attn = (nt(grad, w_proj[...]) + nn(d_low_proj, proj_down[...])).astype(bf16)
     lane = lax.broadcasted_iota(jnp.int32, (WINDOW, pair), 1)
-    for w in range(windows):
+    pairs = [(w, p) for w in range(windows) for p in range(HEADS // 2)]
+
+    def start(w, p):
         at = slice(w * WINDOW, (w + 1) * WINDOW)
-        for p in range(HEADS // 2):
-            cols = [slice(s * width + p * pair, s * width + (p + 1) * pair) for s in range(3)]
-            query = qkv_ref[at, cols[0]]
-            keys = qkv_ref[at, cols[1]]
-            values = qkv_ref[at, cols[2]]
-            d_out = d_attn[at, p * pair : (p + 1) * pair]
-            d_q, d_k, d_v = [], [], []
-            for h in range(2):
-                mine = (lane < head) if h == 0 else (lane >= head)
-                probs = probs_ref[w * HEADS + 2 * p + h]
-                d_probs = nt(values, jnp.where(mine, d_out, 0))
-                inner = jnp.sum(d_probs * probs, axis=0, keepdims=True)
-                d_scores = (probs * (d_probs - inner) * scale).astype(bf16)
-                d_v.append(nn(probs.astype(bf16), d_out))
-                d_k.append(nn(d_scores, query))
-                d_q.append(tn(d_scores, keys))
-            for s, parts in enumerate((d_q, d_k, d_v)):
-                d_qkv_ref[at, cols[s]] = jnp.where(lane < head, parts[0], parts[1]).astype(bf16)
+        values = qkv_ref[at, 2 * width + p * pair : 2 * width + (p + 1) * pair]
+        scaled = d_attn[at, p * pair : (p + 1) * pair] * jnp.asarray(scale, bf16)
+        for h in range(2):
+            mine = (lane < head) if h == 0 else (lane >= head)
+            probs_grad[w * HEADS + 2 * p + h] = nt(values, jnp.where(mine, scaled, 0))
+
+    def middle(w, p):
+        for h in range(2):
+            index = w * HEADS + 2 * p + h
+            probs = probs_ref[index]
+            d_probs = probs_grad[index]
+            inner = jnp.sum(d_probs * probs, axis=0, keepdims=True)
+            scores_grad[index] = (probs * (d_probs - inner)).astype(bf16)
+
+    def end(w, p):
+        at = slice(w * WINDOW, (w + 1) * WINDOW)
+        cols = [slice(s * width + p * pair, s * width + (p + 1) * pair) for s in range(3)]
+        query = qkv_ref[at, cols[0]]
+        keys_t = qkv_ref[at, cols[1]].T
+        d_out = d_attn[at, p * pair : (p + 1) * pair]
+        d_q, d_k, d_v = [], [], []
+        for h in range(2):
+            index = w * HEADS + 2 * p + h
+            d_scores = scores_grad[index]
+            d_v.append(nn(probs_ref[index].astype(bf16), d_out))
+            d_k.append(nn(d_scores, query))
+            d_q.append(nn(keys_t[h * head : (h + 1) * head], d_scores).astype(bf16))
+        d_qkv_ref[at, cols[0]] = jnp.concatenate(d_q, 0).T
+        for s, parts in ((1, d_k), (2, d_v)):
+            d_qkv_ref[at, cols[s]] = jnp.where(lane < head, parts[0], parts[1]).astype(bf16)
+
+    for i in range(len(pairs) + 2):
+        if i < len(pairs):
+            start(*pairs[i])
+        if 1 <= i <= len(pairs):
+            middle(*pairs[i - 1])
+        if i >= 2:
+            end(*pairs[i - 2])
     d_qkv = d_qkv_ref[...]
     d_low = nt(d_qkv, qkv_up[...]).astype(bf16)
     d_low_ref[...] = d_low
@@ -525,7 +558,12 @@
                 struct((total, width), bf16),
                 struct((total, rank), bf16),
             ],
-            [columns, pltpu.VMEM((total, width), f32)],
+            [
+                columns,
+                pltpu.VMEM((total, width), f32),
+                pltpu.VMEM((windows * HEADS, WINDOW, WINDOW), f32),
+                pltpu.VMEM((windows * HEADS, WINDOW, WINDOW), bf16),
+            ],
             name="forward",
         )(*x_quads, key_cols, query_cols, *weights)
         out = exchange({0: o0, **{q: (o1, o2, o3)[q - 1] for q in APART}}, sizes, 1)
@@ -538,7 +576,11 @@
                 struct((rank, 3 * width), f32),
                 struct((rank, 3 * width), f32),
             ],
-            [columns],
+            [
+                columns,
+                pltpu.VMEM((windows * HEADS, WINDOW, WINDOW), f32),
+                pltpu.VMEM((windows * HEADS, WINDOW, WINDOW), bf16),
+            ],
             name="backward",
         )(*g_quads, normed, low, qkv, probs, attn, low_proj, qkv_up, w_proj, proj_down, proj_up)
         sums = sum_over(keep, send, sizes)

time: 48.6 us -> 46.1 us (0.949)
  Pallas kernels: 15.3 us -> 12.8 us
    pallas_call x1, Pallas kernels: 5.3 us -> 3.44 us  [layer(): call(backward_kernel, [struct((total, width), f32), struct((total, 3 * wi...]
    pallas_call x1, Pallas kernels: 3.75 us -> 3.15 us  [layer(): call(forward_kernel, [quarter] * 4 + [struct((total, width), f32), struct...]
  transfers between devices with their start and end apart: 14 -> 14, of which waited for: 6 -> 6; matrix products, arithmetic and copies ran while one was open for 0% -> 0% of each run, Pallas kernels for 17% -> 16%
where the time goes in v4:
time: 46.1 us; the launch traced here: 46 us
  waiting for transfers between devices  18 us (39%)
  starting transfers between devices  14.3 us (31%)
  Pallas kernels  12.8 us (28%)
  between operations  0.75 us (2%)
    ppermute x9, starting transfers between devices, exchange(): moved[quad] = lax.ppermute(moved[quad], ('lon', 'lat'), pairs)  12.2 us
    ppermute x5, waiting for transfers between devices, swap(): return lax.ppermute(value, axis, [(i, i ^ bit) for i in range(length)])  9.25 us
    ppermute x9, waiting for transfers between devices, exchange(): moved[quad] = lax.ppermute(moved[quad], ('lon', 'lat'), pairs)  8.76 us
    pallas_call x1, Pallas kernels, layer(): call(backward_kernel, [struct((total, width), f32), struct((total, 3 * wi...  3.44 us
    pallas_call x1, Pallas kernels, layer(): call(forward_kernel, [quarter] * 4 + [struct((total, width), f32), struct...  3.15 us
    pallas_call x1, Pallas kernels, score_columns(): call(functools.partial(table_kernel, count=len(weights)), [struct((window...  2.25 us
    ppermute x5, starting transfers between devices, swap(): return lax.ppermute(value, axis, [(i, i ^ bit) for i in range(length)])  2.14 us
    pallas_call x1, Pallas kernels, pack(): call(pack_kernel, [struct((HALF_LAT, HALF_LON, levels, width), bf16)] * 8...  1.21 us
  transfers between devices with their start and end apart: 14, of which 6 were waited for; matrix products, arithmetic and copies ran while one was open for 0% of the time, Pallas kernels for 16%

profile of v4, /device:TPU:0, one launch (start us, length us, event | category | flops | bytes accessed | tf_op | source)
XLA Modules:
  0.0 46.0 jit_solution(15688720571265554681)
XLA Ops:
  0.6 1.2 %pack.1 = (bf16[3,6,4,512]{3,2,1,0:T(4,128)(2,1)S(1)}, bf16[3,6,4,512]{3,2,1,0:T(4,128)(2,1)S(1)}, bf16[3,6,4,512]{3,2,1,0:T(4,128)(2,1)S(1)}, bf16[3,6,4,512]{3...) custom-call(bf16[6,12,4,512]{3,2,1,0:T(4,128)(2,1)} %bitcast.6, ...), custom_call_target="tpu_custom_call" | custom-call | tf_op jit(solution)/shard_map/pack/pallas_call | solution.py:86
  1.8 2.5 %collective-permute-start = (bf16[3,6,4,512]{3,2,1,0:T(4,128)(2,1)S(1)}, bf16[3,6,4,512]{3,2,1,0:T(4,128)(2,1)S(1)}, u32[]{:S(2)}, u32[]{:S(2)}) collective-permute-start(bf16[3,6,4,512]{3,2,1,0:T(4,128)(2,1)S(1)} %get-tuple-element.51), channel_id=1, source_target_pairs={{0,12},{1,13},{2,14},{3,15},{4,0},{5,1},{6,2},{7,3},{8,4},{9,5},{1... | collective-permute-start | bytes 221192 | tf_op jit(solution)/shard_map/ppermute | solution.py:474
  4.3 3.6 %collective-permute-start.1 = (bf16[3,6,4,512]{3,2,1,0:T(4,128)(2,1)S(1)}, bf16[3,6,4,512]{3,2,1,0:T(4,128)(2,1)S(1)}, u32[]{:S(2)}, u32[]{:S(2)}) collective-permute-start(bf16[3,6,4,512]{3,2,1,0:T(4,128)(2,1)S(1)} %get-tuple-element.52), channel_id=1, source_target_pairs={{0,3},{1,0},{2,1},{3,2},{4,7},{5,4},{6,5},{7,6},{8,11},{9,8},{10,9... | collective-permute-start | bytes 221192 | tf_op jit(solution)/shard_map/ppermute | solution.py:474
  7.9 0.3 collective-permute-start.2
  8.2 0.5 %collective-permute-start.3 = (bf16[3,6,4,512]{3,2,1,0:T(4,128)(2,1)S(1)}, bf16[3,6,4,512]{3,2,1,0:T(4,128)(2,1)S(1)}, u32[]{:S(2)}, u32[]{:S(2)}) collective-permute-start(bf16[3,6,4,512]{3,2,1,0:T(4,128)(2,1)S(1)} %get-tuple-element.65), channel_id=1, source_target_pairs={{0,12},{1,13},{2,14},{3,15},{4,0},{5,1},{6,2},{7,3},{8,4},{9,5},{1... | collective-permute-start | bytes 221192 | tf_op jit(solution)/shard_map/ppermute | solution.py:474
  8.7 0.4 collective-permute-start.4
  9.2 2.0 %collective-permute-start.5 = (bf16[3,6,4,512]{3,2,1,0:T(4,128)(2,1)S(1)}, bf16[3,6,4,512]{3,2,1,0:T(4,128)(2,1)S(1)}, u32[]{:S(2)}, u32[]{:S(2)}) collective-permute-start(bf16[3,6,4,512]{3,2,1,0:T(4,128)(2,1)S(1)} %get-tuple-element.67), channel_id=1, source_target_pairs={{0,15},{1,12},{2,13},{3,14},{4,3},{5,0},{6,1},{7,2},{8,7},{9,4},{1... | collective-permute-start | bytes 221192 | tf_op jit(solution)/shard_map/ppermute | solution.py:474
  11.1 2.3 %table.1 = (bf16[2,144,1024]{2,1,0:T(8,128)(2,1)S(1)}, bf16[2,144,128]{2,1,0:T(8,128)(2,1)S(1)}, f32[1,512]{1,0:T(1,128)S(1)}, bf16[512,1536]{1,0:T(8,128)(2,1)S...) custom-call(f32[8,37]{1,0:T(8,128)} %refs_0_.1, ...), custom_call_target="tpu_custom_call" | custom-call | tf_op jit(solution)/shard_map/table/pallas_call | solution.py:238
  13.4 3.1 %forward.1 = (bf16[3,6,4,512]{3,2,1,0:T(4,128)(2,1)S(1)}, bf16[3,6,4,512]{3,2,1,0:T(4,128)(2,1)S(1)}, bf16[3,6,4,512]{3,2,1,0:T(4,128)(2,1)S(1)}, bf16[3,6,4,512...) custom-call(bf16[3,6,4,512]{3,2,1,0:T(4,128)(2,1)S(1)} %get-tuple-el, ...), custom_call_target="tpu_custom_call" | custom-call | tf_op jit(solution)/shard_map/forward/pallas_call | solution.py:548
  16.6 3.4 %backward.1 = (f32[288,512]{1,0:T(8,128)S(1)}, bf16[288,1536]{1,0:T(8,128)(2,1)S(1)}, bf16[288,16]{1,0:T(8,128)(2,1)S(1)}, f32[16,1536]{1,0:T(8,128)S(1)}, f32[16,1536]{1,0:T(8,128)S(1)}) custom-call(bf16[3,6,4,512]{3,2,1,0:T(4,128)(2,1)S(1)} %get-tuple-element.64.g0, bf16[3,6,4,512]{3,2,1,0:T(4,128)(2,1)S(1)} %collective-permute-done.3.g1, ...), custom_call_target="tpu_custom_call" | custom-call | tf_op jit(solution)/shard_map/backward/pallas_call | solution.py:570
  20.0 1.3 %collective-permute-done.9 = f32[16,1536]{1,0:T(8,128)S(1)} collective-permute-done((f32[16,1536]{1,0:T(8,128)S(1)}, f32[16,1536]{1,0:T(8,128)S(1)}, u32[]{:S(2)}, u32[]{:S(2)}) %collective-permute-start.9) | collective-permute-done | bytes 98336 | tf_op jit(solution)/shard_map/ppermute | solution.py:479
  21.4 4.1 %collective-permute-done.10 = bf16[16,1536]{1,0:T(8,128)(2,1)S(1)} collective-permute-done((bf16[16,1536]{1,0:T(8,128)(2,1)S(1)}, bf16[16,1536]{1,0:T(8,128)(2,1)S(1)}, u32[]{:S(2)}, u32[]{:S(2)}) %collective-permute-start.10) | collective-permute-done | bytes 49184 | tf_op jit(solution)/shard_map/ppermute | solution.py:479
  25.5 1.4 %collective-permute-start.11 = (bf16[16,1536]{1,0:T(8,128)(2,1)S(1)}, bf16[16,1536]{1,0:T(8,128)(2,1)S(1)}, u32[]{:S(2)}, u32[]{:S(2)}) collective-permute-start(bf16[16,1536]{1,0:T(8,128)(2,1)S(1)} %add_convert_fusion.1), channel_id=1, source_target_pairs={{0,2},{1,3},{2,0},{3,1},{4,6},{5,7},{6,4},{7,5},{8,10},{9,11},{10,... | collective-permute-start | bytes 147464 | tf_op jit(solution)/shard_map/ppermute | solution.py:479
  27.0 3.9 %collective-permute-done.11 = bf16[16,1536]{1,0:T(8,128)(2,1)S(1)} collective-permute-done((bf16[16,1536]{1,0:T(8,128)(2,1)S(1)}, bf16[16,1536]{1,0:T(8,128)(2,1)S(1)}, u32[]{:S(2)}, u32[]{:S(2)}) %collective-permute-start.11) | collective-permute-done | bytes 49184 | tf_op jit(solution)/shard_map/ppermute | solution.py:479
  30.8 0.4 collective-permute-start.12
  31.2 1.2 %norm_back.1 = (bf16[3,6,4,512]{3,2,1,0:T(4,128)(2,1)S(1)}, bf16[2,3,6,4,512]{4,3,2,1,0:T(4,128)(2,1)S(1)}, bf16[2,3,6,4,512]{4,3,2,1,0:T(4,128)(2,1)S(1)}, bf16[2,3,6,4,512]{4,3,2,1,0:T(4,128)(2,1)S(1)}) custom-call(f32[288,512]{1,0:T(8,128)S(1)} %get-tuple-element.74.refs_0_, bf16[288,1536]{1,0:T(8,128)(2,1)S(1)} %get-tuple-element.75.refs_1_, ...), custom_call_target="tpu_custom_call" | custom-call | tf_op jit(solution)/shard_map/norm_back/pallas_call | solution.py:590
  32.5 1.1 %collective-permute-start.7 = (bf16[2,3,6,4,512]{4,3,2,1,0:T(4,128)(2,1)S(1)}, bf16[2,3,6,4,512]{4,3,2,1,0:T(4,128)(2,1)S(1)}, u32[]{:S(2)}, u32[]{:S(2)}) collective-permute-start(bf16[2,3,6,4,512]{4,3,2,1,0:T(4,128)(2,1)S(1)} %get-tuple-element.84), channel_id=1, source_target_pairs={{0,1},{1,2},{2,3},{3,0},{4,5},{5,6},{6,7},{7,4},{8,9},{9,10},{10,1... | collective-permute-start | bytes 442376 | tf_op jit(solution)/shard_map/ppermute | solution.py:474
  33.7 1.7 %collective-permute-start.8 = (bf16[2,3,6,4,512]{4,3,2,1,0:T(4,128)(2,1)S(1)}, bf16[2,3,6,4,512]{4,3,2,1,0:T(4,128)(2,1)S(1)}, u32[]{:S(2)}, u32[]{:S(2)}) collective-permute-start(bf16[2,3,6,4,512]{4,3,2,1,0:T(4,128)(2,1)S(1)} %get-tuple-element.85), channel_id=1, source_target_pairs={{0,5},{1,6},{2,7},{3,4},{4,9},{5,10},{6,11},{7,8},{8,13},{9,14},{1... | collective-permute-start | bytes 442376 | tf_op jit(solution)/shard_map/ppermute | solution.py:474
  35.4 0.2 collective-permute-start.13
  35.6 1.5 %collective-permute-done.6.refs_2_ = bf16[2,3,6,4,512]{4,3,2,1,0:T(4,128)(2,1)S(1)} collective-permute-done((bf16[2,3,6,4,512]{4,3,2,1,0:T(4,128)(2,1)S(1)}, bf16[2,3,6,4,512]{4,3,2,1,0:T(4,128)(2,1)S(1)}, u32[]{:S(2)}, u32[]{:S(2)}) %collective-permute-start.6) | collective-permute-done | bytes 147488 | tf_op jit(solution)/shard_map/ppermute | solution.py:474
  37.1 3.2 %collective-permute-done.7.refs_3_ = bf16[2,3,6,4,512]{4,3,2,1,0:T(4,128)(2,1)S(1)} collective-permute-done((bf16[2,3,6,4,512]{4,3,2,1,0:T(4,128)(2,1)S(1)}, bf16[2,3,6,4,512]{4,3,2,1,0:T(4,128)(2,1)S(1)}, u32[]{:S(2)}, u32[]{:S(2)}) %collective-permute-start.7) | collective-permute-done | bytes 147488 | tf_op jit(solution)/shard_map/ppermute | solution.py:474
  40.3 4.0 %collective-permute-done.8.refs_4_ = bf16[2,3,6,4,512]{4,3,2,1,0:T(4,128)(2,1)S(1)} collective-permute-done((bf16[2,3,6,4,512]{4,3,2,1,0:T(4,128)(2,1)S(1)}, bf16[2,3,6,4,512]{4,3,2,1,0:T(4,128)(2,1)S(1)}, u32[]{:S(2)}, u32[]{:S(2)}) %collective-permute-start.8) | collective-permute-done | bytes 147488 | tf_op jit(solution)/shard_map/ppermute | solution.py:474
  44.4 0.9 %unpack.1 = (bf16[6,12,4,512]{3,2,1,0:T(4,128)(2,1)}, bf16[6,12,4,512]{3,2,1,0:T(4,128)(2,1)}) custom-call(bf16[3,6,4,512]{3,2,1,0:T(4,128)(2,1)S(1)} %get-tuple-element.63.refs_0_, bf16[3,6,4,512]{3,2,1,0:T(4,128)(2,1)S(1)} %get-tuple-element.82.refs_1_, bf16[2,3,6,4,512]{4,3,2,1,0:T(4,128)(2,1)S(1)} %collective-permute-done.6.refs_2_, ...), custom_call_target="tpu_custom_call" | custom-call | tf_op jit(solution)/shard_map/unpack/pallas_call | solution.py:120
  45.2 0.7 %finish.1 = (f32[16,512]{1,0:T(8,128)}, f32[16,1536]{1,0:T(8,128)}, f32[16,512]{1,0:T(8,128)}, f32[16,512]{1,0:T(8,128)}) custom-call(f32[16,1536]{1,0:T(8,128)S(1)} %convert_add_fusion.mine_ref, f32[16,1536]{1,0:T(8,128)S(1)} %collective-permute-done.13.other_ref), custom_call_target="tpu_custom_call" | custom-call | tf_op jit(solution)/shard_map/finish/pallas_call | solution.py:601
  (15 shorter events, 0.2 us)
Async XLA Ops:
  1.8 7.3 %collective-permute-start = (bf16[3,6,4,512]{3,2,1,0:T(4,128)(2,1)S(1)}, bf16[3,6,4,512]{3,2,1,0:T(4,128)(2,1)S(1)}, u32[]{:S(2)}, u32[]{:S(2)}) collective-permute-start(bf16[3,6,4,512]{3,2,1,0:T(4,128)(2,1)S(1)} %get-tuple-element.51), channel_id=1, source_target_pairs={{0,12},{1,13},{2,14},{3,15},{4,0},{5,1},{6,2},{7,3},{8,4},{9,5},{1... | collective-permute-start | bytes 221192 | tf_op jit(solution)/shard_map/ppermute | solution.py:474
  4.3 9.1 %collective-permute-start.1 = (bf16[3,6,4,512]{3,2,1,0:T(4,128)(2,1)S(1)}, bf16[3,6,4,512]{3,2,1,0:T(4,128)(2,1)S(1)}, u32[]{:S(2)}, u32[]{:S(2)}) collective-permute-start(bf16[3,6,4,512]{3,2,1,0:T(4,128)(2,1)S(1)} %get-tuple-element.52), channel_id=1, source_target_pairs={{0,3},{1,0},{2,1},{3,2},{4,7},{5,4},{6,5},{7,6},{8,11},{9,8},{10,9... | collective-permute-start | bytes 221192 | tf_op jit(solution)/shard_map/ppermute | solution.py:474
  7.9 5.5 %collective-permute-start.2 = (bf16[3,6,4,512]{3,2,1,0:T(4,128)(2,1)S(1)}, bf16[3,6,4,512]{3,2,1,0:T(4,128)(2,1)S(1)}, u32[]{:S(2)}, u32[]{:S(2)}) collective-permute-start(bf16[3,6,4,512]{3,2,1,0:T(4,128)(2,1)S(1)} %get-tuple-element.53), channel_id=1, source_target_pairs={{0,15},{1,12},{2,13},{3,14},{4,3},{5,0},{6,1},{7,2},{8,7},{9,4},{1... | collective-permute-start | bytes 221192 | tf_op jit(solution)/shard_map/ppermute | solution.py:474
  8.2 8.4 %collective-permute-start.3 = (bf16[3,6,4,512]{3,2,1,0:T(4,128)(2,1)S(1)}, bf16[3,6,4,512]{3,2,1,0:T(4,128)(2,1)S(1)}, u32[]{:S(2)}, u32[]{:S(2)}) collective-permute-start(bf16[3,6,4,512]{3,2,1,0:T(4,128)(2,1)S(1)} %get-tuple-element.65), channel_id=1, source_target_pairs={{0,12},{1,13},{2,14},{3,15},{4,0},{5,1},{6,2},{7,3},{8,4},{9,5},{1... | collective-permute-start | bytes 221192 | tf_op jit(solution)/shard_map/ppermute | solution.py:474
  8.7 7.9 %collective-permute-start.4 = (bf16[3,6,4,512]{3,2,1,0:T(4,128)(2,1)S(1)}, bf16[3,6,4,512]{3,2,1,0:T(4,128)(2,1)S(1)}, u32[]{:S(2)}, u32[]{:S(2)}) collective-permute-start(bf16[3,6,4,512]{3,2,1,0:T(4,128)(2,1)S(1)} %get-tuple-element.66), channel_id=1, source_target_pairs={{0,3},{1,0},{2,1},{3,2},{4,7},{5,4},{6,5},{7,6},{8,11},{9,8},{10,9... | collective-permute-start | bytes 221192 | tf_op jit(solution)/shard_map/ppermute | solution.py:474
  9.2 7.4 %collective-permute-start.5 = (bf16[3,6,4,512]{3,2,1,0:T(4,128)(2,1)S(1)}, bf16[3,6,4,512]{3,2,1,0:T(4,128)(2,1)S(1)}, u32[]{:S(2)}, u32[]{:S(2)}) collective-permute-start(bf16[3,6,4,512]{3,2,1,0:T(4,128)(2,1)S(1)} %get-tuple-element.67), channel_id=1, source_target_pairs={{0,15},{1,12},{2,13},{3,14},{4,3},{5,0},{6,1},{7,2},{8,7},{9,4},{1... | collective-permute-start | bytes 221192 | tf_op jit(solution)/shard_map/ppermute | solution.py:474
  20.0 1.3 %collective-permute-start.9 = (f32[16,1536]{1,0:T(8,128)S(1)}, f32[16,1536]{1,0:T(8,128)S(1)}, u32[]{:S(2)}, u32[]{:S(2)}) collective-permute-start(f32[16,1536]{1,0:T(8,128)S(1)} %get-tuple-element.89), channel_id=1, source_target_pairs={{0,4},{4,0},{8,12},{12,8},{1,5},{5,1},{9,13},{13,9},{2,6},{6,2},{1... | collective-permute-start | bytes 294920 | tf_op jit(solution)/shard_map/ppermute | solution.py:479
  21.4 4.2 %collective-permute-start.10 = (bf16[16,1536]{1,0:T(8,128)(2,1)S(1)}, bf16[16,1536]{1,0:T(8,128)(2,1)S(1)}, u32[]{:S(2)}, u32[]{:S(2)}) collective-permute-start(bf16[16,1536]{1,0:T(8,128)(2,1)S(1)} %add_convert_fusion.2), channel_id=1, source_target_pairs={{0,1},{1,0},{2,3},{3,2},{4,5},{5,4},{6,7},{7,6},{8,9},{9,8},{10,11... | collective-permute-start | bytes 147464 | tf_op jit(solution)/shard_map/ppermute | solution.py:479
  25.5 5.3 %collective-permute-start.11 = (bf16[16,1536]{1,0:T(8,128)(2,1)S(1)}, bf16[16,1536]{1,0:T(8,128)(2,1)S(1)}, u32[]{:S(2)}, u32[]{:S(2)}) collective-permute-start(bf16[16,1536]{1,0:T(8,128)(2,1)S(1)} %add_convert_fusion.1), channel_id=1, source_target_pairs={{0,2},{1,3},{2,0},{3,1},{4,6},{5,7},{6,4},{7,5},{8,10},{9,11},{10,... | collective-permute-start | bytes 147464 | tf_op jit(solution)/shard_map/ppermute | solution.py:479
  30.8 4.5 %collective-permute-start.12 = (bf16[16,1536]{1,0:T(8,128)(2,1)S(1)}, bf16[16,1536]{1,0:T(8,128)(2,1)S(1)}, u32[]{:S(2)}, u32[]{:S(2)}) collective-permute-start(bf16[16,1536]{1,0:T(8,128)(2,1)S(1)} %add_convert_fusion), channel_id=1, source_target_pairs={{0,8},{4,12},{8,0},{12,4},{1,9},{5,13},{9,1},{13,5},{2,10},{6,14},... | collective-permute-start | bytes 147464 | tf_op jit(solution)/shard_map/ppermute | solution.py:479
  32.4 4.6 %collective-permute-start.6 = (bf16[2,3,6,4,512]{4,3,2,1,0:T(4,128)(2,1)S(1)}, bf16[2,3,6,4,512]{4,3,2,1,0:T(4,128)(2,1)S(1)}, u32[]{:S(2)}, u32[]{:S(2)}) collective-permute-start(bf16[2,3,6,4,512]{4,3,2,1,0:T(4,128)(2,1)S(1)} %get-tuple-element.83), channel_id=1, source_target_pairs={{0,4},{1,5},{2,6},{3,7},{4,8},{5,9},{6,10},{7,11},{8,12},{9,13},{1... | collective-permute-start | bytes 442376 | tf_op jit(solution)/shard_map/ppermute | solution.py:474
  32.5 7.8 %collective-permute-start.7 = (bf16[2,3,6,4,512]{4,3,2,1,0:T(4,128)(2,1)S(1)}, bf16[2,3,6,4,512]{4,3,2,1,0:T(4,128)(2,1)S(1)}, u32[]{:S(2)}, u32[]{:S(2)}) collective-permute-start(bf16[2,3,6,4,512]{4,3,2,1,0:T(4,128)(2,1)S(1)} %get-tuple-element.84), channel_id=1, source_target_pairs={{0,1},{1,2},{2,3},{3,0},{4,5},{5,6},{6,7},{7,4},{8,9},{9,10},{10,1... | collective-permute-start | bytes 442376 | tf_op jit(solution)/shard_map/ppermute | solution.py:474
  33.7 10.7 %collective-permute-start.8 = (bf16[2,3,6,4,512]{4,3,2,1,0:T(4,128)(2,1)S(1)}, bf16[2,3,6,4,512]{4,3,2,1,0:T(4,128)(2,1)S(1)}, u32[]{:S(2)}, u32[]{:S(2)}) collective-permute-start(bf16[2,3,6,4,512]{4,3,2,1,0:T(4,128)(2,1)S(1)} %get-tuple-element.85), channel_id=1, source_target_pairs={{0,5},{1,6},{2,7},{3,4},{4,9},{5,10},{6,11},{7,8},{8,13},{9,14},{1... | collective-permute-start | bytes 442376 | tf_op jit(solution)/shard_map/ppermute | solution.py:474
  35.4 9.9 %collective-permute-start.13 = (f32[16,1536]{1,0:T(8,128)S(1)}, f32[16,1536]{1,0:T(8,128)S(1)}, u32[]{:S(2)}, u32[]{:S(2)}) collective-permute-start(f32[16,1536]{1,0:T(8,128)S(1)} %convert_add_fusion.mine_ref), channel_id=1, source_target_pairs={{0,4},{4,0},{8,12},{12,8},{1,5},{5,1},{9,13},{13,9},{2,6},{6,2},{1... | collective-permute-start | bytes 294920 | tf_op jit(solution)/shard_map/ppermute | solution.py:479

commit v5 on v4

--- a/solution.py
+++ b/solution.py
@@ -207,25 +207,27 @@
         term = lat_ref[:, lat : lat + 1] * nt(lon_ref[...], ids_ref[lat].astype(f32))
         ids = term if ids is None else ids + term
     half = WINDOW // WIN_LEV
-    key_lane = lax.broadcasted_iota(jnp.int32, (half, HEADS * LANES), 1) % LANES
-    query_lane = lax.broadcasted_iota(jnp.int32, (half, LANES), 1)
+    lane = lax.broadcasted_iota(jnp.int32, (half, LANES), 1)
     for w in range(windows):
         key_rows, query_rows = [], []
         for lev in range(WIN_LEV):
             mine = ids[:, w * WIN_LEV + lev : w * WIN_LEV + lev + 1]
             rows = slice(lev * half, (lev + 1) * half)
+            mask = jnp.where(
+                lane == MARK,
+                masked_value * mine,
+                jnp.where(lane == MARK + 1, masked_value * (1.0 - mine), 0.0),
+            )
             key_rows.append(
-                jnp.where(
-                    key_lane == MARK,
-                    masked_value * mine,
-                    jnp.where(key_lane == MARK + 1, masked_value * (1.0 - mine), keys[rows]),
+                jnp.concatenate(
+                    [keys[rows, h * LANES : (h + 1) * LANES] + mask for h in range(HEADS)], 1
                 )
             )
             query_rows.append(
                 jnp.where(
-                    query_lane == MARK,
+                    lane == MARK,
                     1.0 - mine,
-                    jnp.where(query_lane == MARK + 1, mine, query_ref[rows, :]),
+                    jnp.where(lane == MARK + 1, mine, query_ref[rows, :]),
                 )
             )
         key_out[w] = jnp.concatenate(key_rows, 0).astype(bf16)
@@ -293,19 +295,21 @@
     windows = total // WINDOW
     head = width // HEADS
     pair = 2 * head
-    rows = rows_ref[...]
-    average = jnp.mean(rows, axis=-1, keepdims=True)
-    centered = rows - average
-    variance = jnp.mean(centered * centered, axis=-1, keepdims=True)
-    inv_std = lax.rsqrt(variance + epsilon)
-    unit = centered * inv_std
-    normed = (unit * gain[...]).astype(bf16)
-    unit_ref[...] = unit
-    inv_ref[...] = inv_std
-    normed_ref[...] = normed
-    low = nt(normed, qkv_down[...]).astype(bf16)
-    low_ref[...] = low
-    qkv_ref[...] = (nn(normed, w_qkv[...]) + nn(low, qkv_up[...])).astype(bf16)
+    for w in range(windows):
+        at = slice(w * WINDOW, (w + 1) * WINDOW)
+        rows = rows_ref[at, :]
+        average = jnp.mean(rows, axis=-1, keepdims=True)
+        centered = rows - average
+        variance = jnp.mean(centered * centered, axis=-1, keepdims=True)
+        inv_std = lax.rsqrt(variance + epsilon)
+        unit = centered * inv_std
+        normed = (unit * gain[...]).astype(bf16)
+        unit_ref[at, :] = unit
+        inv_ref[at, :] = inv_std
+        normed_ref[at, :] = normed
+        low = nt(normed, qkv_down[...]).astype(bf16)
+        low_ref[at, :] = low
+        qkv_ref[at, :] = (nn(normed, w_qkv[...]) + nn(low, qkv_up[...])).astype(bf16)
     scale = 1.0 / math.sqrt(head)
     assert math.frexp(scale)[0] == 0.5
     lane = lax.broadcasted_iota(jnp.int32, (WINDOW, pair), 1)
@@ -488,7 +492,7 @@
         raw = total.astype(bf16)
         other = swap(raw, axis, length, bit)
         total = raw.astype(f32) + other.astype(f32)
-    return total, swap(total, "lon", lons, 1)
+    return raw, other, swap(raw, axis, length, 1), swap(raw, axis, length, bit ^ 1)
 
 
 def powers(bit, length):
@@ -497,9 +501,11 @@
         bit *= 2
 
 
-def finish_kernel(mine_ref, other_ref, *outs, scale):
-    half = mine_ref.shape[1]
+def finish_kernel(raw_ref, other_ref, next_raw_ref, next_other_ref, *outs, scale):
+    half = raw_ref.shape[1]
     odd = lax.axis_index("lon") % 2
+    mine = raw_ref[...].astype(f32) + other_ref[...].astype(f32)
+    theirs = next_raw_ref[...].astype(f32) + next_other_ref[...].astype(f32)
 
     def write(first, second):
         start = 0
@@ -515,11 +521,11 @@
 
     @pl.when(odd == 0)
     def _():
-        write(mine_ref, other_ref)
+        write(mine, theirs)
 
     @pl.when(odd == 1)
     def _():
-        write(other_ref, mine_ref)
+        write(theirs, mine)
 
 
 def on_device(sizes):

time: 46.1 us -> 41.9 us (0.909)
  waiting for transfers between devices: 18 us -> 12.2 us
  starting transfers between devices: 14.3 us -> 16 us
    ppermute x5 -> x6, waiting for transfers between devices: 9.25 us -> 5.4 us  [swap(): return lax.ppermute(value, axis, [(i, i ^ bit) for i in range(length)])]
    ppermute x9, waiting for transfers between devices: 8.76 us -> 6.77 us  [exchange(): moved[quad] = lax.ppermute(moved[quad], ('lon', 'lat'), pairs)]
    ppermute x5 -> x6, starting transfers between devices: 2.14 us -> 3.73 us  [swap(): return lax.ppermute(value, axis, [(i, i ^ bit) for i in range(length)])]
  transfers between devices with their start and end apart: 14 -> 15, of which waited for: 6 -> 5; matrix products, arithmetic and copies ran while one was open for 0% -> 0% of each run, Pallas kernels for 16% -> 18%
where the time goes in v5:
time: 41.9 us; the launch traced here: 41.8 us
  starting transfers between devices  16 us (38%)
  Pallas kernels  12.8 us (31%)
  waiting for transfers between devices  12.2 us (29%)
  between operations  0.77 us (2%)
    ppermute x9, starting transfers between devices, exchange(): moved[quad] = lax.ppermute(moved[quad], ('lon', 'lat'), pairs)  12.3 us
    ppermute x9, waiting for transfers between devices, exchange(): moved[quad] = lax.ppermute(moved[quad], ('lon', 'lat'), pairs)  6.77 us
    ppermute x6, waiting for transfers between devices, swap(): return lax.ppermute(value, axis, [(i, i ^ bit) for i in range(length)])  5.4 us
    ppermute x6, starting transfers between devices, swap(): return lax.ppermute(value, axis, [(i, i ^ bit) for i in range(length)])  3.73 us
    pallas_call x1, Pallas kernels, layer(): call(backward_kernel, [struct((total, width), f32), struct((total, 3 * wi...  3.44 us
    pallas_call x1, Pallas kernels, layer(): call(forward_kernel, [quarter] * 4 + [struct((total, width), f32), struct...  3.08 us
    pallas_call x1, Pallas kernels, score_columns(): call(functools.partial(table_kernel, count=len(weights)), [struct((window...  2.25 us
    pallas_call x1, Pallas kernels, pack(): call(pack_kernel, [struct((HALF_LAT, HALF_LON, levels, width), bf16)] * 8...  1.21 us
  transfers between devices with their start and end apart: 15, of which 5 were waited for; matrix products, arithmetic and copies ran while one was open for 0% of the time, Pallas kernels for 18%

profile of v5, /device:TPU:0, one launch (start us, length us, event | category | flops | bytes accessed | tf_op | source)
XLA Modules:
  0.0 41.8 jit_solution(7478694779352732649)
XLA Ops:
  0.6 1.2 %pack.1 = (bf16[3,6,4,512]{3,2,1,0:T(4,128)(2,1)S(1)}, bf16[3,6,4,512]{3,2,1,0:T(4,128)(2,1)S(1)}, bf16[3,6,4,512]{3,2,1,0:T(4,128)(2,1)S(1)}, bf16[3,6,4,512]{3...) custom-call(bf16[6,12,4,512]{3,2,1,0:T(4,128)(2,1)} %bitcast.6, ...), custom_call_target="tpu_custom_call" | custom-call | tf_op jit(solution)/shard_map/pack/pallas_call | solution.py:86
  1.8 2.5 %collective-permute-start = (bf16[3,6,4,512]{3,2,1,0:T(4,128)(2,1)S(1)}, bf16[3,6,4,512]{3,2,1,0:T(4,128)(2,1)S(1)}, u32[]{:S(2)}, u32[]{:S(2)}) collective-permute-start(bf16[3,6,4,512]{3,2,1,0:T(4,128)(2,1)S(1)} %get-tuple-element.51), channel_id=1, source_target_pairs={{0,12},{1,13},{2,14},{3,15},{4,0},{5,1},{6,2},{7,3},{8,4},{9,5},{1... | collective-permute-start | bytes 221192 | tf_op jit(solution)/shard_map/ppermute | solution.py:478
  4.3 3.6 %collective-permute-start.1 = (bf16[3,6,4,512]{3,2,1,0:T(4,128)(2,1)S(1)}, bf16[3,6,4,512]{3,2,1,0:T(4,128)(2,1)S(1)}, u32[]{:S(2)}, u32[]{:S(2)}) collective-permute-start(bf16[3,6,4,512]{3,2,1,0:T(4,128)(2,1)S(1)} %get-tuple-element.52), channel_id=1, source_target_pairs={{0,3},{1,0},{2,1},{3,2},{4,7},{5,4},{6,5},{7,6},{8,11},{9,8},{10,9... | collective-permute-start | bytes 221192 | tf_op jit(solution)/shard_map/ppermute | solution.py:478
  7.9 0.3 collective-permute-start.2
  8.2 0.5 %collective-permute-start.3 = (bf16[3,6,4,512]{3,2,1,0:T(4,128)(2,1)S(1)}, bf16[3,6,4,512]{3,2,1,0:T(4,128)(2,1)S(1)}, u32[]{:S(2)}, u32[]{:S(2)}) collective-permute-start(bf16[3,6,4,512]{3,2,1,0:T(4,128)(2,1)S(1)} %get-tuple-element.65), channel_id=1, source_target_pairs={{0,12},{1,13},{2,14},{3,15},{4,0},{5,1},{6,2},{7,3},{8,4},{9,5},{1... | collective-permute-start | bytes 221192 | tf_op jit(solution)/shard_map/ppermute | solution.py:478
  8.7 0.4 %collective-permute-start.4 = (bf16[3,6,4,512]{3,2,1,0:T(4,128)(2,1)S(1)}, bf16[3,6,4,512]{3,2,1,0:T(4,128)(2,1)S(1)}, u32[]{:S(2)}, u32[]{:S(2)}) collective-permute-start(bf16[3,6,4,512]{3,2,1,0:T(4,128)(2,1)S(1)} %get-tuple-element.66), channel_id=1, source_target_pairs={{0,3},{1,0},{2,1},{3,2},{4,7},{5,4},{6,5},{7,6},{8,11},{9,8},{10,9... | collective-permute-start | bytes 221192 | tf_op jit(solution)/shard_map/ppermute | solution.py:478
  9.2 2.0 %collective-permute-start.5 = (bf16[3,6,4,512]{3,2,1,0:T(4,128)(2,1)S(1)}, bf16[3,6,4,512]{3,2,1,0:T(4,128)(2,1)S(1)}, u32[]{:S(2)}, u32[]{:S(2)}) collective-permute-start(bf16[3,6,4,512]{3,2,1,0:T(4,128)(2,1)S(1)} %get-tuple-element.67), channel_id=1, source_target_pairs={{0,15},{1,12},{2,13},{3,14},{4,3},{5,0},{6,1},{7,2},{8,7},{9,4},{1... | collective-permute-start | bytes 221192 | tf_op jit(solution)/shard_map/ppermute | solution.py:478
  11.1 2.3 %table.1 = (bf16[2,144,1024]{2,1,0:T(8,128)(2,1)S(1)}, bf16[2,144,128]{2,1,0:T(8,128)(2,1)S(1)}, f32[1,512]{1,0:T(1,128)S(1)}, bf16[512,1536]{1,0:T(8,128)(2,1)S...) custom-call(f32[8,37]{1,0:T(8,128)} %refs_0_.1, ...), custom_call_target="tpu_custom_call" | custom-call | tf_op jit(solution)/shard_map/table/pallas_call | solution.py:240
  13.4 3.1 %forward.1 = (bf16[3,6,4,512]{3,2,1,0:T(4,128)(2,1)S(1)}, bf16[3,6,4,512]{3,2,1,0:T(4,128)(2,1)S(1)}, bf16[3,6,4,512]{3,2,1,0:T(4,128)(2,1)S(1)}, bf16[3,6,4,512...) custom-call(bf16[3,6,4,512]{3,2,1,0:T(4,128)(2,1)S(1)} %get-tuple-el, ...), custom_call_target="tpu_custom_call" | custom-call | tf_op jit(solution)/shard_map/forward/pallas_call | solution.py:554
  16.5 3.4 %backward.1 = (f32[288,512]{1,0:T(8,128)S(1)}, bf16[288,1536]{1,0:T(8,128)(2,1)S(1)}, bf16[288,16]{1,0:T(8,128)(2,1)S(1)}, f32[16,1536]{1,0:T(8,128)S(1)}, f32[16,1536]{1,0:T(8,128)S(1)}) custom-call(bf16[3,6,4,512]{3,2,1,0:T(4,128)(2,1)S(1)} %get-tuple-element.64.g0, bf16[3,6,4,512]{3,2,1,0:T(4,128)(2,1)S(1)} %collective-permute-done.3.g1, ...), custom_call_target="tpu_custom_call" | custom-call | tf_op jit(solution)/shard_map/backward/pallas_call | solution.py:576
  20.0 1.3 %collective-permute-done.9 = f32[16,1536]{1,0:T(8,128)S(1)} collective-permute-done((f32[16,1536]{1,0:T(8,128)S(1)}, f32[16,1536]{1,0:T(8,128)S(1)}, u32[]{:S(2)}, u32[]{:S(2)}) %collective-permute-start.9) | collective-permute-done | bytes 98336 | tf_op jit(solution)/shard_map/ppermute | solution.py:483
  21.4 4.1 %collective-permute-done.10 = bf16[16,1536]{1,0:T(8,128)(2,1)S(1)} collective-permute-done((bf16[16,1536]{1,0:T(8,128)(2,1)S(1)}, bf16[16,1536]{1,0:T(8,128)(2,1)S(1)}, u32[]{:S(2)}, u32[]{:S(2)}) %collective-permute-start.10) | collective-permute-done | bytes 49184 | tf_op jit(solution)/shard_map/ppermute | solution.py:483
  25.5 1.4 %collective-permute-start.11 = (bf16[16,1536]{1,0:T(8,128)(2,1)S(1)}, bf16[16,1536]{1,0:T(8,128)(2,1)S(1)}, u32[]{:S(2)}, u32[]{:S(2)}) collective-permute-start(bf16[16,1536]{1,0:T(8,128)(2,1)S(1)} %add_convert_fusion.1), channel_id=1, source_target_pairs={{0,2},{1,3},{2,0},{3,1},{4,6},{5,7},{6,4},{7,5},{8,10},{9,11},{10,... | collective-permute-start | bytes 147464 | tf_op jit(solution)/shard_map/ppermute | solution.py:483
  26.9 1.2 %norm_back.1 = (bf16[3,6,4,512]{3,2,1,0:T(4,128)(2,1)S(1)}, bf16[2,3,6,4,512]{4,3,2,1,0:T(4,128)(2,1)S(1)}, bf16[2,3,6,4,512]{4,3,2,1,0:T(4,128)(2,1)S(1)}, bf16[2,3,6,4,512]{4,3,2,1,0:T(4,128)(2,1)S(1)}) custom-call(f32[288,512]{1,0:T(8,128)S(1)} %get-tuple-element.74.refs_0_, bf16[288,1536]{1,0:T(8,128)(2,1)S(1)} %get-tuple-element.75.refs_1_, ...), custom_call_target="tpu_custom_call" | custom-call | tf_op jit(solution)/shard_map/norm_back/pallas_call | solution.py:596
  28.2 1.9 %collective-permute-start.7 = (bf16[2,3,6,4,512]{4,3,2,1,0:T(4,128)(2,1)S(1)}, bf16[2,3,6,4,512]{4,3,2,1,0:T(4,128)(2,1)S(1)}, u32[]{:S(2)}, u32[]{:S(2)}) collective-permute-start(bf16[2,3,6,4,512]{4,3,2,1,0:T(4,128)(2,1)S(1)} %get-tuple-element.84), channel_id=1, source_target_pairs={{0,1},{1,2},{2,3},{3,0},{4,5},{5,6},{6,7},{7,4},{8,9},{9,10},{10,1... | collective-permute-start | bytes 442376 | tf_op jit(solution)/shard_map/ppermute | solution.py:478
  30.0 1.1 %collective-permute-start.8 = (bf16[2,3,6,4,512]{4,3,2,1,0:T(4,128)(2,1)S(1)}, bf16[2,3,6,4,512]{4,3,2,1,0:T(4,128)(2,1)S(1)}, u32[]{:S(2)}, u32[]{:S(2)}) collective-permute-start(bf16[2,3,6,4,512]{4,3,2,1,0:T(4,128)(2,1)S(1)} %get-tuple-element.85), channel_id=1, source_target_pairs={{0,5},{1,6},{2,7},{3,4},{4,9},{5,10},{6,11},{7,8},{8,13},{9,14},{1... | collective-permute-start | bytes 442376 | tf_op jit(solution)/shard_map/ppermute | solution.py:478
  31.1 0.5 %collective-permute-start.14 = (bf16[16,1536]{1,0:T(8,128)(2,1)S(1)}, bf16[16,1536]{1,0:T(8,128)(2,1)S(1)}, u32[]{:S(2)}, u32[]{:S(2)}) collective-permute-start(bf16[16,1536]{1,0:T(8,128)(2,1)S(1)} %add_convert_fusion.raw_ref), channel_id=1, source_target_pairs={{0,12},{4,8},{8,4},{12,0},{1,13},{5,9},{9,5},{13,1},{2,14},{6,10},... | collective-permute-start | bytes 147464 | tf_op jit(solution)/shard_map/ppermute | solution.py:483
  31.6 0.3 collective-permute-start.13
  32.0 0.8 %collective-permute-done.6.refs_2_ = bf16[2,3,6,4,512]{4,3,2,1,0:T(4,128)(2,1)S(1)} collective-permute-done((bf16[2,3,6,4,512]{4,3,2,1,0:T(4,128)(2,1)S(1)}, bf16[2,3,6,4,512]{4,3,2,1,0:T(4,128)(2,1)S(1)}, u32[]{:S(2)}, u32[]{:S(2)}) %collective-permute-start.6) | collective-permute-done | bytes 147488 | tf_op jit(solution)/shard_map/ppermute | solution.py:478
  32.7 1.4 %collective-permute-start.12 = (bf16[16,1536]{1,0:T(8,128)(2,1)S(1)}, bf16[16,1536]{1,0:T(8,128)(2,1)S(1)}, u32[]{:S(2)}, u32[]{:S(2)}) collective-permute-start(bf16[16,1536]{1,0:T(8,128)(2,1)S(1)} %add_convert_fusion.raw_ref), channel_id=1, source_target_pairs={{0,8},{4,12},{8,0},{12,4},{1,9},{5,13},{9,1},{13,5},{2,10},{6,14},... | collective-permute-start | bytes 147464 | tf_op jit(solution)/shard_map/ppermute | solution.py:483
  34.1 2.1 %collective-permute-done.7.refs_3_ = bf16[2,3,6,4,512]{4,3,2,1,0:T(4,128)(2,1)S(1)} collective-permute-done((bf16[2,3,6,4,512]{4,3,2,1,0:T(4,128)(2,1)S(1)}, bf16[2,3,6,4,512]{4,3,2,1,0:T(4,128)(2,1)S(1)}, u32[]{:S(2)}, u32[]{:S(2)}) %collective-permute-start.7) | collective-permute-done | bytes 147488 | tf_op jit(solution)/shard_map/ppermute | solution.py:478
  36.3 3.9 %collective-permute-done.8.refs_4_ = bf16[2,3,6,4,512]{4,3,2,1,0:T(4,128)(2,1)S(1)} collective-permute-done((bf16[2,3,6,4,512]{4,3,2,1,0:T(4,128)(2,1)S(1)}, bf16[2,3,6,4,512]{4,3,2,1,0:T(4,128)(2,1)S(1)}, u32[]{:S(2)}, u32[]{:S(2)}) %collective-permute-start.8) | collective-permute-done | bytes 147488 | tf_op jit(solution)/shard_map/ppermute | solution.py:478
  40.1 0.9 %unpack.1 = (bf16[6,12,4,512]{3,2,1,0:T(4,128)(2,1)}, bf16[6,12,4,512]{3,2,1,0:T(4,128)(2,1)}) custom-call(bf16[3,6,4,512]{3,2,1,0:T(4,128)(2,1)S(1)} %get-tuple-element.63.refs_0_, bf16[3,6,4,512]{3,2,1,0:T(4,128)(2,1)S(1)} %get-tuple-element.82.refs_1_, bf16[2,3,6,4,512]{4,3,2,1,0:T(4,128)(2,1)S(1)} %collective-permute-done.6.refs_2_, ...), custom_call_target="tpu_custom_call" | custom-call | tf_op jit(solution)/shard_map/unpack/pallas_call | solution.py:120
  41.0 0.7 %finish.1 = (f32[16,512]{1,0:T(8,128)}, f32[16,1536]{1,0:T(8,128)}, f32[16,512]{1,0:T(8,128)}, f32[16,512]{1,0:T(8,128)}) custom-call(bf16[16,1536]{1,0:T(8,128)(2,1)S(1)} %add_convert_fusion.raw_ref, bf16[16,1536]{1,0:T(8,128)(2,1)S(1)} %collective-permute-done.12.other_ref, bf16[16,1536]{1,0:T(8,128)(2,1)S(1)} %collective-permute-done.13.next_raw_ref, ...), custom_call_target="tpu_custom_call" | custom-call | tf_op jit(solution)/shard_map/finish/pallas_call | solution.py:607
  (16 shorter events, 0.2 us)
Async XLA Ops:
  1.8 7.3 %collective-permute-start = (bf16[3,6,4,512]{3,2,1,0:T(4,128)(2,1)S(1)}, bf16[3,6,4,512]{3,2,1,0:T(4,128)(2,1)S(1)}, u32[]{:S(2)}, u32[]{:S(2)}) collective-permute-start(bf16[3,6,4,512]{3,2,1,0:T(4,128)(2,1)S(1)} %get-tuple-element.51), channel_id=1, source_target_pairs={{0,12},{1,13},{2,14},{3,15},{4,0},{5,1},{6,2},{7,3},{8,4},{9,5},{1... | collective-permute-start | bytes 221192 | tf_op jit(solution)/shard_map/ppermute | solution.py:478
  4.3 9.1 %collective-permute-start.1 = (bf16[3,6,4,512]{3,2,1,0:T(4,128)(2,1)S(1)}, bf16[3,6,4,512]{3,2,1,0:T(4,128)(2,1)S(1)}, u32[]{:S(2)}, u32[]{:S(2)}) collective-permute-start(bf16[3,6,4,512]{3,2,1,0:T(4,128)(2,1)S(1)} %get-tuple-element.52), channel_id=1, source_target_pairs={{0,3},{1,0},{2,1},{3,2},{4,7},{5,4},{6,5},{7,6},{8,11},{9,8},{10,9... | collective-permute-start | bytes 221192 | tf_op jit(solution)/shard_map/ppermute | solution.py:478
  7.9 5.5 %collective-permute-start.2 = (bf16[3,6,4,512]{3,2,1,0:T(4,128)(2,1)S(1)}, bf16[3,6,4,512]{3,2,1,0:T(4,128)(2,1)S(1)}, u32[]{:S(2)}, u32[]{:S(2)}) collective-permute-start(bf16[3,6,4,512]{3,2,1,0:T(4,128)(2,1)S(1)} %get-tuple-element.53), channel_id=1, source_target_pairs={{0,15},{1,12},{2,13},{3,14},{4,3},{5,0},{6,1},{7,2},{8,7},{9,4},{1... | collective-permute-start | bytes 221192 | tf_op jit(solution)/shard_map/ppermute | solution.py:478
  8.2 8.3 %collective-permute-start.3 = (bf16[3,6,4,512]{3,2,1,0:T(4,128)(2,1)S(1)}, bf16[3,6,4,512]{3,2,1,0:T(4,128)(2,1)S(1)}, u32[]{:S(2)}, u32[]{:S(2)}) collective-permute-start(bf16[3,6,4,512]{3,2,1,0:T(4,128)(2,1)S(1)} %get-tuple-element.65), channel_id=1, source_target_pairs={{0,12},{1,13},{2,14},{3,15},{4,0},{5,1},{6,2},{7,3},{8,4},{9,5},{1... | collective-permute-start | bytes 221192 | tf_op jit(solution)/shard_map/ppermute | solution.py:478
  8.7 7.8 %collective-permute-start.4 = (bf16[3,6,4,512]{3,2,1,0:T(4,128)(2,1)S(1)}, bf16[3,6,4,512]{3,2,1,0:T(4,128)(2,1)S(1)}, u32[]{:S(2)}, u32[]{:S(2)}) collective-permute-start(bf16[3,6,4,512]{3,2,1,0:T(4,128)(2,1)S(1)} %get-tuple-element.66), channel_id=1, source_target_pairs={{0,3},{1,0},{2,1},{3,2},{4,7},{5,4},{6,5},{7,6},{8,11},{9,8},{10,9... | collective-permute-start | bytes 221192 | tf_op jit(solution)/shard_map/ppermute | solution.py:478
  9.2 7.4 %collective-permute-start.5 = (bf16[3,6,4,512]{3,2,1,0:T(4,128)(2,1)S(1)}, bf16[3,6,4,512]{3,2,1,0:T(4,128)(2,1)S(1)}, u32[]{:S(2)}, u32[]{:S(2)}) collective-permute-start(bf16[3,6,4,512]{3,2,1,0:T(4,128)(2,1)S(1)} %get-tuple-element.67), channel_id=1, source_target_pairs={{0,15},{1,12},{2,13},{3,14},{4,3},{5,0},{6,1},{7,2},{8,7},{9,4},{1... | collective-permute-start | bytes 221192 | tf_op jit(solution)/shard_map/ppermute | solution.py:478
  20.0 1.3 %collective-permute-start.9 = (f32[16,1536]{1,0:T(8,128)S(1)}, f32[16,1536]{1,0:T(8,128)S(1)}, u32[]{:S(2)}, u32[]{:S(2)}) collective-permute-start(f32[16,1536]{1,0:T(8,128)S(1)} %get-tuple-element.89), channel_id=1, source_target_pairs={{0,4},{4,0},{8,12},{12,8},{1,5},{5,1},{9,13},{13,9},{2,6},{6,2},{1... | collective-permute-start | bytes 294920 | tf_op jit(solution)/shard_map/ppermute | solution.py:483
  21.3 4.2 %collective-permute-start.10 = (bf16[16,1536]{1,0:T(8,128)(2,1)S(1)}, bf16[16,1536]{1,0:T(8,128)(2,1)S(1)}, u32[]{:S(2)}, u32[]{:S(2)}) collective-permute-start(bf16[16,1536]{1,0:T(8,128)(2,1)S(1)} %add_convert_fusion.2), channel_id=1, source_target_pairs={{0,1},{1,0},{2,3},{3,2},{4,5},{5,4},{6,7},{7,6},{8,9},{9,8},{10,11... | collective-permute-start | bytes 147464 | tf_op jit(solution)/shard_map/ppermute | solution.py:483
  25.5 5.7 %collective-permute-start.11 = (bf16[16,1536]{1,0:T(8,128)(2,1)S(1)}, bf16[16,1536]{1,0:T(8,128)(2,1)S(1)}, u32[]{:S(2)}, u32[]{:S(2)}) collective-permute-start(bf16[16,1536]{1,0:T(8,128)(2,1)S(1)} %add_convert_fusion.1), channel_id=1, source_target_pairs={{0,2},{1,3},{2,0},{3,1},{4,6},{5,7},{6,4},{7,5},{8,10},{9,11},{10,... | collective-permute-start | bytes 147464 | tf_op jit(solution)/shard_map/ppermute | solution.py:483
  28.1 4.6 %collective-permute-start.6 = (bf16[2,3,6,4,512]{4,3,2,1,0:T(4,128)(2,1)S(1)}, bf16[2,3,6,4,512]{4,3,2,1,0:T(4,128)(2,1)S(1)}, u32[]{:S(2)}, u32[]{:S(2)}) collective-permute-start(bf16[2,3,6,4,512]{4,3,2,1,0:T(4,128)(2,1)S(1)} %get-tuple-element.83), channel_id=1, source_target_pairs={{0,4},{1,5},{2,6},{3,7},{4,8},{5,9},{6,10},{7,11},{8,12},{9,13},{1... | collective-permute-start | bytes 442376 | tf_op jit(solution)/shard_map/ppermute | solution.py:478
  28.2 8.1 %collective-permute-start.7 = (bf16[2,3,6,4,512]{4,3,2,1,0:T(4,128)(2,1)S(1)}, bf16[2,3,6,4,512]{4,3,2,1,0:T(4,128)(2,1)S(1)}, u32[]{:S(2)}, u32[]{:S(2)}) collective-permute-start(bf16[2,3,6,4,512]{4,3,2,1,0:T(4,128)(2,1)S(1)} %get-tuple-element.84), channel_id=1, source_target_pairs={{0,1},{1,2},{2,3},{3,0},{4,5},{5,6},{6,7},{7,4},{8,9},{9,10},{10,1... | collective-permute-start | bytes 442376 | tf_op jit(solution)/shard_map/ppermute | solution.py:478
  30.0 10.1 %collective-permute-start.8 = (bf16[2,3,6,4,512]{4,3,2,1,0:T(4,128)(2,1)S(1)}, bf16[2,3,6,4,512]{4,3,2,1,0:T(4,128)(2,1)S(1)}, u32[]{:S(2)}, u32[]{:S(2)}) collective-permute-start(bf16[2,3,6,4,512]{4,3,2,1,0:T(4,128)(2,1)S(1)} %get-tuple-element.85), channel_id=1, source_target_pairs={{0,5},{1,6},{2,7},{3,4},{4,9},{5,10},{6,11},{7,8},{8,13},{9,14},{1... | collective-permute-start | bytes 442376 | tf_op jit(solution)/shard_map/ppermute | solution.py:478
  31.1 9.9 %collective-permute-start.14 = (bf16[16,1536]{1,0:T(8,128)(2,1)S(1)}, bf16[16,1536]{1,0:T(8,128)(2,1)S(1)}, u32[]{:S(2)}, u32[]{:S(2)}) collective-permute-start(bf16[16,1536]{1,0:T(8,128)(2,1)S(1)} %add_convert_fusion.raw_ref), channel_id=1, source_target_pairs={{0,12},{4,8},{8,4},{12,0},{1,13},{5,9},{9,5},{13,1},{2,14},{6,10},... | collective-permute-start | bytes 147464 | tf_op jit(solution)/shard_map/ppermute | solution.py:483
  31.6 9.4 %collective-permute-start.13 = (bf16[16,1536]{1,0:T(8,128)(2,1)S(1)}, bf16[16,1536]{1,0:T(8,128)(2,1)S(1)}, u32[]{:S(2)}, u32[]{:S(2)}) collective-permute-start(bf16[16,1536]{1,0:T(8,128)(2,1)S(1)} %add_convert_fusion.raw_ref), channel_id=1, source_target_pairs={{0,4},{4,0},{8,12},{12,8},{1,5},{5,1},{9,13},{13,9},{2,6},{6,2},{1... | collective-permute-start | bytes 147464 | tf_op jit(solution)/shard_map/ppermute | solution.py:483
  32.7 8.3 %collective-permute-start.12 = (bf16[16,1536]{1,0:T(8,128)(2,1)S(1)}, bf16[16,1536]{1,0:T(8,128)(2,1)S(1)}, u32[]{:S(2)}, u32[]{:S(2)}) collective-permute-start(bf16[16,1536]{1,0:T(8,128)(2,1)S(1)} %add_convert_fusion.raw_ref), channel_id=1, source_target_pairs={{0,8},{4,12},{8,0},{12,4},{1,9},{5,13},{9,1},{13,5},{2,10},{6,14},... | collective-permute-start | bytes 147464 | tf_op jit(solution)/shard_map/ppermute | solution.py:483
